TPU v7x, 128 devices: a whole 4x4x4 slice. The times are simulated.
128 devices in a mesh: dp: 4 (over z), w: 4 (over y), h: 8 (over x, core).
Axes of the slice: x: 4, y: 4, z: 4, core: 2. Of those that a mesh axis runs over, the one named last changes fastest.
Arguments:
- field: float32 [12, 256, 128, 256], P('dp', None, 'h', 'w')
- target: float32 [12, 256, 128, 256], P('dp', None, 'h', 'w')
- lat_weight: float32 [128], P('h')
- leg_fwd: float32 [64, 64, 128], P('w', None, 'h')
- leg_inv: float32 [64, 64, 128], P('w', None, 'h')
- spec_w: float32 [2, 64, 256, 256], replicated
- w_in: bfloat16 [256, 512], replicated
- w_out: bfloat16 [512, 256], replicated
Outputs:
- output 1: float32 [], replicated
- output 2: float32 [12, 256, 128, 256], P('dp', None, 'h', 'w')
- output 3: float32 [2, 64, 256, 256], P(None, 'h')
- output 4: float32 [256, 512], replicated
- output 5: float32 [512, 256], replicated
All inputs are finite; a program needn't handle non-finite values.
Results may differ from a plain program's by a relative error of at most 0.00130349.
Values sent between devices are 32-bit elements.
A program may use at most 1 GiB of HBM per device.

v0:
```python
import functools
import jax
import jax.numpy as jnp
from jax import lax
from jax.sharding import PartitionSpec as P

NORM_EPS = 1e-5
PRECISE = lax.Precision.HIGHEST


def precise_product(einsum_form, operand_a, operand_b):
    return jnp.einsum(einsum_form, operand_a, operand_b, precision=PRECISE, preferred_element_type=jnp.float32)


def lon_forward(grid_vals, num_modes):
    lon_spec = jnp.fft.rfft(grid_vals, axis=3, norm="ortho")[:, :, :, :num_modes]
    return jnp.stack([lon_spec.real, lon_spec.imag])


def lon_inverse(coeffs, lon_count):
    pad_width = ((0, 0), (0, 0), (0, 0), (0, lon_count // 2 + 1 - coeffs.shape[4]))
    padded = jnp.pad(lax.complex(coeffs[0], coeffs[1]), pad_width)
    return jnp.fft.irfft(padded, n=lon_count, axis=3, norm="ortho")


def spectral_mix(coeffs, kernel):
    einsum_form = "bilm,lio->bolm"
    real_part = precise_product(einsum_form, coeffs[0], kernel[0]) - precise_product(einsum_form, coeffs[1], kernel[1])
    imag_part = precise_product(einsum_form, coeffs[0], kernel[1]) + precise_product(einsum_form, coeffs[1], kernel[0])
    return jnp.stack([real_part, imag_part])


def spectral_input_grad(d_mixed, kernel):
    einsum_form = "bolm,lio->bilm"
    real_part = precise_product(einsum_form, d_mixed[0], kernel[0]) + precise_product(einsum_form, d_mixed[1], kernel[1])
    imag_part = precise_product(einsum_form, d_mixed[1], kernel[0]) - precise_product(einsum_form, d_mixed[0], kernel[1])
    return jnp.stack([real_part, imag_part])


def spectral_kernel_grad(coeffs, d_mixed):
    einsum_form = "bilm,bolm->lio"
    real_part = precise_product(einsum_form, coeffs[0], d_mixed[0]) + precise_product(einsum_form, coeffs[1], d_mixed[1])
    imag_part = precise_product(einsum_form, coeffs[0], d_mixed[1]) - precise_product(einsum_form, coeffs[1], d_mixed[0])
    return jnp.stack([real_part, imag_part])


def solution(mesh):
    dp_size = mesh.shape["dp"]
    w_size = mesh.shape["w"]
    h_size = mesh.shape["h"]
    grid_axes = ("h", "w")
    all_axes = ("dp", "h", "w")

    def degree_from_lat(spec_loc, table):
        part_sums = precise_product("mlt,xbctm->xbclm", table, spec_loc)
        return lax.psum_scatter(part_sums, "h", scatter_dimension=3, tiled=True)

    def lat_from_degree(coeffs, table):
        coeffs_all = lax.all_gather(coeffs, "h", axis=3, tiled=True)
        return precise_product("mlt,xbclm->xbctm", table, coeffs_all)

    def local_step(field, target, lat_weight, leg_fwd, leg_inv, spec_w, w_in, w_out):
        batch_loc, chan_count, lat_loc, lon_loc = field.shape
        lon_count = lon_loc * w_size
        num_modes = leg_fwd.shape[0] * w_size
        grid_points = lat_loc * h_size * lon_count
        total_points = batch_loc * dp_size * chan_count * grid_points
        chan_mean = lax.psum(jnp.sum(field, axis=(2, 3), keepdims=True), grid_axes) / grid_points
        centred = field - chan_mean
        variance = lax.psum(jnp.sum(centred * centred, axis=(2, 3), keepdims=True), grid_axes) / grid_points
        inv_std = lax.rsqrt(variance + NORM_EPS)
        normed = centred * inv_std
        lon_whole = lax.all_to_all(normed, "w", 1, 3, tiled=True)
        spec_half, fwd_pull = jax.vjp(functools.partial(lon_forward, num_modes=num_modes), lon_whole)
        spec_loc = lax.all_to_all(spec_half, "w", 4, 2, tiled=True)
        coeffs = degree_from_lat(spec_loc, leg_fwd)
        mixed = spectral_mix(coeffs, spec_w)
        back_loc = lat_from_degree(mixed, leg_inv)
        back_half = lax.all_to_all(back_loc, "w", 2, 4, tiled=True)
        y_half, inv_pull = jax.vjp(functools.partial(lon_inverse, lon_count=lon_count), back_half)
        y_grid = lax.all_to_all(y_half, "w", 3, 1, tiled=True)
        y_bf = y_grid.astype(jnp.bfloat16)
        hidden = jnp.einsum("bctp,cf->bftp", y_bf, w_in, preferred_element_type=jnp.float32)
        activation, gelu_pull = jax.vjp(jax.nn.gelu, hidden)
        act_bf = activation.astype(jnp.bfloat16)
        mlp_out = jnp.einsum("bftp,fc->bctp", act_bf, w_out, preferred_element_type=jnp.float32)
        residual = field + y_grid + mlp_out - target
        d_out = lat_weight[None, None, :, None] * residual
        loss = lax.psum(jnp.sum(d_out * residual), all_axes) / total_points
        d_out_bf = d_out.astype(jnp.bfloat16)
        grad_w_out = lax.psum(jnp.einsum("bftp,bctp->fc", act_bf, d_out_bf, preferred_element_type=jnp.float32), all_axes)
        d_act = jnp.einsum("bctp,fc->bftp", d_out_bf, w_out, preferred_element_type=jnp.float32)
        d_hidden = gelu_pull(d_act)[0].astype(jnp.bfloat16)
        grad_w_in = lax.psum(jnp.einsum("bctp,bftp->cf", y_bf, d_hidden, preferred_element_type=jnp.float32), all_axes)
        d_y = d_out + jnp.einsum("bftp,cf->bctp", d_hidden, w_in, preferred_element_type=jnp.float32)
        d_y_half = lax.all_to_all(d_y, "w", 1, 3, tiled=True)
        d_back_half = inv_pull(d_y_half)[0]
        d_back_loc = lax.all_to_all(d_back_half, "w", 4, 2, tiled=True)
        d_mixed = degree_from_lat(d_back_loc, leg_inv)
        grad_spec = lax.psum(spectral_kernel_grad(coeffs, d_mixed), ("dp", "w"))
        d_coeffs = spectral_input_grad(d_mixed, spec_w)
        d_spec_loc = lat_from_degree(d_coeffs, leg_fwd)
        d_spec_half = lax.all_to_all(d_spec_loc, "w", 2, 4, tiled=True)
        d_lon_whole = fwd_pull(d_spec_half)[0]
        d_normed = lax.all_to_all(d_lon_whole, "w", 3, 1, tiled=True)
        norm_stats = lax.psum(jnp.stack([jnp.sum(d_normed, axis=(2, 3), keepdims=True), jnp.sum(d_normed * normed, axis=(2, 3), keepdims=True)]), grid_axes) / grid_points
        d_field = d_out + inv_std * (d_normed - norm_stats[0] - normed * norm_stats[1])
        return loss, d_field, grad_spec, grad_w_in, grad_w_out

    grid_spec = P("dp", None, "h", "w")
    table_spec = P("w", None, "h")
    kernel_spec = P(None, "h", None, None)
    return jax.shard_map(local_step, mesh=mesh, in_specs=(grid_spec, grid_spec, P("h"), table_spec, table_spec, kernel_spec, P(), P()), out_specs=(P(), grid_spec, kernel_spec, P(), P()), check_vma=False)
```

profile of v0, /device:TPU:1, one launch (start us, length us, event | category | flops | bytes accessed | tf_op | source)
XLA Modules:
  0.0 1296.6 jit_solution(8240300775585119251)
XLA Ops:
  9.5 63.8 %psum.42 = f32[3,256,1,1]{1,0,3,2:T(4,128)S(1)} all-reduce(f32[3,256,1,1]{1,0,3,2:T(4,128)S(1)} %bitcast.308), channel_id=1, replica_groups=mesh['dp'=4,'w'=4,'h'=8] {'h','w'}, use_global_device_ids=true, to_apply=%region_1.0 | all-reduce | flops 768 | bytes 6144 | tf_op jit(solution)/shard_map/psum | solution.py:68
  73.7 62.7 %psum.43 = f32[3,256,1,1]{1,0,3,2:T(4,128)S(1)} all-reduce(f32[3,256,1,1]{1,0,3,2:T(4,128)S(1)} %bitcast.309), channel_id=1, replica_groups=mesh['dp'=4,'w'=4,'h'=8] {'h','w'}, use_global_device_ids=true, to_apply=%region_3.0 | all-reduce | flops 768 | bytes 6144 | tf_op jit(solution)/shard_map/psum | solution.py:70
  163.2 27.1 %all-to-all-done = f32[4,1,196608]{2,1,0:T(1,128)} async-done(((f32[4,1,196608]{2,1,0:T(1,128)}), f32[4,1,196608]{2,1,0:T(1,128)}, u32[]{:S(2)}, u32[]{:S(2)}) %all-to-all-start) | async-done | bytes 3145760 | tf_op jit(solution)/shard_map/all_to_all | solution.py:73
  190.8 11.9 reduce.8
  210.2 9.4 copy.323
  249.7 19.2 %all_to_all.121 = f32[4,1,98304]{2,1,0:T(1,128)} all-to-all(f32[4,1,98304]{2,1,0:T(1,128)} %reshape.69), channel_id=1, replica_groups=mesh['dp'=4,'w'=4,'h'=8] {'w'}, dimensions={0} | all-to-all | bytes 3145728 | tf_op jit(solution)/shard_map/all_to_all | solution.py:75
  301.0 44.4 %reduce-scatter.5.cloned.1.call-done = f32[2,3,256,8,16]{2,3,1,0,4:T(8,128)} async-done(((f32[2,3,256,64,16]{2,3,1,0,4:T(8,128)}), f32[2,3,256,8,16]{2,3,1,0,4:T(8,128)}) %reduce-scatter.5.cloned.1.call-update) | async-done | bytes 786448 | tf_op jit(solution)/shard_map/reduce_scatter | solution.py:56
  360.1 41.3 %all-gather.3.cloned.1.call-done = f32[2,3,256,64,16]{2,4,1,3,0:T(8,128)} async-done(((f32[2,3,256,8,16]{2,4,1,3,0:T(8,128)}), f32[2,3,256,64,16]{2,4,1,3,0:T(8,128)}) %all-gather.3.cloned.1.call-update) | async-done | bytes 6291472 | tf_op jit(solution)/shard_map/all_gather | solution.py:59
  401.4 8.6 fusion.38
  410.0 11.4 copy.217
  421.4 8.3 reshape.71
  429.6 25.1 %all_to_all.122 = f32[4,1,98304]{2,1,0:T(1,128)} all-to-all(f32[4,1,98304]{2,1,0:T(1,128)} %reshape.71), channel_id=1, replica_groups=mesh['dp'=4,'w'=4,'h'=8] {'w'}, dimensions={0} | all-to-all | bytes 3145728 | tf_op jit(solution)/shard_map/all_to_all | solution.py:79
  462.1 10.5 reshape.72
  472.6 10.4 copy.271
  545.3 41.7 %all_to_all.123 = f32[4,1,196608]{2,1,0:T(1,128)} all-to-all(f32[4,1,196608]{2,1,0:T(1,128)} %reshape.73), channel_id=1, replica_groups=mesh['dp'=4,'w'=4,'h'=8] {'w'}, dimensions={0} | all-to-all | bytes 6291456 | tf_op jit(solution)/shard_map/all_to_all | solution.py:81
  587.0 11.6 reduce.11
  606.1 9.4 copy.322
  657.1 35.5 %all-to-all-done.4 = f32[4,1,196608]{2,1,0:T(1,128)} async-done(((f32[4,1,196608]{2,1,0:T(1,128)}), f32[4,1,196608]{2,1,0:T(1,128)}, u32[]{:S(2)}, u32[]{:S(2)}) %all-to-all-start.4) | async-done | bytes 3145760 | tf_op jit(solution)/shard_map/all_to_all | solution.py:96
  692.6 11.6 reduce.12
  751.5 22.0 %all_to_all.124 = f32[4,1,98304]{2,1,0:T(1,128)} all-to-all(f32[4,1,98304]{2,1,0:T(1,128)} %reshape.77), channel_id=1, replica_groups=mesh['dp'=4,'w'=4,'h'=8] {'w'}, dimensions={0} | all-to-all | bytes 3145728 | tf_op jit(solution)/shard_map/all_to_all | solution.py:98
  804.4 43.3 %reduce-scatter.7.cloned.1.call-done = f32[2,3,256,8,16]{2,3,1,0,4:T(8,128)} async-done(((f32[2,3,256,64,16]{2,3,1,0,4:T(8,128)}), f32[2,3,256,8,16]{2,3,1,0,4:T(8,128)}) %reduce-scatter.7.cloned.1.call-update) | async-done | bytes 786448 | tf_op jit(solution)/shard_map/reduce_scatter | solution.py:56
  871.6 34.4 %all-gather.5.cloned.1.call-done = f32[2,3,256,64,16]{2,4,1,3,0:T(8,128)} async-done(((f32[2,3,256,8,16]{2,4,1,3,0:T(8,128)}), f32[2,3,256,64,16]{2,4,1,3,0:T(8,128)}) %all-gather.5.cloned.1.call-update) | async-done | bytes 6291472 | tf_op jit(solution)/shard_map/all_gather | solution.py:59
  906.0 8.6 fusion.41
  914.6 11.4 copy.235
  967.0 10.5 reshape.80
  977.5 10.4 copy.237
  1061.2 33.0 %all-to-all-done.7 = f32[4,1,196608]{2,1,0:T(1,128)} async-done(((f32[4,1,196608]{2,1,0:T(1,128)}), f32[4,1,196608]{2,1,0:T(1,128)}, u32[]{:S(2)}, u32[]{:S(2)}) %all-to-all-start.7) | async-done | bytes 3145760 | tf_op jit(solution)/shard_map/all_to_all | solution.py:105
  1094.2 11.8 reduce.15
  1113.5 9.4 copy.320
  1123.0 9.0 copy.241
  1145.4 62.4 %psum.45 = f32[2,3,256,1,1]{2,1,4,3,0:T(4,128)S(1)} all-reduce(f32[2,3,256,1,1]{2,1,4,3,0:T(4,128)S(1)} %pad_maximum_fusion.16), channel_id=1, replica_groups=mesh['dp'=4,'w'=4,'h'=8] {'h','w'}, use_global_device_ids=true, to_apply=%region_10.11 | all-reduce | flops 1536 | bytes 12288 | tf_op jit(solution)/shard_map/psum | solution.py:106
  1214.1 67.3 %psum.44 = f32[]{:T(128)} all-reduce(f32[]{:T(128)} %get-tuple-element.28), channel_id=1, replica_groups=mesh['dp'=4,'w'=4,'h'=8] {'dp','h','w'}, use_global_device_ids=true, to_apply=%region_6.7 | all-reduce | flops 1 | bytes 8 | tf_op jit(solution)/shard_map/psum | solution.py:89
  (221 shorter events, 481.3 us)
Async XLA Ops:
  7.2 618.2 %copy-start = (bf16[512,256]{1,0:T(8,128)(2,1)S(1)}, bf16[512,256]{1,0:T(8,128)(2,1)}, u32[]{:S(2)}) copy-start(bf16[512,256]{1,0:T(8,128)(2,1)} %param.18) | copy-start | bytes 786436
  7.2 66.1 %copy-start.2 = (f32[3,256,16,64]{1,3,2,0:T(8,128)S(1)}, f32[3,256,16,64]{1,3,2,0:T(8,128)}, u32[]{:S(2)}) copy-start(f32[3,256,16,64]{1,3,2,0:T(8,128)} %param.11) | copy-start | bytes 9437188
  73.3 65.8 %copy-start.36 = (f32[3,256]{1,0:T(4,128)}, f32[3,256]{1,0:T(4,128)S(1)}, u32[]{:S(2)}) copy-start(f32[3,256]{1,0:T(4,128)S(1)} %multiply_bitcast_fusion) | copy-start | bytes 9220
  153.2 37.1 %all-to-all-start = ((f32[4,1,196608]{2,1,0:T(1,128)}), f32[4,1,196608]{2,1,0:T(1,128)}, u32[]{:S(2)}, u32[]{:S(2)}) async-start(f32[4,1,196608]{2,1,0:T(1,128)} %reshape.67), calls=%async_computation | async-start | bytes 6291456 | tf_op jit(solution)/shard_map/all_to_all | solution.py:73
  157.8 187.7 %reduce-scatter.5.cloned.1.call-start = ((), (), s32[]{:S(2)}) async-start(), calls=%async_computation.10 | async-start | bytes 7077888 | tf_op jit(solution)/shard_map/reduce_scatter | solution.py:56
  227.0 5.7 copy-start.10
  299.2 102.2 %all-gather.3.cloned.1.call-start = ((), (), s32[]{:S(2)}) async-start(), calls=%async_computation.11 | async-start | bytes 7077888 | tf_op jit(solution)/shard_map/all_gather | solution.py:59
  346.6 9.4 copy-start.20
  346.6 9.4 copy-start.26
  356.1 45.3 %copy-start.31 = (f32[16,64,16]{1,2,0:T(8,128)S(1)}, f32[16,64,16]{1,2,0:T(8,128)}, u32[]{:S(2)}) copy-start(f32[16,64,16]{1,2,0:T(8,128)} %param.15) | copy-start | bytes 196612
  515.8 5.3 copy-start.9
  515.8 5.3 copy-start.17
  629.2 5.0 copy-start.7
  629.2 6.6 copy-start.30
  652.4 40.2 %all-to-all-start.4 = ((f32[4,1,196608]{2,1,0:T(1,128)}), f32[4,1,196608]{2,1,0:T(1,128)}, u32[]{:S(2)}, u32[]{:S(2)}) async-start(f32[4,1,196608]{2,1,0:T(1,128)} %reshape.75), calls=%async_computation.5 | async-start | bytes 6291456 | tf_op jit(solution)/shard_map/all_to_all | solution.py:96
  657.1 190.6 %reduce-scatter.7.cloned.1.call-start = ((), (), s32[]{:S(2)}) async-start(), calls=%async_computation.12 | async-start | bytes 7077888 | tf_op jit(solution)/shard_map/reduce_scatter | solution.py:56
  728.8 5.7 copy-start.11
  803.9 102.1 %all-gather.5.cloned.1.call-start = ((), (), s32[]{:S(2)}) async-start(), calls=%async_computation.13 | async-start | bytes 7077888 | tf_op jit(solution)/shard_map/all_gather | solution.py:59
  848.8 11.3 copy-start.22
  848.8 11.3 copy-start.24
  864.7 41.3 %copy-start.33 = (f32[16,64,16]{1,2,0:T(8,128)S(1)}, f32[16,64,16]{1,2,0:T(8,128)}, u32[]{:S(2)}) copy-start(f32[16,64,16]{1,2,0:T(8,128)} %param.14) | copy-start | bytes 196612
  934.3 25.0 %all-to-all-start.6 = ((f32[4,1,98304]{2,1,0:T(1,128)}), f32[4,1,98304]{2,1,0:T(1,128)}, u32[]{:S(2)}, u32[]{:S(2)}) async-start(f32[4,1,98304]{2,1,0:T(1,128)} %reshape.79), calls=%async_computation.8 | async-start | bytes 3145728 | tf_op jit(solution)/shard_map/all_to_all | solution.py:103
  938.7 343.3 %all-reduce.19.cloned.1.call-start = ((), (), s32[]{:S(2)}) async-start(), calls=%async_computation.15 | async-start | bytes 2097152 | tf_op jit(solution)/shard_map/psum | solution.py:94
  946.6 6.4 copy-start.21
  946.6 6.4 copy-start.23
  992.0 6.3 copy-start.41
  1010.0 7.9 copy-start.4
  1025.6 6.3 copy-start.19
  1051.8 42.4 %all-to-all-start.7 = ((f32[4,1,196608]{2,1,0:T(1,128)}), f32[4,1,196608]{2,1,0:T(1,128)}, u32[]{:S(2)}, u32[]{:S(2)}) async-start(f32[4,1,196608]{2,1,0:T(1,128)} %reshape.81), calls=%async_computation.9 | async-start | bytes 6291456 | tf_op jit(solution)/shard_map/all_to_all | solution.py:105
  1056.5 225.5 %all-reduce.17.cloned.1.call-start = ((), (), s32[]{:S(2)}) async-start(), calls=%async_computation.14 | async-start | bytes 8388608 | tf_op jit(solution)/shard_map/psum | solution.py:100
  1282.0 5.5 copy-start.34
  1282.1 6.3 copy-start.1
  (22 other events, 65.2 us)
Sparse Core Ops, SparseCore 0:
  299.3 46.1 reduce-scatter.4
  360.2 41.0 all-gather.2
  804.0 43.5 reduce-scatter.6
  864.9 41.1 all-gather.4
  944.7 157.6 all-reduce.18
  1106.2 102.8 all-reduce.16
where the time goes:
time: 1310 us; the launch traced here: 1300 us
  blocking collectives  364 us (28%)
  local copies, waits for them, and re-layouts  353 us (27%)
  waiting for transfers between devices  262 us (20%)
  matrix products  157 us (12%)
  other arithmetic  124 us (9%)
  starting transfers between devices  19.3 us (1%)
  between operations  17.6 us (1%)
    unnamed x105, local copies, waits for them, and re-layouts  127 us
    reduce_scatter x2, waiting for transfers between devices, degree_from_lat(): return lax.psum_scatter(part_sums, 'h', scatter_dimension=3, tiled=True)  87.7 us
    all_gather x2, waiting for transfers between devices, lat_from_degree(): coeffs_all = lax.all_gather(coeffs, 'h', axis=3, tiled=True)  75.7 us
    dot_general x16, matrix products, precise_product(): jnp.einsum(einsum_form, operand_a, operand_b, precision=PRECISE, preferre...  73.5 us
    psum x1, blocking collectives, local_step(): loss = lax.psum(jnp.sum(d_out * residual), all_axes) / total_points  67.3 us
    psum x1, blocking collectives, local_step(): lax.psum(jnp.sum(field, axis=(2, 3), keepdims=True), grid_axes)  63.8 us
    psum x1, blocking collectives, local_step(): lax.psum(jnp.sum(centred * centred, axis=(2, 3), keepdims=True), grid_axes)  62.7 us
    psum x1, blocking collectives, local_step(): lax.psum(jnp.stack([jnp.sum(d_normed, axis=(2, 3), keepdims=True), jnp.su...  62.4 us
  transfers between devices with their start and end apart: 10, of which 8 were waited for; matrix products, arithmetic and copies ran while one was open for 14% of the time, Pallas kernels for 0%

commit v1 on v0

v1 whole, which is shorter than its diff:
```python
import functools
import jax
import jax.numpy as jnp
import numpy as np
from jax import lax
from jax.sharding import PartitionSpec as P

NORM_EPS = 1e-5
PRECISE = lax.Precision.HIGHEST


def mm(form, a, b):
    return jnp.einsum(form, a, b, precision=PRECISE, preferred_element_type=jnp.float32)


def dft_tables(lon_count, num_modes):
    modes, lons = np.arange(num_modes), np.arange(lon_count)
    angle = 2.0 * np.pi * ((modes[:, None] * lons[None, :]) % lon_count) / lon_count
    scale = lon_count ** -0.5
    fwd = np.stack([np.cos(angle), -np.sin(angle)], 0) * scale
    weight = np.where(modes == 0, 1.0, 2.0)[None, :, None]
    inv = fwd * weight

    def rows(table):
        table = table.reshape(2, num_modes // 4, 4, lon_count).transpose(1, 0, 2, 3)
        return table.reshape(2 * num_modes, lon_count).astype(np.float32)

    return rows(fwd), rows(inv)


def solution(mesh):
    dp_size = mesh.shape["dp"]
    w_size = mesh.shape["w"]
    h_size = mesh.shape["h"]
    grid_axes = ("h", "w")
    all_axes = ("dp", "h", "w")
    xs = h_size // 2

    def swap(pieces, axes):
        return lax.all_to_all(pieces, axes, 0, 0, tiled=True)

    def local_step(field, target, lat_weight, leg_fwd, leg_inv, spec_w, w_in, w_out):
        nb, nc, nt, npl = field.shape
        nlon = npl * w_size
        tq = nt // w_size
        nm = leg_fwd.shape[0] * w_size
        ng = nm // 4
        half = nc // 2
        ndev = h_size * w_size
        nlat = nt * h_size
        nl = leg_fwd.shape[1]
        l_own = nl // ndev
        grid_points = nlat * nlon
        total_points = nb * dp_size * nc * grid_points
        hi, wi = lax.axis_index("h"), lax.axis_index("w")
        fwd_np, inv_np = dft_tables(nlon, nm)
        f_tab, g_tab = jnp.asarray(fwd_np), jnp.asarray(inv_np)

        x = field.transpose(0, 2, 3, 1)
        tgt = target.transpose(0, 2, 3, 1)

        def to_rows(v):
            v = v.reshape(nb, w_size, tq, npl, nc).transpose(1, 0, 2, 3, 4)
            v = swap(v, "w")
            return v.transpose(1, 2, 0, 3, 4).reshape(nb, tq, nlon, nc)

        def from_rows(v):
            v = v.reshape(nb, tq, w_size, npl, nc).transpose(2, 0, 1, 3, 4)
            v = swap(v, "w")
            return v.transpose(1, 0, 2, 3, 4).reshape(nb, nt, npl, nc)

        loc_mean = jnp.mean(x, axis=(1, 2))
        loc_m2 = jnp.sum((x - loc_mean[:, None, None, :]) ** 2, axis=(1, 2))
        stats = lax.all_gather(jnp.stack([loc_mean, loc_m2]), grid_axes)
        mu = jnp.mean(stats[:, 0], axis=0)
        m2 = jnp.sum(stats[:, 1], axis=0) + (nt * npl) * jnp.sum((stats[:, 0] - mu) ** 2, axis=0)
        inv_std = lax.rsqrt(m2 / grid_points + NORM_EPS)
        lane0 = (hi % 2) * half
        mu_h = lax.dynamic_slice_in_dim(mu, lane0, half, 1)
        std_h = lax.dynamic_slice_in_dim(inv_std, lane0, half, 1)

        def tab(leg):
            v = leg.transpose(0, 2, 1).reshape(xs, 4, nt, nl)
            v = jnp.repeat(v, 2, axis=0)
            v = swap(v, "h")
            return v.transpose(1, 0, 2, 3).reshape(4, nlat, nl)

        p_t, q_t = tab(leg_fwd), tab(leg_inv)

        def spread(v):
            v = v.reshape(nb, tq, w_size, xs, 8, 2, half).transpose(3, 5, 2, 0, 1, 4, 6)
            v = v.reshape(ndev, nb, tq, 8, half)
            v = swap(v, grid_axes)
            return v.transpose(1, 0, 2, 3, 4).reshape(nb, nlat, 8, half)

        def gather(v):
            v = v.reshape(nb, ndev, tq, 8, half).transpose(1, 0, 2, 3, 4)
            v = swap(v, grid_axes)
            v = v.reshape(xs, 2, w_size, nb, tq, 8, half).transpose(3, 4, 2, 0, 5, 1, 6)
            return v.reshape(nb, tq, ng * 8, nc)

        def to_owner(v):
            v = v.reshape(ndev, l_own, nb, 8, half)
            v = swap(v, grid_axes)
            v = v.reshape(xs, 2, w_size, l_own, nb, 8, half).transpose(3, 4, 2, 0, 5, 1, 6)
            return v.reshape(l_own, nb, ng, 2, 4, nc)

        def from_owner(v):
            v = v.reshape(l_own, nb, w_size, xs, 8, 2, half).transpose(3, 5, 2, 0, 1, 4, 6)
            v = v.reshape(ndev, l_own, nb, 8, half)
            v = swap(v, grid_axes)
            return v.reshape(nl, nb, 2, 4, half)

        def leg_down(tab_t, v):
            v = v.reshape(nb, nlat, 2, 4, half)
            return mm("mtl,btrmc->lbrmc", tab_t, v)

        def leg_up(tab_t, v):
            return mm("mtl,lbrmc->btrmc", tab_t, v).reshape(nb, nlat, 8, half)

        x2 = to_rows(x)
        t2 = to_rows(tgt)
        spec = mm("rp,btpc->btrc", f_tab, x2)
        sp = spread(spec)
        has0 = jnp.where((hi // 2 == 0) & (wi == 0), jnp.float32(nlon ** 0.5), 0.0)
        corr = jnp.zeros((8, 1), jnp.float32).at[0, 0].set(1.0) * has0
        sp = sp - corr[None, None] * mu_h[:, None, None, :]
        a_loc = leg_down(p_t, sp) * std_h[None, :, None, None, :]
        a = to_owner(a_loc)
        me = hi * w_size + wi
        ker = lax.dynamic_slice_in_dim(spec_w, me * l_own, l_own, 1)
        kr, ki = ker[0], ker[1]
        b1 = mm("lbgrmi,lio->lbgrmo", a, kr)
        b2 = mm("lbgrmi,lio->lbgrmo", a, ki)
        sgn = jnp.asarray(np.array([-1.0, 1.0], np.float32))[:, None, None]
        mixed = b1 + sgn * b2[:, :, :, ::-1]
        back = gather(leg_up(q_t, from_owner(mixed)))
        y = mm("rp,btrc->btpc", g_tab, back)
        y_bf = y.astype(jnp.bfloat16)
        hid = jnp.einsum("btpc,cf->btpf", y_bf, w_in, preferred_element_type=jnp.float32)
        act, gelu_pull = jax.vjp(jax.nn.gelu, hid)
        act_bf = act.astype(jnp.bfloat16)
        out = jnp.einsum("btpf,fc->btpc", act_bf, w_out, preferred_element_type=jnp.float32)
        resid = x2 + y + out - t2
        q4 = lax.dynamic_slice_in_dim(lat_weight, wi * tq, tq, 0)
        d_out = q4[None, :, None, None] * resid
        loss = lax.psum(jnp.sum(d_out * resid), all_axes) / total_points
        d_out_bf = d_out.astype(jnp.bfloat16)
        g_out = lax.psum(jnp.einsum("btpf,btpc->fc", act_bf, d_out_bf, preferred_element_type=jnp.float32), all_axes)
        d_act = jnp.einsum("btpc,fc->btpf", d_out_bf, w_out, preferred_element_type=jnp.float32)
        d_hid = gelu_pull(d_act)[0].astype(jnp.bfloat16)
        g_in = lax.psum(jnp.einsum("btpc,btpf->cf", y_bf, d_hid, preferred_element_type=jnp.float32), all_axes)
        d_y = d_out + jnp.einsum("btpf,cf->btpc", d_hid, w_in, preferred_element_type=jnp.float32)
        d_back = spread(mm("rp,btpc->btrc", g_tab, d_y))
        d_mixed = to_owner(leg_down(q_t, d_back))
        d1 = mm("lbgrmo,lio->lbgrmi", d_mixed, kr)
        d2 = mm("lbgrmo,lio->lbgrmi", d_mixed, ki)
        d_a = d1 - sgn * d2[:, :, :, ::-1]
        rot = -sgn * d_mixed[:, :, :, ::-1]
        gr = mm("lbgrmi,lbgrmo->lio", a, d_mixed)
        gi = mm("lbgrmi,lbgrmo->lio", a, rot)
        grad_spec = lax.psum(jnp.stack([gr, gi]), "dp")
        grad_spec = lax.all_gather(grad_spec, "w", axis=1, tiled=True)
        d_sp = leg_up(p_t, from_owner(d_a))
        s1_h = has0 * jnp.sum(d_sp[:, :, 0], axis=1)
        s1 = lax.dynamic_update_slice_in_dim(jnp.zeros((nb, nc), jnp.float32), s1_h, lane0, 1)
        s2 = jnp.sum(d_a * a, axis=(0, 2, 3, 4))
        bstat = lax.psum(jnp.stack([s1, s2]), grid_axes) / grid_points
        d_n = mm("rp,btrc->btpc", f_tab, gather(d_sp))
        row = lambda v: v[:, None, None, :]
        normed = (x2 - row(mu)) * row(inv_std)
        d_x = d_out + row(inv_std) * (d_n - row(bstat[0]) - normed * row(bstat[1]))
        d_field = from_rows(d_x).transpose(0, 3, 1, 2)
        return loss, d_field, grad_spec, g_in, g_out

    grid_spec = P("dp", None, "h", "w")
    table_spec = P("w", None, "h")
    kernel_spec = P(None, "h", None, None)
    return jax.shard_map(local_step, mesh=mesh, in_specs=(grid_spec, grid_spec, P("h"), table_spec, table_spec, P(), P(), P()), out_specs=(P(), grid_spec, kernel_spec, P(), P()), check_vma=False)
```

time: 1310 us -> 737 us (0.56)
  local copies, waits for them, and re-layouts: 353 us -> 86 us
  other arithmetic: 124 us -> 7.18 us
  matrix products: 157 us -> 58.2 us
  blocking collectives: 364 us -> 287 us
  waiting for transfers between devices: 262 us -> 212 us
  starting transfers between devices: 19.3 us -> 59.1 us
    psum x2, waiting for transfers between devices: 0.04 us -> 117 us  [the longest x1 72.3 us: local_step(): lax.psum(jnp.einsum('btpc,btpf->cf', y_bf, d_hid, preferred_element_type=...]
    unnamed x105 -> x69, local copies, waits for them, and re-layouts: 127 us -> 18.5 us
    all_to_all x14 -> x2, local copies, waits for them, and re-layouts: 101 us -> 4.42 us  [swap(): return lax.all_to_all(pieces, axes, 0, 0, tiled=True)]
    psum x4 -> x2, blocking collectives: 256 us -> 161 us  [the longest x1 83.9 us: local_step(): loss = lax.psum(jnp.sum(d_out * resid), all_axes) / total_points]
    reduce_scatter x2 -> x0, waiting for transfers between devices: 87.7 us -> none  [degree_from_lat(): return lax.psum_scatter(part_sums, 'h', scatter_dimension=3, tiled=True)]
    all_gather x2 -> x1, waiting for transfers between devices: 75.7 us -> 0.01 us  [local_step(): grad_spec = lax.all_gather(grad_spec, 'w', axis=1, tiled=True)]
    all_to_all x8 -> x2, other arithmetic: 76.7 us -> 5.03 us  [swap(): return lax.all_to_all(pieces, axes, 0, 0, tiled=True)]
    another operation x11 -> x0, matrix products: 58 us -> none  [the longest x6 34.2 us: lon_forward(): jnp.fft.rfft(grid_vals, axis=3, norm='ortho')[:, :, :, :num_modes]]
  transfers between devices with their start and end apart: 10 -> 13, of which waited for: 8 -> 7; matrix products, arithmetic and copies ran while one was open for 14% -> 13% of each run, Pallas kernels for 0% -> 0%
where the time goes in v1:
time: 737 us; the launch traced here: 729 us
  blocking collectives  287 us (39%)
  waiting for transfers between devices  212 us (29%)
  local copies, waits for them, and re-layouts  86 us (12%)
  starting transfers between devices  59.1 us (8%)
  matrix products  58.2 us (8%)
  between operations  18.3 us (2%)
    all_to_all x10, waiting for transfers between devices, swap(): return lax.all_to_all(pieces, axes, 0, 0, tiled=True)  95.9 us
    psum x1, blocking collectives, local_step(): loss = lax.psum(jnp.sum(d_out * resid), all_axes) / total_points  83.9 us
    psum x1, blocking collectives, local_step(): bstat = lax.psum(jnp.stack([s1, s2]), grid_axes) / grid_points  77.6 us
    psum x1, waiting for transfers between devices, local_step(): lax.psum(jnp.einsum('btpc,btpf->cf', y_bf, d_hid, preferred_element_type=...  72.3 us
    all_to_all x3, blocking collectives, swap(): return lax.all_to_all(pieces, axes, 0, 0, tiled=True)  71.3 us
    all_to_all x10, starting transfers between devices, swap(): return lax.all_to_all(pieces, axes, 0, 0, tiled=True)  59 us
    all_gather x1, blocking collectives, local_step(): stats = lax.all_gather(jnp.stack([loc_mean, loc_m2]), grid_axes)  54.7 us
    psum x1, waiting for transfers between devices, local_step(): grad_spec = lax.psum(jnp.stack([gr, gi]), 'dp')  44.2 us
  transfers between devices with their start and end apart: 13, of which 7 were waited for; matrix products, arithmetic and copies ran while one was open for 13% of the time, Pallas kernels for 0%

profile of v1, /device:TPU:1, one launch (start us, length us, event | category | flops | bytes accessed | tf_op | source)
XLA Modules:
  0.0 728.7 jit_solution(3766585596664814325)
XLA Ops:
  8.0 4.0 copy.110
  12.0 5.3 all-to-all-start
  20.3 34.3 %all-to-all-done = f32[4,3,4,64,256]{4,3,2,1,0:T(8,128)} async-done(((f32[4,3,4,64,256]{4,3,2,1,0:T(8,128)}), f32[4,3,4,64,256]{4,3,2,1,0:T(8,128)}, u32[]{:S(2)}, u32[]{:S(2)}) %all-to-all-start) | async-done | bytes 3145760 | tf_op jit(solution)/shard_map/all_to_all | solution.py:40
  54.6 5.9 all-to-all-start.2
  65.9 5.6 all-to-all-start.1
  71.6 54.7 %all-gather = f32[64,3,256]{2,1,0:T(4,128)S(1)} all-gather(f32[2,3,256]{2,1,0:T(4,128)S(1)} %pad_maximum_fusion.1), channel_id=2, replica_groups=mesh['dp'=4,'w'=4,'h'=8] {'h','w'}, dimensions={0}, use_global_device_ids=true | all-gather | bytes 202752 | tf_op jit(solution)/shard_map/all_gather | solution.py:74
  137.9 8.3 %all-to-all-start.3 = ((f32[32,2,3,8,128]{4,3,2,1,0:T(8,128)}), f32[32,2,3,8,128]{4,3,2,1,0:T(8,128)}, u32[]{:S(2)}, u32[]{:S(2)}) async-start(f32[32,2,3,8,128]{4,3,2,1,0:T(8,128)} %bitcast.271), calls=%async_computation.3 | async-start | bytes 1572864 | tf_op jit(solution)/shard_map/all_to_all | solution.py:40
  149.6 9.7 %all-to-all-done.3 = f32[32,2,3,8,128]{4,3,2,1,0:T(8,128)} async-done(((f32[32,2,3,8,128]{4,3,2,1,0:T(8,128)}), f32[32,2,3,8,128]{4,3,2,1,0:T(8,128)}, u32[]{:S(2)}, u32[]{:S(2)}) %all-to-all-start.3) | async-done | bytes 786464 | tf_op jit(solution)/shard_map/all_to_all | solution.py:40
  159.3 5.7 all-to-all-start.5
  183.5 5.9 all-to-all-start.4
  189.4 3.9 copy.126
  193.3 9.2 %all-to-all-done.4 = f32[32,2,3,8,128]{4,3,2,1,0:T(8,128)} async-done(((f32[32,2,3,8,128]{4,3,2,1,0:T(8,128)}), f32[32,2,3,8,128]{4,3,2,1,0:T(8,128)}, u32[]{:S(2)}, u32[]{:S(2)}) %all-to-all-start.4) | async-done | bytes 786464 | tf_op jit(solution)/shard_map/all_to_all | solution.py:40
  202.5 4.6 all-to-all-start.7
  217.9 25.5 %all-to-all-done.7 = f32[4,3,4,64,256]{4,3,2,1,0:T(8,128)} async-done(((f32[4,3,4,64,256]{4,3,2,1,0:T(8,128)}), f32[4,3,4,64,256]{4,3,2,1,0:T(8,128)}, u32[]{:S(2)}, u32[]{:S(2)}) %all-to-all-start.7) | async-done | bytes 3145760 | tf_op jit(solution)/shard_map/all_to_all | solution.py:40
  243.4 7.3 all-to-all-start.6
  250.8 3.9 copy.127
  254.7 17.4 %all-to-all-done.6 = f32[32,3,4,8,128]{4,3,2,1,0:T(8,128)} async-done(((f32[32,3,4,8,128]{4,3,2,1,0:T(8,128)}), f32[32,3,4,8,128]{4,3,2,1,0:T(8,128)}, u32[]{:S(2)}, u32[]{:S(2)}) %all-to-all-start.6) | async-done | bytes 1572896 | tf_op jit(solution)/shard_map/all_to_all | solution.py:40
  279.5 4.0 fusion.7
  283.5 4.9 fusion.6
  290.0 6.3 fusion.18
  301.0 29.2 %all_to_all.65 = f32[32,3,4,8,128]{4,3,2,1,0:T(8,128)S(1)} all-to-all(f32[32,3,4,8,128]{4,3,2,1,0:T(8,128)S(1)} %bitcast.263), channel_id=1, replica_groups=mesh['dp'=4,'w'=4,'h'=8] {'h','w'}, dimensions={0} | all-to-all | bytes 3145728 | tf_op jit(solution)/shard_map/all_to_all | solution.py:40
  332.1 18.1 %all_to_all.66 = f32[32,2,3,8,128]{4,3,2,1,0:T(8,128)S(1)} all-to-all(f32[32,2,3,8,128]{4,3,2,1,0:T(8,128)S(1)} %bitcast.273), channel_id=1, replica_groups=mesh['dp'=4,'w'=4,'h'=8] {'h','w'}, dimensions={0} | all-to-all | bytes 1572864 | tf_op jit(solution)/shard_map/all_to_all | solution.py:40
  360.2 44.2 %all-reduce.4.cloned.1.call-done = f32[2,2,256,256]{3,2,1,0:T(8,128)} async-done(((f32[2,2,256,256]{3,2,1,0:T(8,128)}), f32[2,2,256,256]{3,2,1,0:T(8,128)}) %all-reduce.4.cloned.1.call-update) | async-done | bytes 1048592 | tf_op jit(solution)/shard_map/psum | solution.py:162
  417.2 24.0 %all_to_all.67 = f32[32,2,3,8,128]{4,3,2,1,0:T(8,128)S(1)} all-to-all(f32[32,2,3,8,128]{4,3,2,1,0:T(8,128)S(1)} %bitcast.275), channel_id=1, replica_groups=mesh['dp'=4,'w'=4,'h'=8] {'h','w'}, dimensions={0} | all-to-all | bytes 1572864 | tf_op jit(solution)/shard_map/all_to_all | solution.py:40
  446.1 5.5 all-to-all-start.11
  453.2 77.6 %psum.36 = f32[2,3,256]{2,1,0:T(4,128)S(1)} all-reduce(f32[2,3,256]{2,1,0:T(4,128)S(1)} %pad_maximum_fusion.2), channel_id=1, replica_groups=mesh['dp'=4,'w'=4,'h'=8] {'h','w'}, use_global_device_ids=true, to_apply=%region_9.10 | all-reduce | flops 1536 | bytes 12288 | tf_op jit(solution)/shard_map/psum | solution.py:168
  538.6 4.9 all-to-all-start.12
  547.4 5.3 convolution_bitcast_fusion.2
  552.7 83.9 %psum.35 = f32[]{:T(128)} all-reduce(f32[]{:T(128)} %get-tuple-element.25), channel_id=1, replica_groups=mesh['dp'=4,'w'=4,'h'=8] {'dp','h','w'}, use_global_device_ids=true, to_apply=%region_6.7 | all-reduce | flops 1 | bytes 8 | tf_op jit(solution)/shard_map/psum | solution.py:147
  637.2 3.9 copy.146
  641.1 72.3 %all-reduce.6.cloned.1.call-done = (f32[256,512]{1,0:T(8,128)}, f32[512,256]{1,0:T(8,128)}) async-done(((f32[256,512]{1,0:T(8,128)}, f32[512,256]{1,0:T(8,128)}), (f32[256,512]{1,0:T(8,128)}, f32[512,256]{1,0:T(8,128)})) %all-reduce.6.cloned.1.call-update) | async-done | bytes 1048592 | tf_op jit(solution)/shard_map/psum | solution.py:152
  713.4 4.7 copy.211
  (151 shorter events, 110.7 us)
Async XLA Ops:
  8.0 270.2 %copy-start = (bf16[512,256]{1,0:T(8,128)(2,1)S(1)}, bf16[512,256]{1,0:T(8,128)(2,1)}, u32[]{:S(2)}) copy-start(bf16[512,256]{1,0:T(8,128)(2,1)} %param.20) | copy-start | bytes 786436
  12.0 5.3 copy-start.23
  12.0 7.8 %copy-start.2 = (f32[3,256,16,64]{1,3,2,0:T(8,128)S(1)}, f32[3,256,16,64]{1,3,2,0:T(8,128)}, u32[]{:S(2)}) copy-start(f32[3,256,16,64]{1,3,2,0:T(8,128)} %param.13) | copy-start | bytes 9437188
  12.0 42.6 %all-to-all-start = ((f32[4,3,4,64,256]{4,3,2,1,0:T(8,128)}), f32[4,3,4,64,256]{4,3,2,1,0:T(8,128)}, u32[]{:S(2)}, u32[]{:S(2)}) async-start(f32[4,3,4,64,256]{4,3,2,1,0:T(8,128)} %copy.110), calls=%async_computation | async-start | bytes 6291456 | tf_op jit(solution)/shard_map/all_to_all | solution.py:40
  54.6 11.3 %all-to-all-start.2 = ((f32[8,1,4096]{2,1,0:T(1,128)}), f32[8,1,4096]{2,1,0:T(1,128)}, u32[]{:S(2)}, u32[]{:S(2)}) async-start(f32[8,1,4096]{2,1,0:T(1,128)} %reshape.255), calls=%async_computation.2 | async-start | bytes 262144 | tf_op jit(solution)/shard_map/all_to_all | solution.py:40
  64.6 62.5 %copy-start.28 = (f32[2,4]{1,0:T(2,128)S(1)}, f32[2,4]{1,0:T(2,128)}, u32[]{:S(2)}) copy-start(f32[2,4]{1,0:T(2,128)} %constant.100.clone.1) | copy-start | bytes 100
  65.9 67.6 %all-to-all-start.1 = ((f32[32,3,4,8,128]{4,3,2,1,0:T(8,128)}), f32[32,3,4,8,128]{4,3,2,1,0:T(8,128)}, u32[]{:S(2)}, u32[]{:S(2)}) async-start(f32[32,3,4,8,128]{4,3,2,1,0:T(8,128)} %bitcast.257), calls=%async_computation.1 | async-start | bytes 3145728 | tf_op jit(solution)/shard_map/all_to_all | solution.py:40
  137.9 21.4 %all-to-all-start.3 = ((f32[32,2,3,8,128]{4,3,2,1,0:T(8,128)}), f32[32,2,3,8,128]{4,3,2,1,0:T(8,128)}, u32[]{:S(2)}, u32[]{:S(2)}) async-start(f32[32,2,3,8,128]{4,3,2,1,0:T(8,128)} %bitcast.271), calls=%async_computation.3 | async-start | bytes 1572864 | tf_op jit(solution)/shard_map/all_to_all | solution.py:40
  159.3 24.2 %all-to-all-start.5 = ((f32[8,1,4096]{2,1,0:T(1,128)}), f32[8,1,4096]{2,1,0:T(1,128)}, u32[]{:S(2)}, u32[]{:S(2)}) async-start(f32[8,1,4096]{2,1,0:T(1,128)} %reshape.253), calls=%async_computation.5 | async-start | bytes 262144 | tf_op jit(solution)/shard_map/all_to_all | solution.py:40
  165.0 10.4 %copy-start.27 = (f32[2]{0:T(128)S(1)}, f32[2]{0:T(128)}, u32[]{:S(2)}) copy-start(f32[2]{0:T(128)} %constant.124.clone) | copy-start | bytes 28
  183.5 19.0 %all-to-all-start.4 = ((f32[32,2,3,8,128]{4,3,2,1,0:T(8,128)}), f32[32,2,3,8,128]{4,3,2,1,0:T(8,128)}, u32[]{:S(2)}, u32[]{:S(2)}) async-start(f32[32,2,3,8,128]{4,3,2,1,0:T(8,128)} %bitcast.272), calls=%async_computation.4 | async-start | bytes 1572864 | tf_op jit(solution)/shard_map/all_to_all | solution.py:40
  202.5 40.9 %all-to-all-start.7 = ((f32[4,3,4,64,256]{4,3,2,1,0:T(8,128)}), f32[4,3,4,64,256]{4,3,2,1,0:T(8,128)}, u32[]{:S(2)}, u32[]{:S(2)}) async-start(f32[4,3,4,64,256]{4,3,2,1,0:T(8,128)} %copy.126), calls=%async_computation.7 | async-start | bytes 6291456 | tf_op jit(solution)/shard_map/all_to_all | solution.py:40
  216.6 34.1 %copy-start.30 = (f32[16]{0:T(128)S(1)}, f32[16]{0:T(128)}, u32[]{:S(2)}) copy-start(f32[16]{0:T(128)} %param.15) | copy-start | bytes 196
  243.4 28.7 %all-to-all-start.6 = ((f32[32,3,4,8,128]{4,3,2,1,0:T(8,128)}), f32[32,3,4,8,128]{4,3,2,1,0:T(8,128)}, u32[]{:S(2)}, u32[]{:S(2)}) async-start(f32[32,3,4,8,128]{4,3,2,1,0:T(8,128)} %copy.124), calls=%async_computation.6 | async-start | bytes 3145728 | tf_op jit(solution)/shard_map/all_to_all | solution.py:40
  250.6 153.8 %all-reduce.4.cloned.1.call-start = ((), (), s32[]{:S(2)}) async-start(), calls=%async_computation.13 | async-start | bytes 2097152 | tf_op jit(solution)/shard_map/psum | solution.py:162
  276.5 3.0 copy-start.13
  279.5 4.0 copy-start.12
  283.5 6.0 copy-start.9
  301.0 29.3 %copy-start.17 = (f32[4,8,16,64]{3,2,1,0:T(8,128)S(1)}, f32[4,8,16,64]{3,2,1,0:T(8,128)}, u32[]{:S(2)}) copy-start(f32[4,8,16,64]{3,2,1,0:T(8,128)} %copy-done.16) | copy-start | bytes 393220
  354.4 3.0 copy-start.29
  354.4 3.2 copy-start.6
  360.2 281.0 %all-gather.3.cloned.1.call-start = ((), (), s32[]{:S(2)}) async-start(), calls=%async_computation.14 | async-start | bytes 5242880 | tf_op jit(solution)/shard_map/all_gather | solution.py:163
  413.2 28.0 %copy-start.15 = (f32[4,8,16,64]{3,2,1,0:T(8,128)S(1)}, f32[4,8,16,64]{3,2,1,0:T(8,128)}, u32[]{:S(2)}) copy-start(f32[4,8,16,64]{3,2,1,0:T(8,128)} %copy.114) | copy-start | bytes 393220
  446.1 84.8 %all-to-all-start.11 = ((f32[32,3,4,8,128]{4,3,2,1,0:T(8,128)}), f32[32,3,4,8,128]{4,3,2,1,0:T(8,128)}, u32[]{:S(2)}, u32[]{:S(2)}) async-start(f32[32,3,4,8,128]{4,3,2,1,0:T(8,128)} %copy.141), calls=%async_computation.11 | async-start | bytes 3145728 | tf_op jit(solution)/shard_map/all_to_all | solution.py:40
  451.6 81.0 %copy-start.25 = (f32[3,256]{1,0:T(4,128)S(1)}, f32[3,256]{1,0:T(4,128)}, u32[]{:S(2)}) copy-start(f32[3,256]{1,0:T(4,128)} %copy-done.24) | copy-start | bytes 9220
  538.6 5.0 copy-start.4
  538.6 98.7 %all-to-all-start.12 = ((f32[4,3,4,64,256]{4,3,2,1,0:T(8,128)}), f32[4,3,4,64,256]{4,3,2,1,0:T(8,128)}, u32[]{:S(2)}, u32[]{:S(2)}) async-start(f32[4,3,4,64,256]{4,3,2,1,0:T(8,128)} %bitcast.255), calls=%async_computation.12 | async-start | bytes 6291456 | tf_op jit(solution)/shard_map/all_to_all | solution.py:40
  543.5 169.9 %all-reduce.6.cloned.1.call-start = ((), (), s32[]{:S(2)}) async-start(), calls=%async_computation.15 | async-start | bytes 2097152 | tf_op jit(solution)/shard_map/psum | solution.py:152
  543.5 3.9 copy-start.11
  713.4 4.7 copy-start.22
  713.4 5.5 copy-start.21
  713.4 6.3 copy-start.1
  (12 other events, 21.4 us)
Sparse Core Ops, SparseCore 0:
  360.3 44.1 all-reduce.3
  406.1 74.2 all-gather.2
Sparse Core Ops, SparseCore 1:
  552.8 160.6 all-reduce.5

commit v2 on v1

v2 whole, which is shorter than its diff:
```python
import functools
import jax
import jax.numpy as jnp
import numpy as np
from jax import lax
from jax.experimental import pallas as pl
from jax.experimental.pallas import tpu as pltpu
from jax.sharding import PartitionSpec as P

NORM_EPS = 1e-5
PRECISE = lax.Precision.HIGHEST
MESH = pl.DeviceIdType.MESH
F32 = jnp.float32


def mm(form, a, b):
    return jnp.einsum(form, a, b, precision=PRECISE, preferred_element_type=F32)


def dot(a, b):
    return jnp.dot(a, b, precision=PRECISE, preferred_element_type=F32)


def dft_tables(lon_count, num_modes):
    modes, lons = np.arange(num_modes), np.arange(lon_count)
    angle = 2.0 * np.pi * ((modes[:, None] * lons[None, :]) % lon_count) / lon_count
    fwd = np.stack([np.cos(angle), -np.sin(angle)], 0) * lon_count ** -0.5
    inv = fwd * np.where(modes == 0, 1.0, 2.0)[None, :, None]

    def rows(table):
        table = table.reshape(2, num_modes // 4, 4, lon_count).transpose(1, 0, 2, 3)
        return table.reshape(2 * num_modes, lon_count).astype(np.float32)

    return rows(fwd), rows(inv)


class Plane:
    def __init__(self, h_size, w_size):
        self.h_size, self.w_size = h_size, w_size
        self.h, self.w = lax.axis_index("h"), lax.axis_index("w")
        self.me = self.h * w_size + self.w
        self.group = self.w * (h_size // 2) + self.h // 2
        self.half = self.h % 2

    def barrier(self):
        sem = pltpu.get_barrier_semaphore()
        count = self.h_size * self.w_size

        def body(k, _):
            h, w = self.peer(k)
            pl.semaphore_signal(sem, inc=1, device_id={"h": h, "w": w}, device_id_type=MESH)
            return 0

        lax.fori_loop(1, count, body, 0)
        pl.semaphore_wait(sem, count - 1)

    def peer(self, k):
        return (self.h + k // self.w_size) % self.h_size, (self.w + k % self.w_size) % self.w_size

    def each(self, refs):
        src, dst, _, recv = refs(self.h, self.w, self.me, self.group, self.half)
        pltpu.make_async_copy(src, dst, recv).start()

        def body(k, _):
            h, w = self.peer(k)
            src, dst, send, recv = refs(h, w, h * self.w_size + w, w * (self.h_size // 2) + h // 2, h % 2)
            pltpu.make_async_remote_copy(src_ref=src, dst_ref=dst, send_sem=send, recv_sem=recv,
                                         device_id={"h": h, "w": w}, device_id_type=MESH).start()
            return 0

        lax.fori_loop(1, self.h_size * self.w_size, body, 0)


def drain(ref, sem):
    pltpu.make_async_copy(ref, ref, sem).wait()


def rows_at(i, n):
    return pl.ds(pl.multiple_of(i * n, n), n)


def lanes_at(half):
    return pl.ds(pl.multiple_of(half * 128, 128), 128)


def forward_kernel(h_size, w_size, x, tgt, leg_p, leg_q, spec_w, f_tab,
                   x2_out, t2_out, a_out, y_out, st_out, p_out, q_out,
                   xr, tr, xs, sr, als, ar, bs, br, ys, yr, st_s, st, pt, qt, ker,
                   sem_x, sem_s, sem_a, sem_b, sem_y, sem_m, sem_t):
    pn = Plane(h_size, w_size)
    nb = x.shape[0]
    tq = x.shape[1] // w_size
    npl = x.shape[2]
    l_own = als.shape[1] // 8 // (h_size * w_size)
    load_k = pltpu.make_async_copy(spec_w.at[:, pl.ds(pn.me * l_own, l_own)], ker, sem_m.at[0])
    load_k.start()
    pn.barrier()

    def send_rows(src, dst, b, sem):
        pltpu.make_async_copy(src.at[b, rows_at(pn.w, tq)], dst.at[b, :, rows_at(pn.w, npl)], sem.at[1, b]).start()
        for step in (1, 3, 2):
            w = (pn.w + step) % w_size
            pltpu.make_async_remote_copy(src_ref=src.at[b, rows_at(w, tq)], dst_ref=dst.at[b, :, rows_at(pn.w, npl)],
                                         send_sem=sem.at[0, b], recv_sem=sem.at[1, b],
                                         device_id={"w": w}, device_id_type=MESH).start()

    def send_table(src, dst, k):
        pltpu.make_async_copy(src.at[rows_at(pn.h // 2, 4)], dst.at[:, rows_at(pn.h, src.shape[1])], sem_t.at[1, k]).start()

        def body(step, _):
            h = (pn.h + step) % h_size
            pltpu.make_async_remote_copy(src_ref=src.at[rows_at(h // 2, 4)], dst_ref=dst.at[:, rows_at(pn.h, src.shape[1])],
                                         send_sem=sem_t.at[0, k], recv_sem=sem_t.at[1, k],
                                         device_id={"h": h}, device_id_type=MESH).start()
            return 0
        lax.fori_loop(1, h_size, body, 0)

    for b in range(nb):
        send_rows(x, xr, b, sem_x)
    send_table(leg_p, pt, 0)
    send_table(leg_q, qt, 1)

    for b in range(nb):
        drain(xr.at[b], sem_x.at[1, b])

        def spec(t, total, b=b):
            rows = xr[b, t]
            out = dot(f_tab[...], rows).reshape(-1, 8, rows.shape[1])
            for hf in range(2):
                xs[:, hf, b, rows_at(t, 8), :] = out[:, :, hf * 128:(hf + 1) * 128]
            return total + jnp.sum(rows, axis=0, keepdims=True)

        total = lax.fori_loop(0, tq, spec, jnp.zeros((1, xr.shape[3]), F32))
        pn.each(lambda h, w, lin, g, hf, b=b: (xs.at[g, hf, b], sr.at[b, rows_at(pn.me, 8 * tq)], sem_s.at[0, b], sem_s.at[1, b]))
        mean = total / (tq * xr.shape[2])

        def spread2(t, total, b=b, mean=mean):
            d = xr[b, t] - mean
            return total + jnp.sum(d * d, axis=0, keepdims=True)

        m2 = lax.fori_loop(0, tq, spread2, jnp.zeros((1, xr.shape[3]), F32))
        st_s[2 * b:2 * b + 1, :] = mean
        st_s[2 * b + 1:2 * b + 2, :] = m2
    st_s[2 * nb:, :] = jnp.zeros_like(st_s[2 * nb:, :])
    pn.each(lambda h, w, lin, g, hf: (st_s, st.at[pn.me], sem_m.at[1], sem_m.at[2]))
    for b in range(nb):
        send_rows(tgt, tr, b, sem_y.at[2])

    drain(pt, sem_t.at[1, 0])
    drain(qt, sem_t.at[1, 1])
    first = pn.group == 0

    for b in range(nb):
        drain(sr.at[b], sem_s.at[1, b])
        for mi in range(4):
            parts = []
            for ri in range(2):
                part = sr[b, pl.ds(ri * 4 + mi, sr.shape[1] // 8, stride=8), :]
                if mi == 0 and ri == 0:
                    part = part - jnp.where(first, jnp.mean(part, axis=0, keepdims=True), 0.0)
                parts.append(part)
            out = dot(pt[mi].T, jnp.concatenate(parts, axis=1))
            for ri in range(2):
                als[b, pl.ds(ri * 4 + mi, out.shape[0], stride=8), :] = out[:, ri * 128:(ri + 1) * 128]
        pn.each(lambda h, w, lin, g, hf, b=b: (als.at[b, rows_at(lin, 8 * l_own)], ar.at[b, pn.group, :, lanes_at(pn.half)],
                                               sem_a.at[0, b], sem_a.at[1, b]))

    load_k.wait()
    drain(st, sem_m.at[2])
    count = xr.shape[1] * xr.shape[2]
    mean_d = st[...]
    mu = jnp.mean(mean_d, axis=0)
    dev = mean_d - mu[None]
    dev2 = jnp.sum(dev * dev, axis=0)
    m2 = jnp.sum(mean_d, axis=0)
    row_sign = jnp.where(lax.broadcasted_iota(jnp.int32, (1, 8, 1), 1) < 4, -1.0, 1.0)
    ones = jnp.zeros((8, xr.shape[3]), F32)
    st_out[...] = ones
    for b in range(nb):
        var = (m2[2 * b + 1:2 * b + 2] + count * dev2[2 * b:2 * b + 1]) / (count * h_size * w_size)
        scale = lax.rsqrt(var + NORM_EPS)
        st_out[2 * b:2 * b + 1, :] = mu[2 * b:2 * b + 1]
        st_out[2 * b + 1:2 * b + 2, :] = scale
        drain(ar.at[b], sem_a.at[1, b])
        for l in range(l_own):
            a = ar[b, :, l * 8:(l + 1) * 8, :] * scale[None]
            ar[b, :, l * 8:(l + 1) * 8, :] = a
            a = a.reshape(-1, a.shape[2])
            own = dot(a, ker[0, l])
            other = dot(a, ker[1, l]).reshape(-1, 8, a.shape[1])
            other = jnp.concatenate([other[:, 4:], other[:, :4]], axis=1)
            out = own.reshape(-1, 8, a.shape[1]) + row_sign * other
            for hf in range(2):
                bs[b, :, hf, l * 8:(l + 1) * 8, :] = out[:, :, hf * 128:(hf + 1) * 128]
        pn.each(lambda h, w, lin, g, hf, b=b: (bs.at[b, g, hf], br.at[b, rows_at(pn.me, 8 * l_own)], sem_b.at[0, b], sem_b.at[1, b]))

    for b in range(nb):
        drain(br.at[b], sem_b.at[1, b])
        for mi in range(4):
            parts = [br[b, pl.ds(ri * 4 + mi, br.shape[1] // 8, stride=8), :] for ri in range(2)]
            out = dot(qt[mi], jnp.concatenate(parts, axis=1))
            for ri in range(2):
                ys[b, pl.ds(ri * 4 + mi, out.shape[0], stride=8), :] = out[:, ri * 128:(ri + 1) * 128]
        pn.each(lambda h, w, lin, g, hf, b=b: (ys.at[b, rows_at(lin, 8 * tq)], yr.at[b, pn.group, :, lanes_at(pn.half)],
                                               sem_y.at[0, 0, b], sem_y.at[0, 1, b]))
    for b in range(nb):
        drain(yr.at[b], sem_y.at[0, 1, b])
    for b in range(nb):
        drain(tr.at[b], sem_y.at[2, 1, b])
    outs = [(xr, x2_out), (tr, t2_out), (ar, a_out), (yr, y_out), (pt, p_out), (qt, q_out)]
    for i, (src, dst) in enumerate(outs):
        pltpu.make_async_copy(src, dst, sem_y.at[1, i // nb, i % nb]).start()
    for i, (src, dst) in enumerate(outs):
        pltpu.make_async_copy(src, dst, sem_y.at[1, i // nb, i % nb]).wait()
    others = h_size * w_size - 1
    for b in range(nb):
        drain(x.at[b, pl.ds(0, (w_size - 1) * tq)], sem_x.at[0, b])
        drain(tgt.at[b, pl.ds(0, (w_size - 1) * tq)], sem_y.at[2, 0, b])
        drain(sr.at[b, pl.ds(0, others * 8 * tq)], sem_s.at[0, b])
        drain(als.at[b, pl.ds(0, others * 8 * l_own)], sem_a.at[0, b])
        drain(br.at[b, pl.ds(0, others * 8 * l_own)], sem_b.at[0, b])
        drain(ys.at[b, pl.ds(0, others * 8 * tq)], sem_y.at[0, 0, b])
    drain(st.at[pl.ds(0, others)], sem_m.at[1])
    for k, tab in enumerate((pt, qt)):
        drain(tab.at[:, pl.ds(0, tab.shape[1] // h_size * (h_size - 1))], sem_t.at[0, k])


def solution(mesh):
    dp_size = mesh.shape["dp"]
    w_size = mesh.shape["w"]
    h_size = mesh.shape["h"]
    grid_axes = ("h", "w")
    all_axes = ("dp", "h", "w")
    xs_ = h_size // 2

    def swap(pieces, axes):
        return lax.all_to_all(pieces, axes, 0, 0, tiled=True)

    def local_step(field, target, lat_weight, leg_fwd, leg_inv, spec_w, w_in, w_out):
        nb, nc, nt, npl = field.shape
        nlon = npl * w_size
        tq = nt // w_size
        nm = leg_fwd.shape[0] * w_size
        ng = nm // 4
        half = nc // 2
        ndev = h_size * w_size
        nlat = nt * h_size
        nl = leg_fwd.shape[1]
        l_own = nl // ndev
        grid_points = nlat * nlon
        total_points = nb * dp_size * nc * grid_points
        hi, wi = lax.axis_index("h"), lax.axis_index("w")
        fwd_np, inv_np = dft_tables(nlon, nm)
        f_tab, g_tab = jnp.asarray(fwd_np), jnp.asarray(inv_np)

        x = field.transpose(0, 2, 3, 1)
        tgt = target.transpose(0, 2, 3, 1)

        def from_rows(v):
            v = v.reshape(nb, tq, w_size, npl, nc).transpose(2, 0, 1, 3, 4)
            v = swap(v, "w")
            return v.transpose(1, 0, 2, 3, 4).reshape(nb, nt, npl, nc)

        any_spec = pl.BlockSpec(memory_space=pl.ANY)
        vmem_spec = pl.BlockSpec(memory_space=pltpu.VMEM)
        sds = lambda *s: jax.ShapeDtypeStruct(s, F32)
        vm = lambda *s: pltpu.VMEM(s, F32)
        x2, t2, a, back, stv, p_t, q_t = pl.pallas_call(
            functools.partial(forward_kernel, h_size, w_size),
            name="forward",
            out_shape=[sds(nb, tq, nlon, nc), sds(nb, tq, nlon, nc), sds(nb, ng, 8 * l_own, nc), sds(nb, ng, 8 * tq, nc),
                       sds(8, nc), sds(4, nlat, nl), sds(4, nlat, nl)],
            in_specs=[any_spec] * 5 + [vmem_spec],
            out_specs=[any_spec] * 4 + [vmem_spec] + [any_spec] * 2,
            scratch_shapes=[
                vm(nb, tq, nlon, nc), vm(nb, tq, nlon, nc), vm(ng, 2, nb, 8 * tq, half), vm(nb, 8 * nlat, half),
                vm(nb, 8 * nl, half), vm(nb, ng, 8 * l_own, nc), vm(nb, ng, 2, 8 * l_own, half), vm(nb, 8 * nl, half),
                vm(nb, 8 * nlat, half), vm(nb, ng, 8 * tq, nc), vm(8, nc), vm(ndev, 8, nc), vm(4, nlat, nl), vm(4, nlat, nl),
                vm(2, l_own, nc, nc),
                pltpu.SemaphoreType.DMA((2, nb)), pltpu.SemaphoreType.DMA((2, nb)), pltpu.SemaphoreType.DMA((2, nb)),
                pltpu.SemaphoreType.DMA((2, nb)), pltpu.SemaphoreType.DMA((3, 2, nb)), pltpu.SemaphoreType.DMA((3,)),
                pltpu.SemaphoreType.DMA((2, 2)),
            ],
            compiler_params=pltpu.CompilerParams(collective_id=0, has_side_effects=True, vmem_limit_bytes=60 * 1024 * 1024),
        )(x, tgt, leg_fwd.transpose(0, 2, 1), leg_inv.transpose(0, 2, 1), spec_w, f_tab)
        mu, inv_std = stv[0:2 * nb:2], stv[1:2 * nb:2]
        a = a.reshape(nb, ng, l_own, 2, 4, nc).transpose(2, 0, 1, 3, 4, 5)
        back = back.reshape(nb, ng, tq, 8, nc).transpose(0, 2, 1, 3, 4).reshape(nb, tq, ng * 8, nc)
        lane0 = (hi % 2) * half

        def spread(v):
            v = v.reshape(nb, tq, w_size, xs_, 8, 2, half).transpose(3, 5, 2, 0, 1, 4, 6)
            v = v.reshape(ndev, nb, tq, 8, half)
            v = swap(v, grid_axes)
            return v.transpose(1, 0, 2, 3, 4).reshape(nb, nlat, 8, half)

        def gather(v):
            v = v.reshape(nb, ndev, tq, 8, half).transpose(1, 0, 2, 3, 4)
            v = swap(v, grid_axes)
            v = v.reshape(xs_, 2, w_size, nb, tq, 8, half).transpose(3, 4, 2, 0, 5, 1, 6)
            return v.reshape(nb, tq, ng * 8, nc)

        def to_owner(v):
            v = v.reshape(ndev, l_own, nb, 8, half)
            v = swap(v, grid_axes)
            v = v.reshape(xs_, 2, w_size, l_own, nb, 8, half).transpose(3, 4, 2, 0, 5, 1, 6)
            return v.reshape(l_own, nb, ng, 2, 4, nc)

        def from_owner(v):
            v = v.reshape(l_own, nb, w_size, xs_, 8, 2, half).transpose(3, 5, 2, 0, 1, 4, 6)
            v = v.reshape(ndev, l_own, nb, 8, half)
            v = swap(v, grid_axes)
            return v.reshape(nl, nb, 2, 4, half)

        def leg_down(tab_t, v):
            v = v.reshape(nb, nlat, 2, 4, half)
            return mm("mtl,btrmc->lbrmc", tab_t, v)

        def leg_up(tab_t, v):
            return mm("mtl,lbrmc->btrmc", tab_t, v).reshape(nb, nlat, 8, half)

        has0 = jnp.where((hi // 2 == 0) & (wi == 0), jnp.float32(nlon ** 0.5), 0.0)
        me = hi * w_size + wi
        ker = lax.dynamic_slice_in_dim(spec_w, me * l_own, l_own, 1)
        kr, ki = ker[0], ker[1]
        sgn = jnp.asarray(np.array([-1.0, 1.0], np.float32))[:, None, None]
        y = mm("rp,btrc->btpc", g_tab, back)
        y_bf = y.astype(jnp.bfloat16)
        hid = jnp.einsum("btpc,cf->btpf", y_bf, w_in, preferred_element_type=F32)
        act, gelu_pull = jax.vjp(jax.nn.gelu, hid)
        act_bf = act.astype(jnp.bfloat16)
        out = jnp.einsum("btpf,fc->btpc", act_bf, w_out, preferred_element_type=F32)
        resid = x2 + y + out - t2
        q4 = lax.dynamic_slice_in_dim(lat_weight, wi * tq, tq, 0)
        d_out = q4[None, :, None, None] * resid
        loss = lax.psum(jnp.sum(d_out * resid), all_axes) / total_points
        d_out_bf = d_out.astype(jnp.bfloat16)
        g_out = lax.psum(jnp.einsum("btpf,btpc->fc", act_bf, d_out_bf, preferred_element_type=F32), all_axes)
        d_act = jnp.einsum("btpc,fc->btpf", d_out_bf, w_out, preferred_element_type=F32)
        d_hid = gelu_pull(d_act)[0].astype(jnp.bfloat16)
        g_in = lax.psum(jnp.einsum("btpc,btpf->cf", y_bf, d_hid, preferred_element_type=F32), all_axes)
        d_y = d_out + jnp.einsum("btpf,cf->btpc", d_hid, w_in, preferred_element_type=F32)
        d_back = spread(mm("rp,btpc->btrc", g_tab, d_y))
        d_mixed = to_owner(leg_down(q_t, d_back))
        d1 = mm("lbgrmo,lio->lbgrmi", d_mixed, kr)
        d2 = mm("lbgrmo,lio->lbgrmi", d_mixed, ki)
        d_a = d1 - sgn * d2[:, :, :, ::-1]
        rot = -sgn * d_mixed[:, :, :, ::-1]
        gr = mm("lbgrmi,lbgrmo->lio", a, d_mixed)
        gi = mm("lbgrmi,lbgrmo->lio", a, rot)
        grad_spec = lax.psum(jnp.stack([gr, gi]), "dp")
        grad_spec = lax.all_gather(grad_spec, "w", axis=1, tiled=True)
        d_sp = leg_up(p_t, from_owner(d_a))
        s1_h = has0 * jnp.sum(d_sp[:, :, 0], axis=1)
        s1 = lax.dynamic_update_slice_in_dim(jnp.zeros((nb, nc), F32), s1_h, lane0, 1)
        s2 = jnp.sum(d_a * a, axis=(0, 2, 3, 4))
        bstat = lax.psum(jnp.stack([s1, s2]), grid_axes) / grid_points
        d_n = mm("rp,btrc->btpc", f_tab, gather(d_sp))
        row = lambda v: v[:, None, None, :]
        normed = (x2 - row(mu)) * row(inv_std)
        d_x = d_out + row(inv_std) * (d_n - row(bstat[0]) - normed * row(bstat[1]))
        d_field = from_rows(d_x).transpose(0, 3, 1, 2)
        return loss, d_field, grad_spec, g_in, g_out

    grid_spec = P("dp", None, "h", "w")
    table_spec = P("w", None, "h")
    kernel_spec = P(None, "h", None, None)
    return jax.shard_map(local_step, mesh=mesh, in_specs=(grid_spec, grid_spec, P("h"), table_spec, table_spec, P(), P(), P()), out_specs=(P(), grid_spec, kernel_spec, P(), P()), check_vma=False)
```

time: 737 us -> 620 us (0.84)
  Pallas kernels: 0 us -> 139 us
  waiting for transfers between devices: 212 us -> 127 us
  blocking collectives: 287 us -> 214 us
  starting transfers between devices: 59.1 us -> 16.3 us
  local copies, waits for them, and re-layouts: 86 us -> 44.5 us
  matrix products: 58.2 us -> 50.4 us
    pallas_call x0 -> x1, Pallas kernels: none -> 139 us  [local_step(): pl.pallas_call(functools.partial(forward_kernel, h_size, w_size), name='f...]
    all_to_all x10 -> x3, waiting for transfers between devices: 95.9 us -> 10.9 us  [swap(): return lax.all_to_all(pieces, axes, 0, 0, tiled=True)]
    all_gather x1 -> x0, blocking collectives: 54.7 us -> none  [local_step(): stats = lax.all_gather(jnp.stack([loc_mean, loc_m2]), grid_axes)]
    all_to_all x10 -> x3, starting transfers between devices: 59 us -> 16 us  [swap(): return lax.all_to_all(pieces, axes, 0, 0, tiled=True)]
    transpose x16 -> x7, local copies, waits for them, and re-layouts: 32.9 us -> 12.9 us  [the longest x4 6.97 us: mm(): return jnp.einsum(form, a, b, precision=PRECISE, preferred_element_type=F32)]
    all_to_all x3 -> x2, blocking collectives: 71.3 us -> 52.2 us  [swap(): return lax.all_to_all(pieces, axes, 0, 0, tiled=True)]
    dot_general x20 -> x15, matrix products: 58.2 us -> 50.4 us  [the longest x9 30.5 us: mm(): return jnp.einsum(form, a, b, precision=PRECISE, preferred_element_type=F32)]
    unnamed x69 -> x45, local copies, waits for them, and re-layouts: 18.5 us -> 12.6 us
  transfers between devices with their start and end apart: 13 -> 6, of which waited for: 7 -> 3; matrix products, arithmetic and copies ran while one was open for 13% -> 7% of each run, Pallas kernels for 0% -> 0%
where the time goes in v2:
time: 620 us; the launch traced here: 611 us
  blocking collectives  214 us (35%)
  Pallas kernels  139 us (22%)
  waiting for transfers between devices  127 us (20%)
  matrix products  50.4 us (8%)
  local copies, waits for them, and re-layouts  44.5 us (7%)
  between operations  18.1 us (3%)
  starting transfers between devices  16.3 us (3%)
    pallas_call x1, Pallas kernels, local_step(): pl.pallas_call(functools.partial(forward_kernel, h_size, w_size), name='f...  139 us
    psum x1, blocking collectives, local_step(): loss = lax.psum(jnp.sum(d_out * resid), all_axes) / total_points  84.2 us
    psum x1, blocking collectives, local_step(): bstat = lax.psum(jnp.stack([s1, s2]), grid_axes) / grid_points  77.2 us
    psum x1, waiting for transfers between devices, local_step(): lax.psum(jnp.einsum('btpc,btpf->cf', y_bf, d_hid, preferred_element_type=...  72 us
    all_to_all x2, blocking collectives, swap(): return lax.all_to_all(pieces, axes, 0, 0, tiled=True)  52.2 us
    psum x1, waiting for transfers between devices, local_step(): grad_spec = lax.psum(jnp.stack([gr, gi]), 'dp')  44 us
    dot_general x9, matrix products, mm(): return jnp.einsum(form, a, b, precision=PRECISE, preferred_element_type=F32)  30.5 us
    all_to_all x3, starting transfers between devices, swap(): return lax.all_to_all(pieces, axes, 0, 0, tiled=True)  16 us
  transfers between devices with their start and end apart: 6, of which 3 were waited for; matrix products, arithmetic and copies ran while one was open for 7% of the time, Pallas kernels for 0%

profile of v2, /device:TPU:1, one launch (start us, length us, event | category | flops | bytes accessed | tf_op | source)
XLA Modules:
  0.0 611.3 jit_solution(1640953620354146290)
XLA Ops:
  8.8 139.1 %forward.1 = (f32[3,4,256,256]{3,2,1,0:T(8,128)}, f32[3,4,256,256]{3,2,1,0:T(8,128)}, f32[3,16,16,256]{3,2,1,0:T(8,128)}, f32[3,16,32,256]{3,2,1,0:T(8,128)}, f3...) custom-call(f32[3,16,64,256]{3,2,1,0:T(8,128)} %bitcast.195, f32[3,16,64,256]{3,2,1,0:T(8,128)} %bitcast.196, ...), custom_call_target="tpu_custom_call" | custom-call | tf_op jit(solution)/shard_map/forward/pallas_call | solution.py:268
  147.9 4.1 fusion.12
  153.9 3.0 copy-done.20
  157.0 3.6 fusion.7
  160.6 5.1 fusion.6
  167.3 6.3 %fusion.18 = f32[3,4,128,256]{2,3,1,0:T(8,128)} fusion(f32[128,256,1,1]{0,1,3,2:T(8,128)S(1)} %copy-done.11, f32[3,4,256,256]{3,2,1,0:T(8,128)S(1)} %fusion.34, f32[3,4,256,256]{3,2,1,0:T(8,128)S(1)} %get-tuple-element.24, f32[4]{0:T(128)S(1)} %dynamic_slice.6), kind=kOutput, calls=%fused_computation.30 | convolution fusion | flops 1209532416 | bytes 7995408 | tf_op jit(solution)/shard_map/rp,btpc->btrc/dot_general | solution.py:17
  173.7 3.0 copy.82
  178.3 28.2 %all_to_all.25 = f32[32,3,4,8,128]{4,3,2,1,0:T(8,128)S(1)} all-to-all(f32[32,3,4,8,128]{4,3,2,1,0:T(8,128)S(1)} %bitcast.191), channel_id=1, replica_groups=mesh['dp'=4,'w'=4,'h'=8] {'h','w'}, dimensions={0} | all-to-all | bytes 3145728 | tf_op jit(solution)/shard_map/all_to_all | solution.py:237
  209.3 5.4 all-to-all-start.1
  214.9 2.2 reshape.91
  217.2 10.9 %all-to-all-done.1 = f32[32,2,3,8,128]{4,3,2,1,0:T(8,128)} async-done(((f32[32,2,3,8,128]{4,3,2,1,0:T(8,128)}), f32[32,2,3,8,128]{4,3,2,1,0:T(8,128)}, u32[]{:S(2)}, u32[]{:S(2)}) %all-to-all-start.1) | async-done | bytes 786464 | tf_op jit(solution)/shard_map/all_to_all | solution.py:237
  228.1 2.6 copy.88
  230.7 2.7 reshape.84
  234.7 3.3 convolution_bitcast_fusion.4
  238.0 1.8 convolution_bitcast_fusion.3
  240.9 44.0 %all-reduce.4.cloned.1.call-done = f32[2,2,256,256]{3,2,1,0:T(8,128)} async-done(((f32[2,2,256,256]{3,2,1,0:T(8,128)}), f32[2,2,256,256]{3,2,1,0:T(8,128)}) %all-reduce.4.cloned.1.call-update) | async-done | bytes 1048592 | tf_op jit(solution)/shard_map/psum | solution.py:351
  284.9 3.0 fusion.31
  288.0 2.1 rev.6
  290.1 3.9 fusion.27
  294.0 2.4 reshape.85
  298.0 24.0 %all_to_all.26 = f32[32,2,3,8,128]{4,3,2,1,0:T(8,128)S(1)} all-to-all(f32[32,2,3,8,128]{4,3,2,1,0:T(8,128)S(1)} %bitcast.199), channel_id=1, replica_groups=mesh['dp'=4,'w'=4,'h'=8] {'h','w'}, dimensions={0} | all-to-all | bytes 1572864 | tf_op jit(solution)/shard_map/all_to_all | solution.py:237
  326.8 6.0 all-to-all-start.3
  334.5 77.2 %psum.36 = f32[2,3,256]{2,1,0:T(4,128)S(1)} all-reduce(f32[2,3,256]{2,1,0:T(4,128)S(1)} %pad_maximum_fusion.1), channel_id=1, replica_groups=mesh['dp'=4,'w'=4,'h'=8] {'h','w'}, use_global_device_ids=true, to_apply=%region_4.5 | all-reduce | flops 1536 | bytes 12288 | tf_op jit(solution)/shard_map/psum | solution.py:357
  414.1 5.4 multiply_add_fusion
  419.5 1.9 copy.160
  421.4 4.6 all-to-all-start.4
  426.1 3.8 convolution_bitcast_fusion.2
  429.9 5.3 convolution_bitcast_fusion.1
  435.2 84.2 %psum.35 = f32[]{:T(128)} all-reduce(f32[]{:T(128)} %get-tuple-element.23), channel_id=1, replica_groups=mesh['dp'=4,'w'=4,'h'=8] {'dp','h','w'}, use_global_device_ids=true, to_apply=%region_1.2 | all-reduce | flops 1 | bytes 8 | tf_op jit(solution)/shard_map/psum | solution.py:336
  520.1 3.9 copy.98
  524.0 72.0 %all-reduce.6.cloned.1.call-done = (f32[256,512]{1,0:T(8,128)}, f32[512,256]{1,0:T(8,128)}) async-done(((f32[256,512]{1,0:T(8,128)}, f32[512,256]{1,0:T(8,128)}), (f32[256,512]{1,0:T(8,128)}, f32[512,256]{1,0:T(8,128)})) %all-reduce.6.cloned.1.call-update) | async-done | bytes 1048592 | tf_op jit(solution)/shard_map/psum | solution.py:341
  596.0 4.7 copy.166
  (75 shorter events, 23.4 us)
Async XLA Ops:
  8.0 145.1 %copy-start = (bf16[512,256]{1,0:T(8,128)(2,1)S(1)}, bf16[512,256]{1,0:T(8,128)(2,1)}, u32[]{:S(2)}) copy-start(bf16[512,256]{1,0:T(8,128)(2,1)} %param.18) | copy-start | bytes 786436
  8.8 139.1 %copy-start.11 = (f32[128,256,1,1]{0,1,3,2:T(8,128)S(1)}, f32[128,256,1,1]{0,1,3,2:T(8,128)}, u32[]{:S(2)}) copy-start(f32[128,256,1,1]{0,1,3,2:T(8,128)} %constant.79) | copy-start | bytes 393220
  147.9 4.1 copy-start.10
  152.1 1.9 copy-start.9
  152.1 4.9 copy-start.20
  153.1 7.6 %copy-start.7 = (f32[3,4,256,512]{3,2,1,0:T(8,128)}, f32[3,4,256,512]{3,2,1,0:T(8,128)S(1)}, u32[]{:S(2)}) copy-start(f32[3,4,256,512]{3,2,1,0:T(8,128)S(1)} %fusion.22) | copy-start | bytes 18874372
  160.6 6.1 %copy-start.4 = (f32[3,4,256,256]{3,2,1,0:T(8,128)}, f32[3,4,256,256]{3,2,1,0:T(8,128)S(1)}, u32[]{:S(2)}) copy-start(f32[3,4,256,256]{3,2,1,0:T(8,128)S(1)} %get-tuple-element.24) | copy-start | bytes 9437188
  165.7 1.6 copy-start.3
  178.3 28.4 %copy-start.15 = (f32[4,128,64]{2,1,0:T(8,128)S(1)}, f32[4,128,64]{2,1,0:T(8,128)}, u32[]{:S(2)}) copy-start(f32[4,128,64]{2,1,0:T(8,128)} %get-tuple-element.16) | copy-start | bytes 393220
  209.3 24.1 %copy-start.19 = (f32[2]{0:T(128)S(1)}, f32[2]{0:T(128)}, u32[]{:S(2)}) copy-start(f32[2]{0:T(128)} %constant.78) | copy-start | bytes 28
  209.3 18.8 %all-to-all-start.1 = ((f32[32,2,3,8,128]{4,3,2,1,0:T(8,128)}), f32[32,2,3,8,128]{4,3,2,1,0:T(8,128)}, u32[]{:S(2)}, u32[]{:S(2)}) async-start(f32[32,2,3,8,128]{4,3,2,1,0:T(8,128)} %bitcast.198), calls=%async_computation.1 | async-start | bytes 1572864 | tf_op jit(solution)/shard_map/all_to_all | solution.py:237
  214.7 70.2 %all-reduce.4.cloned.1.call-start = ((), (), s32[]{:S(2)}) async-start(), calls=%async_computation.5 | async-start | bytes 2097152 | tf_op jit(solution)/shard_map/psum | solution.py:351
  234.7 3.3 copy-start.8
  240.9 49.2 %copy-start.18 = (f32[2]{0:T(128)S(1)}, f32[2]{0:T(128)}, u32[]{:S(2)}) copy-start(f32[2]{0:T(128)} %constant.75.clone) | copy-start | bytes 28
  240.9 283.1 %all-gather.2.cloned.1.call-start = ((), (), s32[]{:S(2)}) async-start(), calls=%async_computation.6 | async-start | bytes 5242880 | tf_op jit(solution)/shard_map/all_gather | solution.py:352
  294.0 28.0 %copy-start.14 = (f32[4,128,64]{2,1,0:T(8,128)S(1)}, f32[4,128,64]{2,1,0:T(8,128)}, u32[]{:S(2)}) copy-start(f32[4,128,64]{2,1,0:T(8,128)} %get-tuple-element.17) | copy-start | bytes 393220
  323.4 1.1 copy-start.2
  325.6 7.3 %copy-start.17 = (f32[8,256]{1,0:T(8,128)S(1)}, f32[8,256]{1,0:T(8,128)}, u32[]{:S(2)}) copy-start(f32[8,256]{1,0:T(8,128)} %get-tuple-element.15) | copy-start | bytes 24580
  326.8 84.9 %all-to-all-start.3 = ((f32[32,3,4,8,128]{4,3,2,1,0:T(8,128)}), f32[32,3,4,8,128]{4,3,2,1,0:T(8,128)}, u32[]{:S(2)}, u32[]{:S(2)}) async-start(f32[32,3,4,8,128]{4,3,2,1,0:T(8,128)} %copy.93), calls=%async_computation.3 | async-start | bytes 3145728 | tf_op jit(solution)/shard_map/all_to_all | solution.py:237
  332.9 80.6 %copy-start.16 = (f32[128,256,1,1]{1,0,3,2:T(8,128)S(1)}, f32[128,256,1,1]{1,0,3,2:T(8,128)}, u32[]{:S(2)}) copy-start(f32[128,256,1,1]{1,0,3,2:T(8,128)} %constant.80) | copy-start | bytes 393220
  411.8 2.4 copy-start.5
  421.4 98.7 %all-to-all-start.4 = ((f32[4,3,4,64,256]{4,3,2,1,0:T(8,128)}), f32[4,3,4,64,256]{4,3,2,1,0:T(8,128)}, u32[]{:S(2)}, u32[]{:S(2)}) async-start(f32[4,3,4,64,256]{4,3,2,1,0:T(8,128)} %bitcast.187), calls=%async_computation.4 | async-start | bytes 6291456 | tf_op jit(solution)/shard_map/all_to_all | solution.py:237
  426.0 170.0 %all-reduce.6.cloned.1.call-start = ((), (), s32[]{:S(2)}) async-start(), calls=%async_computation.7 | async-start | bytes 2097152 | tf_op jit(solution)/shard_map/psum | solution.py:341
  426.1 3.9 copy-start.6
  596.0 4.7 copy-start.13
  596.0 5.5 copy-start.12
  596.0 6.3 %copy-start.1 = (bf16[512,256]{1,0:T(8,128)(2,1)S(1)}, bf16[512,256]{1,0:T(8,128)(2,1)}, u32[]{:S(2)}) copy-start(bf16[512,256]{1,0:T(8,128)(2,1)} %param.18) | copy-start | bytes 786436
Sparse Core Ops, SparseCore 0:
  241.0 43.8 all-reduce.3
  286.6 73.7 all-gather.1
Sparse Core Ops, SparseCore 1:
  435.3 160.6 all-reduce.5

commit v3 on v0

v3 whole, which is shorter than its diff:
```python
import functools
import jax
import jax.numpy as jnp
import numpy as np
from jax import lax
from jax.experimental import pallas as pl
from jax.experimental.pallas import tpu as pltpu
from jax.sharding import PartitionSpec as P

NORM_EPS = 1e-5
PRECISE = lax.Precision.HIGHEST
MESH = pl.DeviceIdType.MESH
F32 = jnp.float32
BF16 = jnp.bfloat16
GELU_C = float(np.sqrt(2.0 / np.pi))
GELU_A = 0.044715
NN = (((1,), (0,)), ((), ()))
NT = (((1,), (1,)), ((), ()))
TN = (((0,), (0,)), ((), ()))


def dot(a, b, dims=NN):
    return lax.dot_general(a, b, dims, precision=PRECISE, preferred_element_type=F32)


def bdot(a, b, dims=NN):
    return lax.dot_general(a, b, dims, preferred_element_type=F32)


def dft_tables(lon_count, num_modes):
    modes, lons = np.arange(num_modes), np.arange(lon_count)
    angle = 2.0 * np.pi * ((modes[:, None] * lons[None, :]) % lon_count) / lon_count
    fwd = np.stack([np.cos(angle), -np.sin(angle)], 0) * lon_count ** -0.5
    inv = fwd * np.where(modes == 0, 1.0, 2.0)[None, :, None]

    def rows(table):
        table = table.reshape(2, num_modes // 4, 4, lon_count).transpose(1, 0, 2, 3)
        return table.reshape(2 * num_modes, lon_count).astype(np.float32)

    return rows(fwd), rows(inv)


def drain(ref, sem):
    pltpu.make_async_copy(ref, ref, sem).wait()


def rows_at(i, n):
    return pl.ds(pl.multiple_of(i * n, n), n)


def lanes_at(half):
    return pl.ds(pl.multiple_of(half * 128, 128), 128)


def push(src, dst, sems, device):
    pltpu.make_async_remote_copy(src_ref=src, dst_ref=dst, send_sem=sems.at[0], recv_sem=sems.at[1],
                                 device_id=device, device_id_type=MESH).start()


def keep(src, dst, sems):
    pltpu.make_async_copy(src, dst, sems.at[1]).start()


def swap_parts(v):
    return jnp.concatenate([v[:, 4:], v[:, :4]], axis=1)


def block_kernel(sizes, total_points,
                 x, tgt, leg_p, leg_q, spec_w, lat, w1, w2, f_tab, g_tab, ft_tab, gt_tab,
                 dx_out, gs_out, gin_out, gout_out, loss_out,
                 xr, tr, xs, sr, als, ar, bs, br, ys, yr, dout, dsr, dar, dbr, dyr,
                 st_s, st, st2_s, st2, pt, qt, ptt, qtt, ker,
                 gw, gw_z, gw_zs, gw_h, gw_hs, gw_w, gw_ws, gw_w2, gw_h2, gw_f,
                 ls, ls_z, ls_zs, ls_h, ls_hs, ls_w, gsp, gs_z, gs_sum, gs_w,
                 sem_x, sem_t, sem_s, sem_a, sem_b, sem_y, sem_ds, sem_da, sem_db, sem_dy, sem_o,
                 sem_st, sem_tab, sem_k, sem_gw, sem_ls, sem_gs, sem_fin):
    dp_size, h_size, w_size = sizes
    dp, h, w = lax.axis_index("dp"), lax.axis_index("h"), lax.axis_index("w")
    ndev = h_size * w_size
    me = h * w_size + w
    group_of = lambda h, w: (h // 2) * w_size + w
    group, half = group_of(h, w), h % 2
    nb, nt, npl, nc = x.shape
    tq = nt // w_size
    nlon = npl * w_size
    nlat = nt * h_size
    l_own = als.shape[1] // 8 // ndev
    first = group == 0

    load_k = pltpu.make_async_copy(spec_w.at[:, pl.ds(me * l_own, l_own)], ker, sem_k.at[0])
    load_k.start()

    def peer(k):
        return (h + k // w_size) % h_size, (w + k % w_size) % w_size

    barrier = pltpu.get_barrier_semaphore()

    def meet(k, _):
        h2, w2_ = peer(k)
        pl.semaphore_signal(barrier, inc=1, device_id={"h": h2, "w": w2_}, device_id_type=MESH)
        return 0

    def meet_dp(k, _):
        pl.semaphore_signal(barrier, inc=1, device_id={"dp": (dp + k) % dp_size}, device_id_type=MESH)
        return 0

    lax.fori_loop(1, ndev, meet, 0)
    lax.fori_loop(1, dp_size, meet_dp, 0)
    pl.semaphore_wait(barrier, ndev - 1 + dp_size - 1)

    def plane(refs, sems):
        src, dst = refs(me, group, half)
        keep(src, dst, sems)

        def body(k, _):
            h2, w2_ = peer(k)
            src, dst = refs(h2 * w_size + w2_, group_of(h2, w2_), h2 % 2)
            push(src, dst, sems, {"h": h2, "w": w2_})
            return 0

        lax.fori_loop(1, ndev, body, 0)

    def along(axis, size, index, refs, sems):
        src, dst = refs(index)
        keep(src, dst, sems)

        def body(k, _):
            other = (index + k) % size
            src, dst = refs(other)
            push(src, dst, sems, {axis: other})
            return 0

        lax.fori_loop(1, size, body, 0)

    def send_rows(src, dst, b, sem):
        along("w", w_size, w, lambda o: (src.at[b, rows_at(o, tq)], dst.at[b, :, rows_at(w, npl)]), sem.at[b])

    def send_table(src, dst, sems):
        for c in range(2):
            for w2_ in range(w_size):
                h2 = 2 * w + c
                a, z = src.at[w2_ * 4:(w2_ + 1) * 4], dst.at[:, rows_at(h, nt)]
                mine = jnp.logical_and(h2 == h, w == w2_)

                @pl.when(mine)
                def _():
                    keep(a, z, sems)

                @pl.when(jnp.logical_not(mine))
                def _():
                    push(a, z, sems, {"h": h2, "w": w2_})

    def send_spread(b, dst, sem):
        plane(lambda lin, g, hf: (xs.at[g, hf, b], dst.at[b, rows_at(me, 8 * tq)]), sem.at[b])

    def send_owner(b, dst, sem):
        plane(lambda lin, g, hf: (als.at[b, rows_at(lin, 8 * l_own)], dst.at[b, group, :, lanes_at(half)]), sem.at[b])

    def send_back(b, dst, sem):
        plane(lambda lin, g, hf: (bs.at[b, g, hf], dst.at[b, rows_at(me, 8 * l_own)]), sem.at[b])

    def send_gather(b, dst, sem):
        plane(lambda lin, g, hf: (ys.at[b, rows_at(lin, 8 * tq)], dst.at[b, group, :, lanes_at(half)]), sem.at[b])

    def put_spec(b, t, out):
        out = out.reshape(-1, 8, nc)
        for hf in range(2):
            xs[:, hf, b, rows_at(t, 8), :] = out[:, :, hf * 128:(hf + 1) * 128]

    def leg_down(b, tab, src, fix):
        for mi in range(4):
            parts = []
            for ri in range(2):
                part = src[b, pl.ds(ri * 4 + mi, nlat, stride=8), :]
                if fix and mi == 0 and ri == 0:
                    part = part - jnp.where(first, jnp.mean(part, axis=0, keepdims=True), 0.0)
                parts.append(part)
            out = dot(tab[mi], jnp.concatenate(parts, axis=1))
            for ri in range(2):
                als[b, pl.ds(ri * 4 + mi, out.shape[0], stride=8), :] = out[:, ri * 128:(ri + 1) * 128]

    def leg_up(b, tab, src, fix):
        for mi in range(4):
            parts = [src[b, pl.ds(ri * 4 + mi, src.shape[1] // 8, stride=8), :] for ri in range(2)]
            out = dot(tab[mi], jnp.concatenate(parts, axis=1))
            for ri in range(2):
                part = out[:, ri * 128:(ri + 1) * 128]
                if fix and mi == 0 and ri == 0:
                    part = part - jnp.where(first, jnp.mean(part, axis=0, keepdims=True), 0.0)
                ys[b, pl.ds(ri * 4 + mi, nlat, stride=8), :] = part

    def put_back(b, l, out):
        for hf in range(2):
            bs[b, :, hf, l * 8:(l + 1) * 8, :] = out[:, :, hf * 128:(hf + 1) * 128]

    for b in range(nb):
        send_rows(x, xr, b, sem_x)
    send_table(leg_p, pt, sem_tab.at[0])
    send_table(leg_q, qt, sem_tab.at[1])
    st_s[...] = jnp.zeros_like(st_s)
    st2_s[...] = jnp.zeros_like(st2_s)
    gw[...] = jnp.zeros_like(gw)
    ls[...] = jnp.zeros_like(ls)

    for b in range(nb):
        drain(xr.at[b], sem_x.at[b, 1])

        def spec(t, total, b=b):
            rows = xr[b, t]
            put_spec(b, t, dot(f_tab[...], rows))
            return total + jnp.sum(rows, axis=0, keepdims=True)

        total = lax.fori_loop(0, tq, spec, jnp.zeros((1, nc), F32))
        send_spread(b, sr, sem_s)
        mean = total / (tq * nlon)

        def spread2(t, total, b=b, mean=mean):
            d = xr[b, t] - mean
            return total + jnp.sum(d * d, axis=0, keepdims=True)

        st_s[2 * b:2 * b + 1, :] = mean
        st_s[2 * b + 1:2 * b + 2, :] = lax.fori_loop(0, tq, spread2, jnp.zeros((1, nc), F32))
    plane(lambda lin, g, hf: (st_s, st.at[me]), sem_st.at[0])

    for tab, tabt, k in ((pt, ptt, 0), (qt, qtt, 1)):
        drain(tab, sem_tab.at[k, 1])
        for mi in range(4):
            tabt[mi] = tab[mi].T

    for b in range(nb):
        drain(sr.at[b], sem_s.at[b, 1])
        leg_down(b, ptt, sr, True)
        send_owner(b, ar, sem_a)
    send_rows(tgt, tr, 0, sem_t)

    load_k.wait()
    drain(st, sem_st.at[0, 1])
    stats = st[...]
    mu = jnp.mean(stats, axis=0)
    dev = stats - mu[None]
    dev2 = jnp.sum(dev * dev, axis=0)
    m2 = jnp.sum(stats, axis=0)
    count = tq * nlon
    row_sign = jnp.where(lax.broadcasted_iota(jnp.int32, (1, 8, 1), 1) < 4, -1.0, 1.0)
    scales, means = [], []
    for b in range(nb):
        var = (m2[2 * b + 1:2 * b + 2] + count * dev2[2 * b:2 * b + 1]) / (count * ndev)
        scales.append(lax.rsqrt(var + NORM_EPS))
        means.append(mu[2 * b:2 * b + 1])
    for b in range(nb):
        drain(ar.at[b], sem_a.at[b, 1])
        for l in range(l_own):
            a = ar[b, :, l * 8:(l + 1) * 8, :] * scales[b][None]
            ar[b, :, l * 8:(l + 1) * 8, :] = a
            a = a.reshape(-1, nc)
            own = dot(a, ker[0, l]).reshape(-1, 8, nc)
            other = dot(a, ker[1, l]).reshape(-1, 8, nc)
            put_back(b, l, own + row_sign * swap_parts(other))
        send_back(b, br, sem_b)
    send_rows(tgt, tr, 1, sem_t)

    for b in range(nb):
        drain(br.at[b], sem_b.at[b, 1])
        leg_up(b, qt, br, False)
        send_gather(b, yr, sem_y)
    for b in range(2, nb):
        send_rows(tgt, tr, b, sem_t)

    for b in range(nb):
        drain(yr.at[b], sem_y.at[b, 1])
        drain(tr.at[b], sem_t.at[b, 1])
        drain(sr.at[b, pl.ds(0, (ndev - 1) * 8 * tq)], sem_s.at[b, 0])

        def point(t, _, b=b):
            y = dot(gt_tab[...], yr[b, :, rows_at(t, 8), :].reshape(-1, nc))
            yb = y.astype(BF16)
            hid = bdot(yb, w1[...])
            th = jnp.tanh(GELU_C * (hid + GELU_A * (hid * hid * hid)))
            act = (hid * (0.5 * (1.0 + th))).astype(BF16)
            resid = xr[b, t] + y + bdot(act, w2[...]) - tr[b, t]
            d = lat[w * tq + t] * resid
            ls[...] += jnp.sum((d * resid).reshape(-1, 8, nc), axis=0)
            dout[b, t] = d
            db = d.astype(BF16)
            gw[2 * nc:, :] += bdot(act, db, TN)
            slope = 0.5 * (1.0 + th) + (0.5 * GELU_C) * hid * (1.0 - th * th) * (1.0 + (3.0 * GELU_A) * (hid * hid))
            dh = (bdot(db, w2[...], NT) * slope).astype(BF16)
            gin = bdot(yb, dh, TN)
            gw[:nc, :] += gin[:, :nc]
            gw[nc:2 * nc, :] += gin[:, nc:]
            dy = d + bdot(dh, w1[...], NT)
            put_spec(b, t, dot(g_tab[...], dy))
            return 0

        lax.fori_loop(0, tq, point, 0)
        send_spread(b, dsr, sem_ds)

    n_z, n_h, n_w = gw_zs.shape[0], gw_hs.shape[0], gw_ws.shape[0]
    along("dp", dp_size, dp, lambda o: (gw.at[rows_at(o, n_z)], gw_z.at[dp]), sem_gw.at[0])
    along("dp", dp_size, dp, lambda o: (ls, ls_z.at[dp]), sem_ls.at[0])

    for b in range(nb):
        drain(dsr.at[b], sem_ds.at[b, 1])
        drain(als.at[b, pl.ds(0, (ndev - 1) * 8 * l_own)], sem_a.at[b, 0])
        leg_down(b, qtt, dsr, False)
        send_owner(b, dar, sem_da)

    drain(gw_z, sem_gw.at[0, 1])
    drain(ls_z, sem_ls.at[0, 1])
    gw_zs[...] = jnp.sum(gw_z[...], axis=0)
    ls_zs[...] = jnp.sum(ls_z[...], axis=0)
    along("h", h_size, h, lambda o: (gw_zs.at[rows_at(o, n_h)], gw_h.at[h]), sem_gw.at[1])
    along("h", h_size, h, lambda o: (ls_zs, ls_h.at[h]), sem_ls.at[1])

    for b in range(nb):
        drain(dar.at[b], sem_da.at[b, 1])
        drain(br.at[b, pl.ds(0, (ndev - 1) * 8 * l_own)], sem_b.at[b, 0])
        s2 = jnp.zeros((1, nc), F32)
        for l in range(l_own):
            d = dar[b, :, l * 8:(l + 1) * 8, :].reshape(-1, nc)
            own = dot(d, ker[0, l], NT).reshape(-1, 8, nc)
            other = dot(d, ker[1, l], NT).reshape(-1, 8, nc)
            da = own - row_sign * swap_parts(other)
            put_back(b, l, da)
            s2 = s2 + jnp.sum((da * ar[b, :, l * 8:(l + 1) * 8, :]).reshape(-1, nc), axis=0, keepdims=True)
        send_back(b, dbr, sem_db)
        st2_s[b:b + 1, :] = s2
    plane(lambda lin, g, hf: (st2_s, st2.at[me]), sem_st.at[1])

    for l in range(l_own):
        a = ar[:, :, l * 8:(l + 1) * 8, :].reshape(-1, nc)
        d3 = dar[:, :, l * 8:(l + 1) * 8, :].reshape(-1, 8, nc)
        gsp[2 * l] = dot(a, d3.reshape(-1, nc), TN)
        gsp[2 * l + 1] = dot(a, (-row_sign * swap_parts(d3)).reshape(-1, nc), TN)
    along("dp", dp_size, dp, lambda o: (gsp.at[o], gs_z.at[dp]), sem_gs.at[0])

    drain(gw_h, sem_gw.at[1, 1])
    drain(ls_h, sem_ls.at[1, 1])
    gw_hs[...] = jnp.sum(gw_h[...], axis=0)
    ls_hs[...] = jnp.sum(ls_h[...], axis=0)
    along("w", w_size, w, lambda o: (gw_hs.at[rows_at(o, n_w)], gw_w.at[w]), sem_gw.at[2])
    along("w", w_size, w, lambda o: (ls_hs, ls_w.at[w]), sem_ls.at[2])

    for b in range(nb):
        drain(dbr.at[b], sem_db.at[b, 1])
        drain(ys.at[b, pl.ds(0, (ndev - 1) * 8 * tq)], sem_y.at[b, 0])
        leg_up(b, pt, dbr, True)
        send_gather(b, dyr, sem_dy)

    drain(gs_z, sem_gs.at[0, 1])
    gs_sum[...] = jnp.sum(gs_z[...], axis=0)
    along("w", w_size, w, lambda o: (gs_sum, gs_w.at[w]), sem_gs.at[1])
    drain(gw_w, sem_gw.at[2, 1])
    drain(ls_w, sem_ls.at[2, 1])
    gw_ws[...] = jnp.sum(gw_w[...], axis=0)
    loss_out[...] = jnp.sum(ls_w[...], keepdims=True).reshape(1, 1) / total_points
    along("w", w_size, w, lambda o: (gw_ws, gw_w2.at[rows_at(w, n_w)]), sem_gw.at[3])

    drain(st2, sem_st.at[1, 1])
    proj = jnp.sum(st2[...], axis=0) / (count * ndev)
    for b in range(nb):
        drain(dyr.at[b], sem_dy.at[b, 1])

        def finish(t, _, b=b):
            dn = dot(ft_tab[...], dyr[b, :, rows_at(t, 8), :].reshape(-1, nc))
            normed = (xr[b, t] - means[b]) * scales[b]
            dout[b, t] = dout[b, t] + scales[b] * (dn - normed * proj[b:b + 1])
            return 0

        lax.fori_loop(0, tq, finish, 0)
        along("w", w_size, w, lambda o, b=b: (dout.at[b, :, rows_at(o, npl)], dx_out.at[b, rows_at(w, tq)]), sem_o.at[b])

    drain(gs_w, sem_gs.at[1, 1])
    slot = dp // 2
    part = dp % 2
    for o in range(w_size):
        along("dp", dp_size, dp, lambda k, o=o: (gs_w.at[o], gs_out.at[part, l_own * o + slot]), sem_gs.at[2])
    drain(gw_w2, sem_gw.at[3, 1])
    along("h", h_size, h, lambda o: (gw_w2, gw_h2.at[rows_at(h, n_h)]), sem_gw.at[4])
    drain(gw_h2, sem_gw.at[4, 1])
    along("dp", dp_size, dp, lambda o: (gw_h2, gw_f.at[rows_at(dp, n_z)]), sem_gw.at[5])
    drain(gw_f, sem_gw.at[5, 1])
    fin = [(gw_f.at[:nc], gin_out.at[:, :nc]), (gw_f.at[nc:2 * nc], gin_out.at[:, nc:]), (gw_f.at[2 * nc:], gout_out)]
    fin = [pltpu.make_async_copy(s, d, sem_fin.at[i]) for i, (s, d) in enumerate(fin)]
    for c in fin:
        c.start()

    drain(gs_out, sem_gs.at[2, 1])
    for b in range(nb):
        drain(dx_out.at[b], sem_o.at[b, 1])
    for c in fin:
        c.wait()
    rest = ndev - 1
    for b in range(nb):
        drain(x.at[b, pl.ds(0, (w_size - 1) * tq)], sem_x.at[b, 0])
        drain(tgt.at[b, pl.ds(0, (w_size - 1) * tq)], sem_t.at[b, 0])
        drain(dsr.at[b, pl.ds(0, rest * 8 * tq)], sem_ds.at[b, 0])
        drain(als.at[b, pl.ds(0, rest * 8 * l_own)], sem_da.at[b, 0])
        drain(dbr.at[b, pl.ds(0, rest * 8 * l_own)], sem_db.at[b, 0])
        drain(ys.at[b, pl.ds(0, rest * 8 * tq)], sem_dy.at[b, 0])
        drain(dx_out.at[b, pl.ds(0, (w_size - 1) * tq)], sem_o.at[b, 0])
    drain(st.at[pl.ds(0, rest)], sem_st.at[0, 0])
    drain(st2.at[pl.ds(0, rest)], sem_st.at[1, 0])
    for k, tab in enumerate((pt, qt)):
        @pl.when(h // 2 == w)
        def _():
            drain(tab.at[:, pl.ds(0, nlat - nt)], sem_tab.at[k, 0])

        @pl.when(h // 2 != w)
        def _():
            drain(tab, sem_tab.at[k, 0])
    for i, (ref, loss_ref, n) in enumerate(((gw_z, ls_z, dp_size), (gw_h, ls_h, h_size), (gw_w, ls_w, w_size))):
        drain(ref.at[pl.ds(0, n - 1)], sem_gw.at[i, 0])
        drain(loss_ref.at[pl.ds(0, n - 1)], sem_ls.at[i, 0])
    for i, (ref, n, m) in enumerate(((gw_w2, w_size, n_w), (gw_h2, h_size, n_h), (gw_f, dp_size, n_z))):
        drain(ref.at[pl.ds(0, (n - 1) * m)], sem_gw.at[3 + i, 0])
    drain(gs_z.at[pl.ds(0, dp_size - 1)], sem_gs.at[0, 0])
    drain(gs_w.at[pl.ds(0, w_size - 1)], sem_gs.at[1, 0])
    for i in range(dp_size - 1):
        drain(gs_w, sem_gs.at[2, 0])


def solution(mesh):
    dp_size, w_size, h_size = mesh.shape["dp"], mesh.shape["w"], mesh.shape["h"]

    def local_step(field, target, lat_weight, leg_fwd, leg_inv, spec_w, w_in, w_out):
        nb, nc, nt, npl = field.shape
        nlon = npl * w_size
        tq = nt // w_size
        nm = leg_fwd.shape[0] * w_size
        ng = nm // 4
        half = nc // 2
        ndev = h_size * w_size
        nlat = nt * h_size
        nl = leg_fwd.shape[1]
        lo = nl // ndev
        total_points = nb * dp_size * nc * nlat * nlon
        fwd_np, inv_np = dft_tables(nlon, nm)
        any_spec = pl.BlockSpec(memory_space=pl.ANY)
        vmem_spec = pl.BlockSpec(memory_space=pltpu.VMEM)
        sds = lambda *s: jax.ShapeDtypeStruct(s, F32)
        vm = lambda *s: pltpu.VMEM(s, F32)
        dma = lambda *s: pltpu.SemaphoreType.DMA(s)
        rows = 2 * nc + w_out.shape[0]
        n_z, n_h, n_w = rows // dp_size, rows // dp_size // h_size, rows // dp_size // h_size // w_size
        spread, owner, back, gather = vm(nb, 8 * nlat, half), vm(nb, ng, 8 * lo, nc), vm(nb, 8 * nl, half), vm(nb, ng, 8 * tq, nc)
        grid = vm(nb, tq, nlon, nc)
        d_x, g_spec, g_in, g_out, loss = pl.pallas_call(
            functools.partial(block_kernel, (dp_size, h_size, w_size), total_points),
            name="block",
            out_shape=[sds(nb, nt, npl, nc), sds(2, lo * w_size, nc, nc), sds(nc, 2 * nc), sds(2 * nc, nc), sds(1, 1)],
            in_specs=[any_spec] * 5 + [pl.BlockSpec(memory_space=pltpu.SMEM)] + [vmem_spec] * 6,
            out_specs=[any_spec] * 4 + [vmem_spec],
            scratch_shapes=[
                grid, grid, vm(ng, 2, nb, 8 * tq, half), spread, vm(nb, 8 * nl, half), owner, vm(nb, ng, 2, 8 * lo, half), back,
                vm(nb, 8 * nlat, half), gather, grid, spread, owner, back, gather,
                vm(8, nc), vm(ndev, 8, nc), vm(8, nc), vm(ndev, 8, nc), vm(4, nlat, nl), vm(4, nlat, nl), vm(4, nl, nlat), vm(4, nl, nlat),
                vm(2, lo, nc, nc),
                vm(rows, nc), vm(dp_size, n_z, nc), vm(n_z, nc), vm(h_size, n_h, nc), vm(n_h, nc), vm(w_size, n_w, nc), vm(n_w, nc),
                vm(n_h, nc), vm(n_z, nc), vm(rows, nc),
                vm(8, nc), vm(dp_size, 8, nc), vm(8, nc), vm(h_size, 8, nc), vm(8, nc), vm(w_size, 8, nc),
                vm(2 * lo, nc, nc), vm(dp_size, nc, nc), vm(nc, nc), vm(w_size, nc, nc),
            ] + [dma(nb, 2)] * 11 + [dma(2, 2), dma(2, 2), dma(1), dma(6, 2), dma(3, 2), dma(3, 2), dma(3)],
            compiler_params=pltpu.CompilerParams(collective_id=0, has_side_effects=True, vmem_limit_bytes=62 * 1024 * 1024),
        )(field.transpose(0, 2, 3, 1), target.transpose(0, 2, 3, 1), leg_fwd.transpose(0, 2, 1), leg_inv.transpose(0, 2, 1),
          spec_w, lat_weight, w_in, w_out, jnp.asarray(fwd_np), jnp.asarray(inv_np), jnp.asarray(fwd_np.T.copy()), jnp.asarray(inv_np.T.copy()))
        return loss.reshape(()), d_x.transpose(0, 3, 1, 2), g_spec, g_in, g_out

    grid_spec = P("dp", None, "h", "w")
    table_spec = P("w", None, "h")
    kernel_spec = P(None, "h", None, None)
    return jax.shard_map(local_step, mesh=mesh, in_specs=(grid_spec, grid_spec, P("h"), table_spec, table_spec, P(), P(), P()), out_specs=(P(), grid_spec, kernel_spec, P(), P()), check_vma=False)
```

time: 1310 us -> 317 us (0.24)
  blocking collectives: 364 us -> 0 us
  local copies, waits for them, and re-layouts: 353 us -> 7.67 us
  Pallas kernels: 0 us -> 307 us
  waiting for transfers between devices: 262 us -> 0 us
  matrix products: 157 us -> 0 us
  other arithmetic: 124 us -> 0 us
  starting transfers between devices: 19.3 us -> 0 us
  between operations: 17.6 us -> 2.33 us
    pallas_call x0 -> x1, Pallas kernels: none -> 307 us  [local_step(): pl.pallas_call(functools.partial(block_kernel, (dp_size, h_size, w_size),...]
    psum x4 -> x0, blocking collectives: 256 us -> none  [the longest x1 67.3 us: local_step(): loss = lax.psum(jnp.sum(d_out * residual), all_axes) / total_points]
    unnamed x105 -> x10, local copies, waits for them, and re-layouts: 127 us -> 7.67 us
    all_to_all x4 -> x0, blocking collectives: 108 us -> none  [the longest x1 41.7 us: local_step(): y_grid = lax.all_to_all(y_half, 'w', 3, 1, tiled=True)]
    all_to_all x14 -> x0, local copies, waits for them, and re-layouts: 101 us -> none  [the longest x3 25.5 us: local_step(): d_normed = lax.all_to_all(d_lon_whole, 'w', 3, 1, tiled=True)]
    all_to_all x4 -> x0, waiting for transfers between devices: 98.7 us -> none  [the longest x1 35.5 us: local_step(): d_y_half = lax.all_to_all(d_y, 'w', 1, 3, tiled=True)]
    dot_general x22 -> x0, matrix products: 98.5 us -> none  [the longest x16 73.5 us: precise_product(): jnp.einsum(einsum_form, operand_a, operand_b, precision=PRECISE, preferre...]
    reduce_scatter x2 -> x0, waiting for transfers between devices: 87.7 us -> none  [degree_from_lat(): return lax.psum_scatter(part_sums, 'h', scatter_dimension=3, tiled=True)]
  transfers between devices with their start and end apart: 10 -> 0, of which waited for: 8 -> 0; matrix products, arithmetic and copies ran while one was open for 14% -> 0% of each run, Pallas kernels for 0% -> 0%
where the time goes in v3:
time: 317 us
  Pallas kernels  307 us (97%)
  local copies, waits for them, and re-layouts  7.67 us (2%)
    pallas_call x1, Pallas kernels, local_step(): pl.pallas_call(functools.partial(block_kernel, (dp_size, h_size, w_size),...  307 us
    unnamed x10, local copies, waits for them, and re-layouts  7.67 us

profile of v3, /device:TPU:1, one launch (start us, length us, event | category | flops | bytes accessed | tf_op | source)
XLA Modules:
  0.0 316.7 jit_solution(3345388667364041718)
XLA Ops:
  0.6 306.7 %block.1 = (f32[3,16,64,256]{3,2,1,0:T(8,128)}, f32[2,8,256,256]{3,2,1,0:T(8,128)}, f32[256,512]{1,0:T(8,128)}, f32[512,256]{1,0:T(8,128)}, f32[1,1]{1,0:T(1,128)}) custom-call(f32[3,16,64,256]{3,2,1,0:T(8,128)} %bitcast.7, f32[3,16,64,256]{3,2,1,0:T(8,128)} %bitcast.8, f32[16,16,64]{2,1,0:T(8,128)} %bitcast.9, f32[16,16,64]{2,1,0:T(8,128)} %bitcast.10, ...), custom_call_target="tpu_custom_call" | custom-call | tf_op jit(solution)/shard_map/block/pallas_call | solution.py:448
  307.9 0.0 copy-start
  307.9 4.1 %copy.23 = f32[3,256,16,64]{1,3,2,0:T(8,128)} copy(f32[3,256,16,64]{1,3,2,0:T(8,128)} %bitcast.6) | data formatting | bytes 6291456
  312.0 0.0 copy-done
  312.0 0.0 copy-start.2
  312.0 0.0 copy-start.1
  312.0 2.0 copy.24
  314.0 0.0 copy-done.2
  314.0 0.8 copy.25
  314.8 0.0 copy-done.1
  314.8 0.8 copy.26
Async XLA Ops:
  307.9 4.1 %copy-start = (f32[2,8,256,256]{3,2,1,0:T(8,128)S(1)}, f32[2,8,256,256]{3,2,1,0:T(8,128)}, u32[]{:S(2)}) copy-start(f32[2,8,256,256]{3,2,1,0:T(8,128)} %get-tuple-element.22) | copy-start | bytes 12582916
  312.0 2.0 copy-start.2
  312.0 2.8 copy-start.1

commit v4 on v3

--- a/solution.py
+++ b/solution.py
@@ -65,7 +65,7 @@
     return jnp.concatenate([v[:, 4:], v[:, :4]], axis=1)
 
 
-def block_kernel(sizes, total_points,
+def block_kernel(sizes, total_points, stop,
                  x, tgt, leg_p, leg_q, spec_w, lat, w1, w2, f_tab, g_tab, ft_tab, gt_tab,
                  dx_out, gs_out, gin_out, gout_out, loss_out,
                  xr, tr, xs, sr, als, ar, bs, br, ys, yr, dout, dsr, dar, dbr, dyr,
@@ -73,7 +73,7 @@
                  gw, gw_z, gw_zs, gw_h, gw_hs, gw_w, gw_ws, gw_w2, gw_h2, gw_f,
                  ls, ls_z, ls_zs, ls_h, ls_hs, ls_w, gsp, gs_z, gs_sum, gs_w,
                  sem_x, sem_t, sem_s, sem_a, sem_b, sem_y, sem_ds, sem_da, sem_db, sem_dy, sem_o,
-                 sem_st, sem_tab, sem_k, sem_gw, sem_ls, sem_gs, sem_fin):
+                 sem_st, sem_tab, sem_k, sem_gw, sem_ls, sem_gs, sem_gf, sem_fin):
     dp_size, h_size, w_size = sizes
     dp, h, w = lax.axis_index("dp"), lax.axis_index("h"), lax.axis_index("w")
     ndev = h_size * w_size
@@ -86,9 +86,8 @@
     nlat = nt * h_size
     l_own = als.shape[1] // 8 // ndev
     first = group == 0
-
-    load_k = pltpu.make_async_copy(spec_w.at[:, pl.ds(me * l_own, l_own)], ker, sem_k.at[0])
-    load_k.start()
+    rest = ndev - 1
+    unsent = {}
 
     def peer(k):
         return (h + k // w_size) % h_size, (w + k % w_size) % w_size
@@ -106,9 +105,13 @@
 
     lax.fori_loop(1, ndev, meet, 0)
     lax.fori_loop(1, dp_size, meet_dp, 0)
+    load_k = pltpu.make_async_copy(spec_w.at[:, pl.ds(me * l_own, l_own)], ker, sem_k.at[0])
+    load_k.start()
+    for ref in (ar, br, dar, dbr, st_s, st2_s, gw, ls):
+        ref[...] = jnp.zeros_like(ref)
     pl.semaphore_wait(barrier, ndev - 1 + dp_size - 1)
 
-    def plane(refs, sems):
+    def plane(refs, sems, size, key=None):
         src, dst = refs(me, group, half)
         keep(src, dst, sems)
 
@@ -119,8 +122,9 @@
             return 0
 
         lax.fori_loop(1, ndev, body, 0)
-
-    def along(axis, size, index, refs, sems):
+        unsent.setdefault(key, []).append(lambda: drain(size, sems.at[0]))
+
+    def along(axis, size, index, refs, sems, sent=None):
         src, dst = refs(index)
         keep(src, dst, sems)
 
@@ -131,9 +135,48 @@
             return 0
 
         lax.fori_loop(1, size, body, 0)
+        if sent is not None:
+            unsent.setdefault(None, []).append(lambda: drain(sent, sems.at[0]))
+
+    def holds(lin, g):
+        return (lin + 1) * l_own > 4 * g
+
+    def some(refs, sems, used, count, counts, key):
+        src, dst = refs(me, group, half)
+
+        @pl.when(used(me, group))
+        def _():
+            keep(src, dst, sems)
+
+        def body(k, _):
+            h2, w2_ = peer(k)
+            lin, g = h2 * w_size + w2_, group_of(h2, w2_)
+
+            @pl.when(used(lin, g))
+            def _():
+                src, dst = refs(lin, g, h2 % 2)
+                push(src, dst, sems, {"h": h2, "w": w2_})
+            return 0
+
+        lax.fori_loop(1, ndev, body, 0)
+        sent = count - jnp.where(used(me, group), 1, 0)
+        unsent.setdefault(key, []).append(lambda: take(piece, sems.at[0], sent, sorted({n - i for n in counts for i in (0, 1)} - {0})))
+
+    def take(one, sem, count, counts):
+        for n in counts:
+            @pl.when(count == n)
+            def _():
+                drain(als.at[0, pl.ds(0, n * one)], sem)
+
+    n_groups = ((me + 1) * l_own + 3) // 4
+    n_owners = ndev - (4 * group) // l_own
+    piece = 8 * l_own
+    all_groups = [2 * n for n in range(1, (ndev * l_own + 3) // 4 + 1)]
+    all_owners = [ndev - (4 * g) // l_own for g in range(h_size // 2 * w_size)]
 
     def send_rows(src, dst, b, sem):
-        along("w", w_size, w, lambda o: (src.at[b, rows_at(o, tq)], dst.at[b, :, rows_at(w, npl)]), sem.at[b])
+        along("w", w_size, w, lambda o: (src.at[b, rows_at(o, tq)], dst.at[b, :, rows_at(w, npl)]), sem.at[b],
+              x.at[b, pl.ds(0, (w_size - 1) * tq)])
 
     def send_table(src, dst, sems):
         for c in range(2):
@@ -150,17 +193,42 @@
                 def _():
                     push(a, z, sems, {"h": h2, "w": w2_})
 
+        def sent():
+            @pl.when(h // 2 == w)
+            def _():
+                drain(dst.at[:, pl.ds(0, nlat - nt)], sems.at[0])
+
+            @pl.when(h // 2 != w)
+            def _():
+                drain(dst, sems.at[0])
+
+        unsent.setdefault(None, []).append(sent)
+
     def send_spread(b, dst, sem):
-        plane(lambda lin, g, hf: (xs.at[g, hf, b], dst.at[b, rows_at(me, 8 * tq)]), sem.at[b])
+        plane(lambda lin, g, hf: (xs.at[g, hf, b], dst.at[b, rows_at(me, 8 * tq)]), sem.at[b], dst.at[b, pl.ds(0, rest * 8 * tq)], ("xs", b))
 
     def send_owner(b, dst, sem):
-        plane(lambda lin, g, hf: (als.at[b, rows_at(lin, 8 * l_own)], dst.at[b, group, :, lanes_at(half)]), sem.at[b])
+        some(lambda lin, g, hf: (als.at[b, rows_at(lin, 8 * l_own)], dst.at[b, group, :, lanes_at(half)]), sem.at[b],
+             lambda lin, g: holds(lin, group), n_owners, all_owners, ("als", b))
+
+    def got_owner(b, dst, sem):
+        take(piece, sem.at[b, 1], 2 * n_groups, all_groups)
 
     def send_back(b, dst, sem):
-        plane(lambda lin, g, hf: (bs.at[b, g, hf], dst.at[b, rows_at(me, 8 * l_own)]), sem.at[b])
+        some(lambda lin, g, hf: (bs.at[b, g, hf], dst.at[b, rows_at(me, 8 * l_own)]), sem.at[b],
+             lambda lin, g: holds(me, g), 2 * n_groups, all_groups, ("bs", b))
+
+    def got_back(b, dst, sem):
+        take(piece, sem.at[b, 1], n_owners, all_owners)
 
     def send_gather(b, dst, sem):
-        plane(lambda lin, g, hf: (ys.at[b, rows_at(lin, 8 * tq)], dst.at[b, group, :, lanes_at(half)]), sem.at[b])
+        plane(lambda lin, g, hf: (ys.at[b, rows_at(lin, 8 * tq)], dst.at[b, group, :, lanes_at(half)]), sem.at[b],
+              ys.at[b, pl.ds(0, rest * 8 * tq)], ("ys", b))
+
+    def settle(*keys):
+        for key in keys or list(unsent):
+            for wait in unsent.pop(key, []):
+                wait()
 
     def put_spec(b, t, out):
         out = out.reshape(-1, 8, nc)
@@ -168,6 +236,7 @@
             xs[:, hf, b, rows_at(t, 8), :] = out[:, :, hf * 128:(hf + 1) * 128]
 
     def leg_down(b, tab, src, fix):
+        settle(("als", b))
         for mi in range(4):
             parts = []
             for ri in range(2):
@@ -180,6 +249,7 @@
                 als[b, pl.ds(ri * 4 + mi, out.shape[0], stride=8), :] = out[:, ri * 128:(ri + 1) * 128]
 
     def leg_up(b, tab, src, fix):
+        settle(("ys", b))
         for mi in range(4):
             parts = [src[b, pl.ds(ri * 4 + mi, src.shape[1] // 8, stride=8), :] for ri in range(2)]
             out = dot(tab[mi], jnp.concatenate(parts, axis=1))
@@ -193,14 +263,15 @@
         for hf in range(2):
             bs[b, :, hf, l * 8:(l + 1) * 8, :] = out[:, :, hf * 128:(hf + 1) * 128]
 
+    def end(*recvs):
+        for r in recvs:
+            r()
+        settle()
+
     for b in range(nb):
         send_rows(x, xr, b, sem_x)
     send_table(leg_p, pt, sem_tab.at[0])
     send_table(leg_q, qt, sem_tab.at[1])
-    st_s[...] = jnp.zeros_like(st_s)
-    st2_s[...] = jnp.zeros_like(st2_s)
-    gw[...] = jnp.zeros_like(gw)
-    ls[...] = jnp.zeros_like(ls)
 
     for b in range(nb):
         drain(xr.at[b], sem_x.at[b, 1])
@@ -220,17 +291,21 @@
 
         st_s[2 * b:2 * b + 1, :] = mean
         st_s[2 * b + 1:2 * b + 2, :] = lax.fori_loop(0, tq, spread2, jnp.zeros((1, nc), F32))
-    plane(lambda lin, g, hf: (st_s, st.at[me]), sem_st.at[0])
+    plane(lambda lin, g, hf: (st_s, st.at[me]), sem_st.at[0], st.at[pl.ds(0, rest)])
 
     for tab, tabt, k in ((pt, ptt, 0), (qt, qtt, 1)):
         drain(tab, sem_tab.at[k, 1])
         for mi in range(4):
             tabt[mi] = tab[mi].T
+    if stop == 1:
+        return end(load_k.wait, lambda: drain(st, sem_st.at[0, 1]), *[lambda b=b: drain(sr.at[b], sem_s.at[b, 1]) for b in range(nb)])
 
     for b in range(nb):
         drain(sr.at[b], sem_s.at[b, 1])
         leg_down(b, ptt, sr, True)
         send_owner(b, ar, sem_a)
+    if stop == 2:
+        return end(load_k.wait, lambda: drain(st, sem_st.at[0, 1]), *[lambda b=b: got_owner(b, ar, sem_a) for b in range(nb)])
     send_rows(tgt, tr, 0, sem_t)
 
     load_k.wait()
@@ -248,7 +323,7 @@
         scales.append(lax.rsqrt(var + NORM_EPS))
         means.append(mu[2 * b:2 * b + 1])
     for b in range(nb):
-        drain(ar.at[b], sem_a.at[b, 1])
+        got_owner(b, ar, sem_a)
         for l in range(l_own):
             a = ar[b, :, l * 8:(l + 1) * 8, :] * scales[b][None]
             ar[b, :, l * 8:(l + 1) * 8, :] = a
@@ -257,19 +332,23 @@
             other = dot(a, ker[1, l]).reshape(-1, 8, nc)
             put_back(b, l, own + row_sign * swap_parts(other))
         send_back(b, br, sem_b)
+    if stop == 3:
+        return end(lambda: drain(tr.at[0], sem_t.at[0, 1]), *[lambda b=b: got_back(b, br, sem_b) for b in range(nb)])
     send_rows(tgt, tr, 1, sem_t)
 
     for b in range(nb):
-        drain(br.at[b], sem_b.at[b, 1])
+        got_back(b, br, sem_b)
         leg_up(b, qt, br, False)
         send_gather(b, yr, sem_y)
     for b in range(2, nb):
         send_rows(tgt, tr, b, sem_t)
+    if stop == 4:
+        return end(*[lambda b=b: drain(tr.at[b], sem_t.at[b, 1]) for b in range(nb)], *[lambda b=b: drain(yr.at[b], sem_y.at[b, 1]) for b in range(nb)])
 
     for b in range(nb):
         drain(yr.at[b], sem_y.at[b, 1])
         drain(tr.at[b], sem_t.at[b, 1])
-        drain(sr.at[b, pl.ds(0, (ndev - 1) * 8 * tq)], sem_s.at[b, 0])
+        settle(("xs", b))
 
         def point(t, _, b=b):
             y = dot(gt_tab[...], yr[b, :, rows_at(t, 8), :].reshape(-1, nc))
@@ -296,25 +375,30 @@
         send_spread(b, dsr, sem_ds)
 
     n_z, n_h, n_w = gw_zs.shape[0], gw_hs.shape[0], gw_ws.shape[0]
-    along("dp", dp_size, dp, lambda o: (gw.at[rows_at(o, n_z)], gw_z.at[dp]), sem_gw.at[0])
-    along("dp", dp_size, dp, lambda o: (ls, ls_z.at[dp]), sem_ls.at[0])
+    along("dp", dp_size, dp, lambda o: (gw.at[rows_at(o, n_z)], gw_z.at[dp]), sem_gw.at[0], gw_z.at[pl.ds(0, dp_size - 1)])
+    along("dp", dp_size, dp, lambda o: (ls, ls_z.at[dp]), sem_ls.at[0], ls_z.at[pl.ds(0, dp_size - 1)])
+    gw1 = [lambda: drain(gw_z, sem_gw.at[0, 1]), lambda: drain(ls_z, sem_ls.at[0, 1])]
+    if stop == 5:
+        return end(*gw1, *[lambda b=b: drain(dsr.at[b], sem_ds.at[b, 1]) for b in range(nb)])
 
     for b in range(nb):
         drain(dsr.at[b], sem_ds.at[b, 1])
-        drain(als.at[b, pl.ds(0, (ndev - 1) * 8 * l_own)], sem_a.at[b, 0])
         leg_down(b, qtt, dsr, False)
         send_owner(b, dar, sem_da)
-
-    drain(gw_z, sem_gw.at[0, 1])
-    drain(ls_z, sem_ls.at[0, 1])
+    if stop == 6:
+        return end(*gw1, *[lambda b=b: got_owner(b, dar, sem_da) for b in range(nb)])
+
+    for r in gw1:
+        r()
     gw_zs[...] = jnp.sum(gw_z[...], axis=0)
     ls_zs[...] = jnp.sum(ls_z[...], axis=0)
-    along("h", h_size, h, lambda o: (gw_zs.at[rows_at(o, n_h)], gw_h.at[h]), sem_gw.at[1])
-    along("h", h_size, h, lambda o: (ls_zs, ls_h.at[h]), sem_ls.at[1])
-
-    for b in range(nb):
-        drain(dar.at[b], sem_da.at[b, 1])
-        drain(br.at[b, pl.ds(0, (ndev - 1) * 8 * l_own)], sem_b.at[b, 0])
+    along("h", h_size, h, lambda o: (gw_zs.at[rows_at(o, n_h)], gw_h.at[h]), sem_gw.at[1], gw_h.at[pl.ds(0, h_size - 1)])
+    along("h", h_size, h, lambda o: (ls_zs, ls_h.at[h]), sem_ls.at[1], ls_h.at[pl.ds(0, h_size - 1)])
+    gw2 = [lambda: drain(gw_h, sem_gw.at[1, 1]), lambda: drain(ls_h, sem_ls.at[1, 1])]
+
+    for b in range(nb):
+        got_owner(b, dar, sem_da)
+        settle(("bs", b))
         s2 = jnp.zeros((1, nc), F32)
         for l in range(l_own):
             d = dar[b, :, l * 8:(l + 1) * 8, :].reshape(-1, nc)
@@ -325,36 +409,46 @@
             s2 = s2 + jnp.sum((da * ar[b, :, l * 8:(l + 1) * 8, :]).reshape(-1, nc), axis=0, keepdims=True)
         send_back(b, dbr, sem_db)
         st2_s[b:b + 1, :] = s2
-    plane(lambda lin, g, hf: (st2_s, st2.at[me]), sem_st.at[1])
+    plane(lambda lin, g, hf: (st2_s, st2.at[me]), sem_st.at[1], st2.at[pl.ds(0, rest)])
+    if stop == 7:
+        return end(*gw2, lambda: drain(st2, sem_st.at[1, 1]), *[lambda b=b: got_back(b, dbr, sem_db) for b in range(nb)])
 
     for l in range(l_own):
         a = ar[:, :, l * 8:(l + 1) * 8, :].reshape(-1, nc)
         d3 = dar[:, :, l * 8:(l + 1) * 8, :].reshape(-1, 8, nc)
         gsp[2 * l] = dot(a, d3.reshape(-1, nc), TN)
         gsp[2 * l + 1] = dot(a, (-row_sign * swap_parts(d3)).reshape(-1, nc), TN)
-    along("dp", dp_size, dp, lambda o: (gsp.at[o], gs_z.at[dp]), sem_gs.at[0])
-
-    drain(gw_h, sem_gw.at[1, 1])
-    drain(ls_h, sem_ls.at[1, 1])
+    along("dp", dp_size, dp, lambda o: (gsp.at[o], gs_z.at[dp]), sem_gs.at[0], gs_z.at[pl.ds(0, dp_size - 1)])
+
+    for r in gw2:
+        r()
     gw_hs[...] = jnp.sum(gw_h[...], axis=0)
     ls_hs[...] = jnp.sum(ls_h[...], axis=0)
-    along("w", w_size, w, lambda o: (gw_hs.at[rows_at(o, n_w)], gw_w.at[w]), sem_gw.at[2])
-    along("w", w_size, w, lambda o: (ls_hs, ls_w.at[w]), sem_ls.at[2])
-
-    for b in range(nb):
-        drain(dbr.at[b], sem_db.at[b, 1])
-        drain(ys.at[b, pl.ds(0, (ndev - 1) * 8 * tq)], sem_y.at[b, 0])
+    along("w", w_size, w, lambda o: (gw_hs.at[rows_at(o, n_w)], gw_w.at[w]), sem_gw.at[2], gw_w.at[pl.ds(0, w_size - 1)])
+    along("w", w_size, w, lambda o: (ls_hs, ls_w.at[w]), sem_ls.at[2], ls_w.at[pl.ds(0, w_size - 1)])
+    gw3 = [lambda: drain(gw_w, sem_gw.at[2, 1]), lambda: drain(ls_w, sem_ls.at[2, 1])]
+
+    for b in range(nb):
+        got_back(b, dbr, sem_db)
         leg_up(b, pt, dbr, True)
         send_gather(b, dyr, sem_dy)
-
+    if stop == 8:
+        return end(*gw3, lambda: drain(gs_z, sem_gs.at[0, 1]), lambda: drain(st2, sem_st.at[1, 1]),
+                   *[lambda b=b: drain(dyr.at[b], sem_dy.at[b, 1]) for b in range(nb)])
+
+    for r in gw3:
+        r()
+    gw_ws[...] = jnp.sum(gw_w[...], axis=0)
+    loss_out[...] = jnp.sum(ls_w[...], keepdims=True).reshape(1, 1) / total_points
+    along("w", w_size, w, lambda o: (gw_ws, gw_w2.at[rows_at(w, n_w)]), sem_gw.at[3], gw_w2.at[pl.ds(0, (w_size - 1) * n_w)])
     drain(gs_z, sem_gs.at[0, 1])
     gs_sum[...] = jnp.sum(gs_z[...], axis=0)
-    along("w", w_size, w, lambda o: (gs_sum, gs_w.at[w]), sem_gs.at[1])
-    drain(gw_w, sem_gw.at[2, 1])
-    drain(ls_w, sem_ls.at[2, 1])
-    gw_ws[...] = jnp.sum(gw_w[...], axis=0)
-    loss_out[...] = jnp.sum(ls_w[...], keepdims=True).reshape(1, 1) / total_points
-    along("w", w_size, w, lambda o: (gw_ws, gw_w2.at[rows_at(w, n_w)]), sem_gw.at[3])
+    along("w", w_size, w, lambda o: (gs_sum, gs_w.at[w]), sem_gs.at[1], gs_w.at[pl.ds(0, w_size - 1)])
+    drain(gw_w2, sem_gw.at[3, 1])
+    along("h", h_size, h, lambda o: (gw_w2, gw_h2.at[rows_at(h, n_h)]), sem_gw.at[4], gw_h2.at[pl.ds(0, (h_size - 1) * n_h)])
+
+    right, left = (dp + 1) % dp_size, (dp + dp_size - 1) % dp_size
+    block_at = lambda d, o: gs_out.at[d % 2, l_own * o + d // 2]
 
     drain(st2, sem_st.at[1, 1])
     proj = jnp.sum(st2[...], axis=0) / (count * ndev)
@@ -368,56 +462,40 @@
             return 0
 
         lax.fori_loop(0, tq, finish, 0)
-        along("w", w_size, w, lambda o, b=b: (dout.at[b, :, rows_at(o, npl)], dx_out.at[b, rows_at(w, tq)]), sem_o.at[b])
-
-    drain(gs_w, sem_gs.at[1, 1])
-    slot = dp // 2
-    part = dp % 2
+        along("w", w_size, w, lambda o, b=b: (dout.at[b, :, rows_at(o, npl)], dx_out.at[b, rows_at(w, tq)]), sem_o.at[b],
+              dx_out.at[b, pl.ds(0, (w_size - 1) * tq)])
+        if b == 0:
+            drain(gw_h2, sem_gw.at[4, 1])
+            along("dp", dp_size, dp, lambda o: (gw_h2, gw_f.at[rows_at(dp, n_z)]), sem_gw.at[5], gw_f.at[pl.ds(0, (dp_size - 1) * n_z)])
+        if b == nb - 2:
+            drain(gs_w, sem_gs.at[1, 1])
+            for o in range(w_size):
+                pltpu.make_async_copy(gs_w.at[o], block_at(dp, o), sem_gs.at[2, 0]).start()
+                push(gs_w.at[o], block_at(dp, o), sem_gf.at[0, o], {"dp": right})
+                push(gs_w.at[o], block_at(dp, o), sem_gf.at[1, o], {"dp": left})
+
     for o in range(w_size):
-        along("dp", dp_size, dp, lambda k, o=o: (gs_w.at[o], gs_out.at[part, l_own * o + slot]), sem_gs.at[2])
-    drain(gw_w2, sem_gw.at[3, 1])
-    along("h", h_size, h, lambda o: (gw_w2, gw_h2.at[rows_at(h, n_h)]), sem_gw.at[4])
-    drain(gw_h2, sem_gw.at[4, 1])
-    along("dp", dp_size, dp, lambda o: (gw_h2, gw_f.at[rows_at(dp, n_z)]), sem_gw.at[5])
+        way = 0 if o < w_size // 2 else 1
+        source, target = (left, right) if way == 0 else (right, left)
+        drain(gs_w.at[o], sem_gf.at[way, o, 1])
+        push(block_at(source, o), block_at(source, o), sem_gf.at[2, o], {"dp": target})
     drain(gw_f, sem_gw.at[5, 1])
     fin = [(gw_f.at[:nc], gin_out.at[:, :nc]), (gw_f.at[nc:2 * nc], gin_out.at[:, nc:]), (gw_f.at[2 * nc:], gout_out)]
     fin = [pltpu.make_async_copy(s, d, sem_fin.at[i]) for i, (s, d) in enumerate(fin)]
     for c in fin:
         c.start()
 
-    drain(gs_out, sem_gs.at[2, 1])
     for b in range(nb):
         drain(dx_out.at[b], sem_o.at[b, 1])
+    for o in range(w_size):
+        drain(gs_w.at[o], sem_gf.at[1 if o < w_size // 2 else 0, o, 1])
+        drain(gs_w.at[o], sem_gf.at[2, o, 1])
+        for i in range(3):
+            drain(gs_w.at[o], sem_gf.at[i, o, 0])
+    drain(gs_w, sem_gs.at[2, 0])
     for c in fin:
         c.wait()
-    rest = ndev - 1
-    for b in range(nb):
-        drain(x.at[b, pl.ds(0, (w_size - 1) * tq)], sem_x.at[b, 0])
-        drain(tgt.at[b, pl.ds(0, (w_size - 1) * tq)], sem_t.at[b, 0])
-        drain(dsr.at[b, pl.ds(0, rest * 8 * tq)], sem_ds.at[b, 0])
-        drain(als.at[b, pl.ds(0, rest * 8 * l_own)], sem_da.at[b, 0])
-        drain(dbr.at[b, pl.ds(0, rest * 8 * l_own)], sem_db.at[b, 0])
-        drain(ys.at[b, pl.ds(0, rest * 8 * tq)], sem_dy.at[b, 0])
-        drain(dx_out.at[b, pl.ds(0, (w_size - 1) * tq)], sem_o.at[b, 0])
-    drain(st.at[pl.ds(0, rest)], sem_st.at[0, 0])
-    drain(st2.at[pl.ds(0, rest)], sem_st.at[1, 0])
-    for k, tab in enumerate((pt, qt)):
-        @pl.when(h // 2 == w)
-        def _():
-            drain(tab.at[:, pl.ds(0, nlat - nt)], sem_tab.at[k, 0])
-
-        @pl.when(h // 2 != w)
-        def _():
-            drain(tab, sem_tab.at[k, 0])
-    for i, (ref, loss_ref, n) in enumerate(((gw_z, ls_z, dp_size), (gw_h, ls_h, h_size), (gw_w, ls_w, w_size))):
-        drain(ref.at[pl.ds(0, n - 1)], sem_gw.at[i, 0])
-        drain(loss_ref.at[pl.ds(0, n - 1)], sem_ls.at[i, 0])
-    for i, (ref, n, m) in enumerate(((gw_w2, w_size, n_w), (gw_h2, h_size, n_h), (gw_f, dp_size, n_z))):
-        drain(ref.at[pl.ds(0, (n - 1) * m)], sem_gw.at[3 + i, 0])
-    drain(gs_z.at[pl.ds(0, dp_size - 1)], sem_gs.at[0, 0])
-    drain(gs_w.at[pl.ds(0, w_size - 1)], sem_gs.at[1, 0])
-    for i in range(dp_size - 1):
-        drain(gs_w, sem_gs.at[2, 0])
+    settle()
 
 
 def solution(mesh):
@@ -445,9 +523,11 @@
         n_z, n_h, n_w = rows // dp_size, rows // dp_size // h_size, rows // dp_size // h_size // w_size
         spread, owner, back, gather = vm(nb, 8 * nlat, half), vm(nb, ng, 8 * lo, nc), vm(nb, 8 * nl, half), vm(nb, ng, 8 * tq, nc)
         grid = vm(nb, tq, nlon, nc)
-        d_x, g_spec, g_in, g_out, loss = pl.pallas_call(
-            functools.partial(block_kernel, (dp_size, h_size, w_size), total_points),
-            name="block",
+        args = (field.transpose(0, 2, 3, 1), target.transpose(0, 2, 3, 1), leg_fwd.transpose(0, 2, 1), leg_inv.transpose(0, 2, 1),
+          spec_w, lat_weight, w_in, w_out, jnp.asarray(fwd_np), jnp.asarray(inv_np), jnp.asarray(fwd_np.T.copy()), jnp.asarray(inv_np.T.copy()))
+        call = lambda stop: pl.pallas_call(
+            functools.partial(block_kernel, (dp_size, h_size, w_size), total_points, stop),
+            name="block" if stop is None else "stop%d" % stop,
             out_shape=[sds(nb, nt, npl, nc), sds(2, lo * w_size, nc, nc), sds(nc, 2 * nc), sds(2 * nc, nc), sds(1, 1)],
             in_specs=[any_spec] * 5 + [pl.BlockSpec(memory_space=pltpu.SMEM)] + [vmem_spec] * 6,
             out_specs=[any_spec] * 4 + [vmem_spec],
@@ -460,10 +540,10 @@
                 vm(n_h, nc), vm(n_z, nc), vm(rows, nc),
                 vm(8, nc), vm(dp_size, 8, nc), vm(8, nc), vm(h_size, 8, nc), vm(8, nc), vm(w_size, 8, nc),
                 vm(2 * lo, nc, nc), vm(dp_size, nc, nc), vm(nc, nc), vm(w_size, nc, nc),
-            ] + [dma(nb, 2)] * 11 + [dma(2, 2), dma(2, 2), dma(1), dma(6, 2), dma(3, 2), dma(3, 2), dma(3)],
-            compiler_params=pltpu.CompilerParams(collective_id=0, has_side_effects=True, vmem_limit_bytes=62 * 1024 * 1024),
-        )(field.transpose(0, 2, 3, 1), target.transpose(0, 2, 3, 1), leg_fwd.transpose(0, 2, 1), leg_inv.transpose(0, 2, 1),
-          spec_w, lat_weight, w_in, w_out, jnp.asarray(fwd_np), jnp.asarray(inv_np), jnp.asarray(fwd_np.T.copy()), jnp.asarray(inv_np.T.copy()))
+            ] + [dma(nb, 2)] * 11 + [dma(2, 2), dma(2, 2), dma(1), dma(6, 2), dma(3, 2), dma(3, 2), dma(3, w_size, 2), dma(3)],
+            compiler_params=pltpu.CompilerParams(collective_id=0 if stop is None else stop, has_side_effects=True, vmem_limit_bytes=62 * 1024 * 1024),
+        )(*args)
+        d_x, g_spec, g_in, g_out, loss = call(None)
         return loss.reshape(()), d_x.transpose(0, 3, 1, 2), g_spec, g_in, g_out
 
     grid_spec = P("dp", None, "h", "w")

time: 317 us -> 287 us (0.905)
  Pallas kernels: 307 us -> 277 us
    pallas_call x1, Pallas kernels: 307 us -> 277 us  [local_step(): pl.pallas_call(functools.partial(block_kernel, (dp_size, h_size, w_size),...]
where the time goes in v4:
time: 287 us
  Pallas kernels  277 us (97%)
  local copies, waits for them, and re-layouts  7.67 us (3%)
    pallas_call x1, Pallas kernels, local_step(): pl.pallas_call(functools.partial(block_kernel, (dp_size, h_size, w_size),...  277 us
    unnamed x10, local copies, waits for them, and re-layouts  7.67 us

profile of v4, /device:TPU:1, one launch (start us, length us, event | category | flops | bytes accessed | tf_op | source)
XLA Modules:
  0.0 287.0 jit_solution(8079544664092919550)
XLA Ops:
  0.6 277.0 %block.1 = (f32[3,16,64,256]{3,2,1,0:T(8,128)}, f32[2,8,256,256]{3,2,1,0:T(8,128)}, f32[256,512]{1,0:T(8,128)}, f32[512,256]{1,0:T(8,128)}, f32[1,1]{1,0:T(1,128)}) custom-call(f32[3,16,64,256]{3,2,1,0:T(8,128)} %bitcast.7, f32[3,16,64,256]{3,2,1,0:T(8,128)} %bitcast.8, f32[16,16,64]{2,1,0:T(8,128)} %bitcast.9, f32[16,16,64]{2,1,0:T(8,128)} %bitcast.10, ...), custom_call_target="tpu_custom_call" | custom-call | tf_op jit(solution)/shard_map/block/pallas_call | solution.py:528
  278.2 0.0 copy-start
  278.2 4.1 %copy.23 = f32[3,256,16,64]{1,3,2,0:T(8,128)} copy(f32[3,256,16,64]{1,3,2,0:T(8,128)} %bitcast.6) | data formatting | bytes 6291456
  282.3 0.0 copy-done
  282.3 0.0 copy-start.2
  282.3 0.0 copy-start.1
  282.3 2.0 copy.24
  284.3 0.0 copy-done.2
  284.3 0.8 copy.25
  285.1 0.0 copy-done.1
  285.1 0.8 copy.26
Async XLA Ops:
  278.2 4.1 %copy-start = (f32[2,8,256,256]{3,2,1,0:T(8,128)S(1)}, f32[2,8,256,256]{3,2,1,0:T(8,128)}, u32[]{:S(2)}) copy-start(f32[2,8,256,256]{3,2,1,0:T(8,128)} %get-tuple-element.22) | copy-start | bytes 12582916
  282.3 2.0 copy-start.2
  282.3 2.8 copy-start.1

commit v5 on v4

--- a/solution.py
+++ b/solution.py
@@ -69,7 +69,7 @@
                  x, tgt, leg_p, leg_q, spec_w, lat, w1, w2, f_tab, g_tab, ft_tab, gt_tab,
                  dx_out, gs_out, gin_out, gout_out, loss_out,
                  xr, tr, xs, sr, als, ar, bs, br, ys, yr, dout, dsr, dar, dbr, dyr,
-                 st_s, st, st2_s, st2, pt, qt, ptt, qtt, ker,
+                 st_s, st, st2_s, st2, tab_s, tab, pt, qt, ptt, qtt, ker,
                  gw, gw_z, gw_zs, gw_h, gw_hs, gw_w, gw_ws, gw_w2, gw_h2, gw_f,
                  ls, ls_z, ls_zs, ls_h, ls_hs, ls_w, gsp, gs_z, gs_sum, gs_w,
                  sem_x, sem_t, sem_s, sem_a, sem_b, sem_y, sem_ds, sem_da, sem_db, sem_dy, sem_o,
@@ -107,6 +107,8 @@
     lax.fori_loop(1, dp_size, meet_dp, 0)
     load_k = pltpu.make_async_copy(spec_w.at[:, pl.ds(me * l_own, l_own)], ker, sem_k.at[0])
     load_k.start()
+    tab_s[:, :, :leg_p.shape[2]] = leg_p[...]
+    tab_s[:, :, leg_p.shape[2]:] = leg_q[...]
     for ref in (ar, br, dar, dbr, st_s, st2_s, gw, ls):
         ref[...] = jnp.zeros_like(ref)
     pl.semaphore_wait(barrier, ndev - 1 + dp_size - 1)
@@ -270,8 +272,7 @@
 
     for b in range(nb):
         send_rows(x, xr, b, sem_x)
-    send_table(leg_p, pt, sem_tab.at[0])
-    send_table(leg_q, qt, sem_tab.at[1])
+    send_table(tab_s, tab, sem_tab.at[0])
 
     for b in range(nb):
         drain(xr.at[b], sem_x.at[b, 1])
@@ -293,10 +294,13 @@
         st_s[2 * b + 1:2 * b + 2, :] = lax.fori_loop(0, tq, spread2, jnp.zeros((1, nc), F32))
     plane(lambda lin, g, hf: (st_s, st.at[me]), sem_st.at[0], st.at[pl.ds(0, rest)])
 
-    for tab, tabt, k in ((pt, ptt, 0), (qt, qtt, 1)):
-        drain(tab, sem_tab.at[k, 1])
-        for mi in range(4):
-            tabt[mi] = tab[mi].T
+    drain(tab, sem_tab.at[0, 1])
+    for mi in range(4):
+        both = tab[mi]
+        pt[mi] = both[:, :pt.shape[2]]
+        qt[mi] = both[:, pt.shape[2]:]
+        ptt[mi] = both[:, :pt.shape[2]].T
+        qtt[mi] = both[:, pt.shape[2]:].T
     if stop == 1:
         return end(load_k.wait, lambda: drain(st, sem_st.at[0, 1]), *[lambda b=b: drain(sr.at[b], sem_s.at[b, 1]) for b in range(nb)])
 
@@ -529,12 +533,12 @@
             functools.partial(block_kernel, (dp_size, h_size, w_size), total_points, stop),
             name="block" if stop is None else "stop%d" % stop,
             out_shape=[sds(nb, nt, npl, nc), sds(2, lo * w_size, nc, nc), sds(nc, 2 * nc), sds(2 * nc, nc), sds(1, 1)],
-            in_specs=[any_spec] * 5 + [pl.BlockSpec(memory_space=pltpu.SMEM)] + [vmem_spec] * 6,
+            in_specs=[any_spec] * 2 + [vmem_spec] * 2 + [any_spec] + [pl.BlockSpec(memory_space=pltpu.SMEM)] + [vmem_spec] * 6,
             out_specs=[any_spec] * 4 + [vmem_spec],
             scratch_shapes=[
                 grid, grid, vm(ng, 2, nb, 8 * tq, half), spread, vm(nb, 8 * nl, half), owner, vm(nb, ng, 2, 8 * lo, half), back,
                 vm(nb, 8 * nlat, half), gather, grid, spread, owner, back, gather,
-                vm(8, nc), vm(ndev, 8, nc), vm(8, nc), vm(ndev, 8, nc), vm(4, nlat, nl), vm(4, nlat, nl), vm(4, nl, nlat), vm(4, nl, nlat),
+                vm(8, nc), vm(ndev, 8, nc), vm(8, nc), vm(ndev, 8, nc), vm(leg_fwd.shape[0], nt, 2 * nl), vm(4, nlat, 2 * nl), vm(4, nlat, nl), vm(4, nlat, nl), vm(4, nl, nlat), vm(4, nl, nlat),
                 vm(2, lo, nc, nc),
                 vm(rows, nc), vm(dp_size, n_z, nc), vm(n_z, nc), vm(h_size, n_h, nc), vm(n_h, nc), vm(w_size, n_w, nc), vm(n_w, nc),
                 vm(n_h, nc), vm(n_z, nc), vm(rows, nc),

time: 287 us -> 275 us (0.958)
  Pallas kernels: 277 us -> 265 us
    pallas_call x1, Pallas kernels: 277 us -> 265 us  [local_step(): pl.pallas_call(functools.partial(block_kernel, (dp_size, h_size, w_size),...]
where the time goes in v5:
time: 275 us
  Pallas kernels  265 us (96%)
  local copies, waits for them, and re-layouts  7.67 us (3%)
    pallas_call x1, Pallas kernels, local_step(): pl.pallas_call(functools.partial(block_kernel, (dp_size, h_size, w_size),...  265 us
    unnamed x10, local copies, waits for them, and re-layouts  7.67 us

profile of v5, /device:TPU:1, one launch (start us, length us, event | category | flops | bytes accessed | tf_op | source)
XLA Modules:
  0.0 274.9 jit_solution(6922641856128554918)
XLA Ops:
  0.6 264.9 %block.1 = (f32[3,16,64,256]{3,2,1,0:T(8,128)}, f32[2,8,256,256]{3,2,1,0:T(8,128)}, f32[256,512]{1,0:T(8,128)}, f32[512,256]{1,0:T(8,128)}, f32[1,1]{1,0:T(1,128)}) custom-call(f32[3,16,64,256]{3,2,1,0:T(8,128)} %bitcast.7, f32[3,16,64,256]{3,2,1,0:T(8,128)} %bitcast.8, f32[16,16,64]{2,1,0:T(8,128)} %bitcast.9, f32[16,16,64]{2,1,0:T(8,128)} %bitcast.10, ...), custom_call_target="tpu_custom_call" | custom-call | tf_op jit(solution)/shard_map/block/pallas_call | solution.py:532
  266.1 0.0 copy-start
  266.1 4.1 %copy.23 = f32[3,256,16,64]{1,3,2,0:T(8,128)} copy(f32[3,256,16,64]{1,3,2,0:T(8,128)} %bitcast.6) | data formatting | bytes 6291456
  270.2 0.0 copy-done
  270.2 0.0 copy-start.2
  270.2 0.0 copy-start.1
  270.2 2.0 copy.24
  272.2 0.0 copy-done.2
  272.2 0.8 copy.25
  273.0 0.0 copy-done.1
  273.0 0.8 copy.26
Async XLA Ops:
  266.1 4.1 %copy-start = (f32[2,8,256,256]{3,2,1,0:T(8,128)S(1)}, f32[2,8,256,256]{3,2,1,0:T(8,128)}, u32[]{:S(2)}) copy-start(f32[2,8,256,256]{3,2,1,0:T(8,128)} %get-tuple-element.22) | copy-start | bytes 12582916
  270.2 2.0 copy-start.2
  270.2 2.8 %copy-start.1 = (f32[512,256]{1,0:T(8,128)S(1)}, f32[512,256]{1,0:T(8,128)}, u32[]{:S(2)}) copy-start(f32[512,256]{1,0:T(8,128)} %get-tuple-element.24) | copy-start | bytes 1572868

commit v6 on v0

v6 whole, which is shorter than its diff:
```python
import functools
import jax
import jax.numpy as jnp
import numpy as np
from jax import lax
from jax.experimental import pallas as pl
from jax.experimental.pallas import tpu as pltpu
from jax.sharding import PartitionSpec as P

NORM_EPS = 1e-5
PRECISE = lax.Precision.HIGHEST
MESH = pl.DeviceIdType.MESH
F32 = jnp.float32
BF16 = jnp.bfloat16
GELU_C = float(np.sqrt(2.0 / np.pi))
GELU_A = 0.044715
LANES = 128
NN = (((1,), (0,)), ((), ()))
NT = (((1,), (1,)), ((), ()))
TN = (((0,), (0,)), ((), ()))


def dot(a, b, dims=NN):
    return lax.dot_general(a, b, dims, precision=PRECISE, preferred_element_type=F32)


def bdot(a, b, dims=NN):
    return lax.dot_general(a, b, dims, preferred_element_type=F32)


def dft_tables(lon_count, num_modes, h_size):
    modes, lons = np.arange(num_modes), np.arange(lon_count)
    angle = 2.0 * np.pi * ((modes[:, None] * lons[None, :]) % lon_count) / lon_count
    fwd = np.stack([np.cos(angle), -np.sin(angle)], 0) * lon_count ** -0.5
    inv = fwd * np.where(modes == 0, 1.0, 2.0)[None, :, None]

    def rows(table):
        table = table.reshape(2, h_size, num_modes // h_size, lon_count).transpose(1, 0, 2, 3)
        return table.reshape(2 * num_modes, lon_count).astype(np.float32)

    return rows(fwd), rows(inv)


def drain(ref, sem):
    pltpu.make_async_copy(ref, ref, sem).wait()


def rows_at(i, n):
    return pl.ds(pl.multiple_of(i * n, n), n)


def lanes_at(i):
    return pl.ds(pl.multiple_of(i * LANES, LANES), LANES)


def push(src, dst, sems, device):
    pltpu.make_async_remote_copy(src_ref=src, dst_ref=dst, send_sem=sems.at[0], recv_sem=sems.at[1],
                                 device_id=device, device_id_type=MESH).start()


def keep(src, dst, sems):
    pltpu.make_async_copy(src, dst, sems.at[1]).start()


def flip(v):
    return pltpu.roll(v, LANES // 2, 1)


def low(v):
    return lax.broadcasted_iota(jnp.int32, v.shape, 1) < LANES // 2


def weave(a, b):
    return jnp.where(low(a), a, flip(b)), jnp.where(low(a), flip(a), b)


def weave_wide(tiles):
    pairs = [weave(tiles[j], tiles[j + 1]) for j in range(0, len(tiles), 2)]
    return jnp.concatenate([p[0] for p in pairs], axis=1), jnp.concatenate([p[1] for p in pairs], axis=1)


def weave_tiles(a, b):
    out = []
    for j in range(0, a.shape[1], LANES):
        out.extend(weave(a[:, j:j + LANES], b[:, j:j + LANES]))
    return out


def block_kernel(sizes, total_points, stop,
                 x, tgt, leg_p, leg_q, spec_w, lat, w1, w2, f_tab, g_tab, ft_tab, gt_tab,
                 dx_out, gs_out, gin_out, gout_out, loss_out,
                 xh, th, dout, pk, rows, yrow, hy,
                 xs, sr, dsr, ys, yr, dyr, als, ar, dar, bs, br, dbr, asave, dsave,
                 st_s, st_h, st_m, st_w, tab_s, tab, down_p, down_q, up_p, up_q, ker,
                 gw, gw_z, gw_zs, gw_h, gw_hs, gw_w, gw_ws, gw_w2, gw_h2, gw_f,
                 ls, ls_z, ls_zs, ls_h, ls_hs, ls_w, gsp, gs_z, gs_sum, gs_w,
                 sem_in, sem_x, sem_y, sem_d, sem_n, sem_s, sem_ds, sem_u, sem_du, sem_a, sem_da, sem_b, sem_db, sem_o,
                 sem_st, sem_tab, sem_k, sem_gw, sem_ls, sem_gz, sem_gs, sem_gf, sem_fin):
    dp_size, h_size, w_size = sizes
    dp, h, w = lax.axis_index("dp"), lax.axis_index("h"), lax.axis_index("w")
    ndev = h_size * w_size
    me = h * w_size + w
    nb, nt, npl, nc = x.shape
    ntp = nt // 2
    nlon = npl * w_size
    nlat = nt * h_size
    nl = als.shape[1] // 8
    l_own = nl // ndev
    piece = 8 * l_own
    unsent = {}

    def peer(k):
        return (h + k // w_size) % h_size, (w + k % w_size) % w_size

    barrier = pltpu.get_barrier_semaphore()

    def meet(k, _):
        h2, w2_ = peer(k)
        pl.semaphore_signal(barrier, inc=1, device_id={"h": h2, "w": w2_}, device_id_type=MESH)
        return 0

    def meet_dp(k, _):
        pl.semaphore_signal(barrier, inc=1, device_id={"dp": (dp + k) % dp_size}, device_id_type=MESH)
        return 0

    lax.fori_loop(1, ndev, meet, 0)
    lax.fori_loop(1, dp_size, meet_dp, 0)
    loads = [pltpu.make_async_copy(x.at[b], xh.at[b], sem_in.at[b, 0]) for b in range(nb)]
    load_t = [pltpu.make_async_copy(tgt.at[b], th.at[b], sem_in.at[b, 1]) for b in range(nb)]
    load_k = pltpu.make_async_copy(spec_w.at[:, pl.ds(me * l_own, l_own)], ker, sem_k.at[0])
    for c in loads + [load_k] + load_t:
        c.start()
    tab_s[:, :, :nl] = leg_p[...]
    tab_s[:, :, nl:] = leg_q[...]
    for ref in (ar, br, dar, dbr, st_s, gw, ls):
        ref[...] = jnp.zeros_like(ref)

    def settle(*keys):
        for key in keys or list(unsent):
            for wait in unsent.pop(key, []):
                wait()

    def along(axis, size, index, refs, sems, sent, key=None):
        src, dst = refs(index)
        keep(src, dst, sems)

        def body(k, _):
            other = (index + k) % size
            src, dst = refs(other)
            push(src, dst, sems, {axis: other})
            return 0

        lax.fori_loop(1, size, body, 0)
        unsent.setdefault(key, []).append(lambda: drain(sent, sems.at[0]))

    def holds(lin, h2):
        return (lin + 1) * l_own > 8 * h2

    def some(refs, sems, used, count, counts, key):
        src, dst = refs(h, w)
        keep(src, dst, sems)

        def body(k, _):
            h2, w2_ = peer(k)

            @pl.when(used(h2 * w_size + w2_, h2))
            def _():
                src, dst = refs(h2, w2_)
                push(src, dst, sems, {"h": h2, "w": w2_})
            return 0

        lax.fori_loop(1, ndev, body, 0)
        unsent.setdefault(key, []).append(lambda: take(sems.at[0], count - 1, [n - 1 for n in counts if n > 1]))

    def take(sem, count, counts):
        for n in counts:
            @pl.when(count == n)
            def _():
                drain(als.at[0, pl.ds(0, n * piece)], sem)

    n_orders = (((me + 1) * l_own + 7) // 8) * w_size
    n_owners = ndev - (8 * h) // l_own
    all_orders = [w_size * n for n in range(1, h_size + 1)]
    all_owners = [ndev - (8 * g) // l_own for g in range(h_size)]

    def send_home_rows(b, sem):
        along("w", w_size, w, lambda o: (pk.at[b, o], rows.at[b, :, rows_at(w, npl)]), sem.at[b], pk.at[b, pl.ds(0, w_size - 1)], ("pk", b))

    def send_rows_home(b, sem):
        along("w", w_size, w, lambda o: (yrow.at[b, o], hy.at[b, w]), sem.at[b], yrow.at[b, pl.ds(0, w_size - 1)], ("yrow", b))

    def send_orders(b, dst, sem):
        along("h", h_size, h, lambda o: (xs.at[b, o], dst.at[b, rows_at(h, 16 * ntp)]), sem.at[b], xs.at[b, pl.ds(0, h_size - 1)], ("xs", b))

    def send_lats(b, dst, sem):
        along("h", h_size, h, lambda o: (ys.at[b, rows_at(o, 16 * ntp)], dst.at[b, h]), sem.at[b], xs.at[b, pl.ds(0, h_size - 1)], ("ys", b))

    def send_owner(b, dst, sem):
        some(lambda h2, w2_: (als.at[b, rows_at(h2 * w_size + w2_, piece)], dst.at[b, h, :, lanes_at(w)]), sem.at[b],
             lambda lin, h2: holds(lin, h), n_owners, all_owners, ("als", b))

    def got_owner(b, sem):
        take(sem.at[b, 1], n_orders, all_orders)

    def send_back(b, dst, sem):
        some(lambda h2, w2_: (bs.at[b, h2, w2_], dst.at[b, rows_at(me, piece)]), sem.at[b],
             lambda lin, h2: holds(me, h2), n_orders, all_orders, ("bs", b))

    def got_back(b, sem):
        take(sem.at[b, 1], n_owners, all_owners)

    def dft(b, table):
        settle(("xs", b))

        def body(k, _):
            i = 2 * k
            both = jnp.concatenate([rows[b, i], rows[b, i + 1]], axis=1)
            out = dot(table[...], both).reshape(h_size, 16, 2 * LANES)
            xs[b, :, rows_at(i, 16), :] = out[:, :, :LANES]
            xs[b, :, rows_at(i + 1, 16), :] = out[:, :, LANES:]
            return 0

        lax.fori_loop(0, ntp // 2, body, 0)

    def idft(b, table, src):
        settle(("yrow", b))

        def body(k, _):
            i = 2 * k
            both = jnp.concatenate([src[b, :, rows_at(i + j, 16), :].reshape(-1, LANES) for j in range(2)], axis=1)
            out = dot(table[...], both)
            for j in range(2):
                yrow[b, :, i + j] = out[:, j * LANES:(j + 1) * LANES].reshape(w_size, npl, LANES)
            return 0

        lax.fori_loop(0, ntp // 2, body, 0)

    def level(v):
        mean = jnp.mean(v, axis=0, keepdims=True)
        mean = 0.5 * (mean + flip(mean))
        return v - jnp.where(h == 0, mean, 0.0)

    def leg_down(b, table, src, fix):
        settle(("als", b))
        for m in range(8):
            parts = [src[b, pl.ds(ri * 8 + m, ntp * h_size, stride=16), :] for ri in range(2)]
            if fix and m == 0:
                parts[0] = level(parts[0])
            out = dot(table[m], jnp.concatenate(parts, axis=1))
            re0, re1 = out[:nl, :LANES], out[nl:, :LANES]
            im0, im1 = out[:nl, LANES:], out[nl:, LANES:]
            als[b, pl.ds(m, nl, stride=8), :] = jnp.where(low(re0), re0, im1) + flip(jnp.where(low(re0), im0, re1))

    def leg_up(b, table, src, fix):
        settle(("ys", b))
        for m in range(8):
            out = dot(table[m], src[b, pl.ds(m, nl, stride=8), :])
            re, im = weave(out[:nlat // 2], out[nlat // 2:])
            if fix and m == 0:
                re = level(re)
            ys[b, pl.ds(m, ntp * h_size, stride=16), :] = re
            ys[b, pl.ds(8 + m, ntp * h_size, stride=16), :] = im

    def owned(b, l, src):
        tiles = [src[b, :, l * 8:(l + 1) * 8, j * LANES:(j + 1) * LANES].reshape(-1, LANES) for j in range(w_size)]
        return weave_wide(tiles)

    def put_back(b, l, re, im):
        for j, tile in enumerate(weave_tiles(re, im)):
            bs[b, :, j, l * 8:(l + 1) * 8, :] = tile.reshape(h_size, 8, LANES)

    def put_rows(b, i, v0, v1):
        for j, tile in enumerate(weave_tiles(v0, v1)):
            pk[b, j, i] = tile

    def get_rows(b, i):
        return weave_wide([hy[b, j, i] for j in range(w_size)])

    count = nt * npl
    sums = []
    for b in range(nb):
        loads[b].wait()

        def pack(i, total, b=b):
            v0, v1 = xh[b, i], xh[b, i + ntp]
            put_rows(b, i, v0, v1)
            return total + jnp.sum(v0 + v1, axis=0, keepdims=True)

        sums.append(lax.fori_loop(0, ntp, pack, jnp.zeros((1, nc), F32)))
        if b == 0:
            pl.semaphore_wait(barrier, ndev - 1 + dp_size - 1)
        send_home_rows(b, sem_x)
        if b == 0:
            for c in range(2):
                for w2_ in range(w_size):
                    h2 = 2 * w + c
                    src, dst = tab_s.at[8 * c:8 * (c + 1)], tab.at[:, rows_at(h, nt)]
                    mine = jnp.logical_and(h2 == h, w == w2_)

                    @pl.when(mine)
                    def _():
                        keep(src, dst, sem_tab.at[0])

                    @pl.when(jnp.logical_not(mine))
                    def _():
                        push(src, dst, sem_tab.at[0], {"h": h2, "w": w2_})

    def tables_sent():
        @pl.when(h // 2 == w)
        def _():
            drain(tab.at[:, pl.ds(0, nlat - nt)], sem_tab.at[0, 0])

        @pl.when(h // 2 != w)
        def _():
            drain(tab, sem_tab.at[0, 0])

    unsent.setdefault(None, []).append(tables_sent)

    for b in range(nb):
        mean = sums[b] / count

        def spread(t, total, b=b, mean=mean):
            d = xh[b, t] - mean
            return total + jnp.sum(d * d, axis=0, keepdims=True)

        st_s[2 * b:2 * b + 1, :] = mean
        st_s[2 * b + 1:2 * b + 2, :] = lax.fori_loop(0, nt, spread, jnp.zeros((1, nc), F32))
    along("h", h_size, h, lambda o: (st_s, st_h.at[h]), sem_st.at[0], st_h.at[pl.ds(0, h_size - 1)])

    def combine(stats, n):
        mean = jnp.mean(stats, axis=0)
        dev = stats - mean[None]
        dev2 = jnp.sum(dev * dev, axis=0)
        m2 = jnp.sum(stats, axis=0)
        return [(mean[2 * b:2 * b + 1], m2[2 * b + 1:2 * b + 2] + n * dev2[2 * b:2 * b + 1]) for b in range(nb)]

    def stats_w():
        drain(st_h, sem_st.at[0, 1])
        st_m[...] = jnp.zeros_like(st_m)
        for b, (mean, m2) in enumerate(combine(st_h[...], count)):
            st_m[2 * b:2 * b + 1, :] = mean
            st_m[2 * b + 1:2 * b + 2, :] = m2
        along("w", w_size, w, lambda o: (st_m, st_w.at[w]), sem_st.at[1], st_w.at[pl.ds(0, w_size - 1)])

    means, scales = [], []

    def stats_done():
        drain(st_w, sem_st.at[1, 1])
        for mean, m2 in combine(st_w[...], count * h_size):
            means.append(mean)
            scales.append(lax.rsqrt(m2 / (count * ndev) + NORM_EPS))

    def tables_done():
        drain(tab, sem_tab.at[0, 1])
        for m in range(8):
            both = tab[m].reshape(h_size, 2, ntp, 2 * nl)
            t0, t1 = both[:, 0].reshape(-1, 2 * nl), both[:, 1].reshape(-1, 2 * nl)
            for k, (down, up) in enumerate(((down_p, up_p), (down_q, up_q))):
                a, z = t0[:, k * nl:(k + 1) * nl], t1[:, k * nl:(k + 1) * nl]
                up[m, :nlat // 2, :] = a
                up[m, nlat // 2:, :] = z
                down[m, :nl, :] = a.T
                down[m, nl:, :] = z.T

    def fwd_d(b):
        drain(rows.at[b], sem_x.at[b, 1])
        dft(b, f_tab)
        send_orders(b, sr, sem_s)

    def fwd_l(b):
        drain(sr.at[b], sem_s.at[b, 1])
        leg_down(b, down_p, sr, True)
        send_owner(b, ar, sem_a)

    def fwd_o(b):
        got_owner(b, sem_a)
        settle(("bs", b))
        for l in range(l_own):
            re, im = owned(b, l, ar)
            a = jnp.concatenate([re, im], axis=0) * scales[b]
            asave[b, l] = a
            n = a.shape[0] // 2
            own, other = dot(a, ker[0, l]), dot(a, ker[1, l])
            put_back(b, l, own[:n] - other[n:], own[n:] + other[:n])
        send_back(b, br, sem_b)

    def fwd_u(b):
        got_back(b, sem_b)
        leg_up(b, up_q, br, False)
        send_lats(b, yr, sem_u)

    def fwd_i(b):
        drain(yr.at[b], sem_u.at[b, 1])
        idft(b, gt_tab, yr)
        send_rows_home(b, sem_y)

    def pointwise(b):
        drain(hy.at[b], sem_y.at[b, 1])
        load_t[b].wait()
        settle(("pk", b))

        def body(k, _):
            lats = [2 * k, 2 * k + ntp, 2 * k + 1, 2 * k + 1 + ntp]
            y = jnp.concatenate([v for j in range(2) for v in get_rows(b, 2 * k + j)], axis=0)
            yb = y.astype(BF16)
            hid = bdot(yb, w1[...])
            th_ = jnp.tanh(GELU_C * (hid + GELU_A * (hid * hid * hid)))
            act = (hid * (0.5 * (1.0 + th_))).astype(BF16)
            resid = y + bdot(act, w2[...])
            parts = []
            for j, t in enumerate(lats):
                r = resid[j * npl:(j + 1) * npl] + xh[b, t] - th[b, t]
                d = lat[t] * r
                ls[...] += jnp.sum((d * r).reshape(-1, 8, nc), axis=0)
                dout[b, t] = d
                parts.append(d)
            d = jnp.concatenate(parts, axis=0)
            db = d.astype(BF16)
            gw[2 * nc:, :] += bdot(act, db, TN)
            slope = 0.5 * (1.0 + th_) + (0.5 * GELU_C) * hid * (1.0 - th_ * th_) * (1.0 + (3.0 * GELU_A) * (hid * hid))
            dh = (bdot(db, w2[...], NT) * slope).astype(BF16)
            gin = bdot(yb, dh, TN)
            gw[:nc, :] += gin[:, :nc]
            gw[nc:2 * nc, :] += gin[:, nc:]
            dy = d + bdot(dh, w1[...], NT)
            for j in range(2):
                put_rows(b, 2 * k + j, dy[2 * j * npl:(2 * j + 1) * npl], dy[(2 * j + 1) * npl:(2 * j + 2) * npl])
            return 0

        lax.fori_loop(0, ntp // 2, body, 0)
        send_home_rows(b, sem_d)

    def bwd_d(b):
        drain(rows.at[b], sem_d.at[b, 1])
        dft(b, g_tab)
        send_orders(b, dsr, sem_ds)

    def bwd_l(b):
        drain(dsr.at[b], sem_ds.at[b, 1])
        leg_down(b, down_q, dsr, False)
        send_owner(b, dar, sem_da)

    def bwd_o(b):
        got_owner(b, sem_da)
        settle(("bs", b))
        s2 = jnp.zeros((1, nc), F32)
        for l in range(l_own):
            re, im = owned(b, l, dar)
            d = jnp.concatenate([re, im], axis=0)
            dsave[b, l] = d
            n = d.shape[0] // 2
            own, other = dot(d, ker[0, l], NT), dot(d, ker[1, l], NT)
            re, im = own[:n] + other[n:], own[n:] - other[:n]
            put_back(b, l, re, im)
            s2 = s2 + jnp.sum(re * asave[b, l, :n] + im * asave[b, l, n:], axis=0, keepdims=True)
        send_back(b, dbr, sem_db)
        st_s[b:b + 1, :] = s2

    def bwd_u(b):
        got_back(b, sem_db)
        leg_up(b, up_p, dbr, True)
        send_lats(b, dyr, sem_du)

    def bwd_i(b):
        drain(dyr.at[b], sem_du.at[b, 1])
        idft(b, ft_tab, dyr)
        send_rows_home(b, sem_n)

    n_z, n_h, n_w = gw_zs.shape[0], gw_hs.shape[0], gw_ws.shape[0]

    def gw_1():
        along("dp", dp_size, dp, lambda o: (gw.at[rows_at(o, n_z)], gw_z.at[dp]), sem_gw.at[0], gw_z.at[pl.ds(0, dp_size - 1)])
        along("dp", dp_size, dp, lambda o: (ls, ls_z.at[dp]), sem_ls.at[0], ls_z.at[pl.ds(0, dp_size - 1)])

    def gw_2():
        drain(gw_z, sem_gw.at[0, 1])
        drain(ls_z, sem_ls.at[0, 1])
        gw_zs[...] = jnp.sum(gw_z[...], axis=0)
        ls_zs[...] = jnp.sum(ls_z[...], axis=0)
        along("h", h_size, h, lambda o: (gw_zs.at[rows_at(o, n_h)], gw_h.at[h]), sem_gw.at[1], gw_h.at[pl.ds(0, h_size - 1)])
        along("h", h_size, h, lambda o: (ls_zs, ls_h.at[h]), sem_ls.at[1], ls_h.at[pl.ds(0, h_size - 1)])

    def gw_3():
        drain(gw_h, sem_gw.at[1, 1])
        drain(ls_h, sem_ls.at[1, 1])
        gw_hs[...] = jnp.sum(gw_h[...], axis=0)
        ls_hs[...] = jnp.sum(ls_h[...], axis=0)
        along("w", w_size, w, lambda o: (gw_hs.at[rows_at(o, n_w)], gw_w.at[w]), sem_gw.at[2], gw_w.at[pl.ds(0, w_size - 1)])
        along("w", w_size, w, lambda o: (ls_hs, ls_w.at[w]), sem_ls.at[2], ls_w.at[pl.ds(0, w_size - 1)])

    def gw_4():
        drain(gw_w, sem_gw.at[2, 1])
        drain(ls_w, sem_ls.at[2, 1])
        gw_ws[...] = jnp.sum(gw_w[...], axis=0)
        loss_out[...] = jnp.sum(ls_w[...], keepdims=True).reshape(1, 1) / total_points
        along("w", w_size, w, lambda o: (gw_ws, gw_w2.at[rows_at(w, n_w)]), sem_gw.at[3], gw_w2.at[pl.ds(0, (w_size - 1) * n_w)])

    def gw_5():
        drain(gw_w2, sem_gw.at[3, 1])
        along("h", h_size, h, lambda o: (gw_w2, gw_h2.at[rows_at(h, n_h)]), sem_gw.at[4], gw_h2.at[pl.ds(0, (h_size - 1) * n_h)])

    def gw_6():
        drain(gw_h2, sem_gw.at[4, 1])
        along("dp", dp_size, dp, lambda o: (gw_h2, gw_f.at[rows_at(dp, n_z)]), sem_gw.at[5], gw_f.at[pl.ds(0, (dp_size - 1) * n_z)])

    cuts, _, _, n_g, _ = gs_z.shape

    def gs_1():
        for l in range(l_own):
            a = asave[:, l].reshape(-1, nc)
            d = dsave[:, l].reshape(nb, 2, -1, nc)
            gsp[2 * l] = dot(a, d.reshape(-1, nc), TN)
            turned = jnp.concatenate([d[:, 1:], -d[:, :1]], axis=1).reshape(-1, nc)
            gsp[2 * l + 1] = dot(a, turned, TN)
        for q in range(cuts):
            along("dp", dp_size, dp, lambda o, q=q: (gsp.at[o, rows_at(q, n_g)], gs_z.at[q, dp, 0]), sem_gz.at[q],
                  gs_z.at[q, pl.ds(0, dp_size - 1)])

    def gs_2(q):
        drain(gs_z.at[q], sem_gz.at[q, 1])
        gs_sum[q] = jnp.sum(gs_z[q, :, 0], axis=0)
        along("w", w_size, w, lambda o: (gs_sum.at[q], gs_w.at[q, w]), sem_gs.at[q], gs_w.at[q, pl.ds(0, w_size - 1)])

    right, left = (dp + 1) % dp_size, (dp + dp_size - 1) % dp_size
    block_at = lambda d, o, q: gs_out.at[d % 2, l_own * o + d // 2, rows_at(q, n_g)]

    def gs_3(q):
        drain(gs_w.at[q], sem_gs.at[q, 1])
        for o in range(w_size):
            pltpu.make_async_copy(gs_w.at[q, o], block_at(dp, o, q), sem_gf.at[q, 3, o, 0]).start()
            push(gs_w.at[q, o], block_at(dp, o, q), sem_gf.at[q, 0, o], {"dp": right})
            push(gs_w.at[q, o], block_at(dp, o, q), sem_gf.at[q, 1, o], {"dp": left})

    def gs_4(q):
        for o in range(w_size):
            way = 0 if o < w_size // 2 else 1
            source, target = (left, right) if way == 0 else (right, left)
            drain(gs_w.at[q, o], sem_gf.at[q, way, o, 1])
            push(block_at(source, o, q), block_at(source, o, q), sem_gf.at[q, 2, o], {"dp": target})

    def gs_5(q):
        for o in range(w_size):
            drain(gs_w.at[q, o], sem_gf.at[q, 1 if o < w_size // 2 else 0, o, 1])
            drain(gs_w.at[q, o], sem_gf.at[q, 2, o, 1])
            for i in range(4):
                drain(gs_w.at[q, o], sem_gf.at[q, i, o, 0])

    def proj_h():
        st_s[nb:, :] = jnp.zeros_like(st_s[nb:, :])
        along("h", h_size, h, lambda o: (st_s, st_h.at[h]), sem_st.at[2], st_h.at[pl.ds(0, h_size - 1)])

    def proj_w():
        drain(st_h, sem_st.at[2, 1])
        st_m[...] = jnp.sum(st_h[...], axis=0)
        along("w", w_size, w, lambda o: (st_m, st_w.at[w]), sem_st.at[3], st_w.at[pl.ds(0, w_size - 1)])

    proj = []

    def proj_done():
        drain(st_w, sem_st.at[3, 1])
        proj.append(jnp.sum(st_w[...], axis=0) / (count * ndev))

    def finish(b):
        drain(hy.at[b], sem_n.at[b, 1])

        def body(i, _):
            for t, dn in zip((i, i + ntp), get_rows(b, i)):
                normed = (xh[b, t] - means[b]) * scales[b]
                dout[b, t] = dout[b, t] + scales[b] * (dn - normed * proj[0][b:b + 1])
            return 0

        lax.fori_loop(0, ntp, body, 0)
        pltpu.make_async_copy(dout.at[b], dx_out.at[b], sem_o.at[b]).start()

    assert nb == 3
    fwd_d(0)
    stats_w()
    tables_done()
    fwd_d(1)
    fwd_l(0)
    load_k.wait()
    stats_done()
    fwd_d(2)
    fwd_l(1)
    fwd_o(0)
    fwd_l(2)
    fwd_o(1)
    fwd_u(0)
    fwd_o(2)
    fwd_u(1)
    fwd_i(0)
    fwd_u(2)
    fwd_i(1)
    fwd_i(2)
    settle(None)
    pointwise(0)
    pointwise(1)
    pointwise(2)
    gw_1()
    bwd_d(0)
    bwd_d(1)
    bwd_l(0)
    gw_2()
    bwd_d(2)
    bwd_l(1)
    bwd_o(0)
    gw_3()
    bwd_l(2)
    bwd_o(1)
    gw_4()
    bwd_u(0)
    bwd_o(2)
    gs_1()
    proj_h()
    gw_5()
    bwd_u(1)
    bwd_i(0)
    gs_2(0)
    bwd_u(2)
    bwd_i(1)
    gs_2(1)
    gw_6()
    proj_w()
    bwd_i(2)
    gs_3(0)
    gs_3(1)
    proj_done()
    finish(0)
    gs_4(0)
    finish(1)
    gs_4(1)
    drain(gw_f, sem_gw.at[5, 1])
    fin = [(gw_f.at[:nc], gin_out.at[:, :nc]), (gw_f.at[nc:2 * nc], gin_out.at[:, nc:]), (gw_f.at[2 * nc:], gout_out)]
    fin = [pltpu.make_async_copy(s, d, sem_fin.at[i]) for i, (s, d) in enumerate(fin)]
    for c in fin:
        c.start()
    finish(2)
    for q in range(cuts):
        gs_5(q)
    for b in range(nb):
        drain(dx_out.at[b], sem_o.at[b])
    for c in fin:
        c.wait()
    settle()


def solution(mesh):
    dp_size, w_size, h_size = mesh.shape["dp"], mesh.shape["w"], mesh.shape["h"]

    def local_step(field, target, lat_weight, leg_fwd, leg_inv, spec_w, w_in, w_out):
        nb, nc, nt, npl = field.shape
        nlon = npl * w_size
        ntp = nt // 2
        nm = leg_fwd.shape[0] * w_size
        ndev = h_size * w_size
        nlat = nt * h_size
        nl = leg_fwd.shape[1]
        lo = nl // ndev
        assert nm == 8 * h_size and nc == w_size * LANES // 2 and h_size == 2 * w_size and 2 * lo == dp_size and 2 * nl == LANES
        total_points = nb * dp_size * nc * nlat * nlon
        fwd_np, inv_np = dft_tables(nlon, nm, h_size)
        any_spec = pl.BlockSpec(memory_space=pl.ANY)
        vmem_spec = pl.BlockSpec(memory_space=pltpu.VMEM)
        sds = lambda *s: jax.ShapeDtypeStruct(s, F32)
        vm = lambda *s: pltpu.VMEM(s, F32)
        dma = lambda *s: pltpu.SemaphoreType.DMA(s)
        n_rows = 2 * nc + w_out.shape[0]
        n_z, n_h, n_w = n_rows // dp_size, n_rows // dp_size // h_size, n_rows // dp_size // h_size // w_size
        home = vm(nb, nt, npl, nc)
        woven = vm(nb, w_size, ntp, npl, LANES)
        order = vm(nb, 16 * nlat // 2, LANES)
        degree = vm(nb, 8 * nl, LANES)
        owner = vm(nb, h_size, 8 * lo, w_size * LANES)
        saved = vm(nb, lo, 2 * nm, nc)
        cuts = 2
        args = (field.transpose(0, 2, 3, 1), target.transpose(0, 2, 3, 1), leg_fwd.transpose(0, 2, 1), leg_inv.transpose(0, 2, 1),
                spec_w, lat_weight, w_in, w_out, jnp.asarray(fwd_np), jnp.asarray(inv_np), jnp.asarray(fwd_np.T.copy()), jnp.asarray(inv_np.T.copy()))
        call = lambda stop: pl.pallas_call(
            functools.partial(block_kernel, (dp_size, h_size, w_size), total_points, stop),
            name="block" if stop is None else "stop%d" % stop,
            out_shape=[sds(nb, nt, npl, nc), sds(2, lo * w_size, nc, nc), sds(nc, 2 * nc), sds(2 * nc, nc), sds(1, 1)],
            in_specs=[any_spec] * 2 + [vmem_spec] * 2 + [any_spec] + [pl.BlockSpec(memory_space=pltpu.SMEM)] + [vmem_spec] * 6,
            out_specs=[any_spec] * 4 + [vmem_spec],
            scratch_shapes=[
                home, home, home, woven, vm(nb, ntp, nlon, LANES), woven, woven,
                vm(nb, h_size, 16 * ntp, LANES), order, order, order, vm(nb, h_size, 16 * ntp, LANES), vm(nb, h_size, 16 * ntp, LANES),
                degree, owner, owner, vm(nb, h_size, w_size, 8 * lo, LANES), degree, degree, saved, saved,
                vm(8, nc), vm(h_size, 8, nc), vm(8, nc), vm(w_size, 8, nc),
                vm(leg_fwd.shape[0], nt, 2 * nl), vm(8, nlat, 2 * nl),
                vm(8, 2 * nl, nlat // 2), vm(8, 2 * nl, nlat // 2), vm(8, nlat, nl), vm(8, nlat, nl),
                vm(2, lo, nc, nc),
                vm(n_rows, nc), vm(dp_size, n_z, nc), vm(n_z, nc), vm(h_size, n_h, nc), vm(n_h, nc), vm(w_size, n_w, nc), vm(n_w, nc),
                vm(n_h, nc), vm(n_z, nc), vm(n_rows, nc),
                vm(8, nc), vm(dp_size, 8, nc), vm(8, nc), vm(h_size, 8, nc), vm(8, nc), vm(w_size, 8, nc),
                vm(2 * lo, nc, nc), vm(cuts, dp_size, 1, nc // cuts, nc), vm(cuts, nc // cuts, nc), vm(cuts, w_size, nc // cuts, nc),
            ] + [dma(nb, 2)] * 13 + [dma(nb), dma(4, 2), dma(1, 2), dma(1), dma(6, 2), dma(3, 2), dma(cuts, 2), dma(cuts, 2), dma(cuts, 4, w_size, 2), dma(3)],
            compiler_params=pltpu.CompilerParams(collective_id=0 if stop is None else stop, has_side_effects=True, vmem_limit_bytes=62 * 1024 * 1024),
        )(*args)
        d_x, g_spec, g_in, g_out, loss = call(None)
        return loss.reshape(()), d_x.transpose(0, 3, 1, 2), g_spec, g_in, g_out

    grid_spec = P("dp", None, "h", "w")
    table_spec = P("w", None, "h")
    kernel_spec = P(None, "h", None, None)
    return jax.shard_map(local_step, mesh=mesh, in_specs=(grid_spec, grid_spec, P("h"), table_spec, table_spec, P(), P(), P()), out_specs=(P(), grid_spec, kernel_spec, P(), P()), check_vma=False)
```

time: 1310 us -> 267 us (0.20)
  blocking collectives: 364 us -> 0 us
  local copies, waits for them, and re-layouts: 353 us -> 7.67 us
  waiting for transfers between devices: 262 us -> 0 us
  Pallas kernels: 0 us -> 254 us
  matrix products: 157 us -> 0 us
  other arithmetic: 124 us -> 0 us
  starting transfers between devices: 19.3 us -> 0 us
  between operations: 17.6 us -> 2.33 us
    psum x4 -> x0, blocking collectives: 256 us -> none  [the longest x1 67.3 us: local_step(): loss = lax.psum(jnp.sum(d_out * residual), all_axes) / total_points]
    pallas_call x0 -> x1, Pallas kernels: none -> 254 us  [local_step(): pl.pallas_call(functools.partial(block_kernel, (dp_size, h_size, w_size),...]
    unnamed x105 -> x10, local copies, waits for them, and re-layouts: 127 us -> 7.67 us
    all_to_all x4 -> x0, blocking collectives: 108 us -> none  [the longest x1 41.7 us: local_step(): y_grid = lax.all_to_all(y_half, 'w', 3, 1, tiled=True)]
    all_to_all x14 -> x0, local copies, waits for them, and re-layouts: 101 us -> none  [the longest x3 25.5 us: local_step(): d_normed = lax.all_to_all(d_lon_whole, 'w', 3, 1, tiled=True)]
    all_to_all x4 -> x0, waiting for transfers between devices: 98.7 us -> none  [the longest x1 35.5 us: local_step(): d_y_half = lax.all_to_all(d_y, 'w', 1, 3, tiled=True)]
    dot_general x22 -> x0, matrix products: 98.5 us -> none  [the longest x16 73.5 us: precise_product(): jnp.einsum(einsum_form, operand_a, operand_b, precision=PRECISE, preferre...]
    reduce_scatter x2 -> x0, waiting for transfers between devices: 87.7 us -> none  [degree_from_lat(): return lax.psum_scatter(part_sums, 'h', scatter_dimension=3, tiled=True)]
  transfers between devices with their start and end apart: 10 -> 0, of which waited for: 8 -> 0; matrix products, arithmetic and copies ran while one was open for 14% -> 0% of each run, Pallas kernels for 0% -> 0%
where the time goes in v6:
time: 267 us; the launch traced here: 264 us
  Pallas kernels  254 us (95%)
  local copies, waits for them, and re-layouts  7.67 us (3%)
    pallas_call x1, Pallas kernels, local_step(): pl.pallas_call(functools.partial(block_kernel, (dp_size, h_size, w_size),...  254 us
    unnamed x10, local copies, waits for them, and re-layouts  7.67 us

profile of v6, /device:TPU:1, one launch (start us, length us, event | category | flops | bytes accessed | tf_op | source)
XLA Modules:
  0.0 264.0 jit_solution(3859119976210021293)
XLA Ops:
  0.6 254.0 %block.1 = (f32[3,16,64,256]{3,2,1,0:T(8,128)}, f32[2,8,256,256]{3,2,1,0:T(8,128)}, f32[256,512]{1,0:T(8,128)}, f32[512,256]{1,0:T(8,128)}, f32[1,1]{1,0:T(1,128)}) custom-call(f32[3,16,64,256]{3,2,1,0:T(8,128)} %bitcast.7, f32[3,16,64,256]{3,2,1,0:T(8,128)} %bitcast.8, f32[16,16,64]{2,1,0:T(8,128)} %bitcast.9, f32[16,16,64]{2,1,0:T(8,128)} %bitcast.10, ...), custom_call_target="tpu_custom_call" | custom-call | tf_op jit(solution)/shard_map/block/pallas_call | solution.py:678
  255.2 0.0 copy-start
  255.2 4.1 %copy.23 = f32[3,256,16,64]{1,3,2,0:T(8,128)} copy(f32[3,256,16,64]{1,3,2,0:T(8,128)} %bitcast.6) | data formatting | bytes 6291456
  259.2 0.0 copy-done
  259.2 0.0 copy-start.2
  259.2 0.0 copy-start.1
  259.3 2.0 copy.24
  261.3 0.0 copy-done.2
  261.3 0.8 copy.25
  262.1 0.0 copy-done.1
  262.1 0.8 copy.26
Async XLA Ops:
  255.2 4.1 %copy-start = (f32[2,8,256,256]{3,2,1,0:T(8,128)S(1)}, f32[2,8,256,256]{3,2,1,0:T(8,128)}, u32[]{:S(2)}) copy-start(f32[2,8,256,256]{3,2,1,0:T(8,128)} %get-tuple-element.22) | copy-start | bytes 12582916
  259.2 2.0 copy-start.2
  259.2 2.8 %copy-start.1 = (f32[512,256]{1,0:T(8,128)S(1)}, f32[512,256]{1,0:T(8,128)}, u32[]{:S(2)}) copy-start(f32[512,256]{1,0:T(8,128)} %get-tuple-element.24) | copy-start | bytes 1572868

commit v7 on v6

v7 whole, which is shorter than its diff:
```python
import functools
import jax
import jax.numpy as jnp
import numpy as np
from jax import lax
from jax.experimental import pallas as pl
from jax.experimental.pallas import tpu as pltpu
from jax.sharding import PartitionSpec as P

NORM_EPS = 1e-5
PRECISE = lax.Precision.HIGHEST
MESH = pl.DeviceIdType.MESH
F32 = jnp.float32
BF16 = jnp.bfloat16
GELU_C = float(np.sqrt(2.0 / np.pi))
GELU_A = 0.044715
LANES = 128
NN = (((1,), (0,)), ((), ()))
NT = (((1,), (1,)), ((), ()))
TN = (((0,), (0,)), ((), ()))


def dot(a, b, dims=NN):
    return lax.dot_general(a, b, dims, precision=PRECISE, preferred_element_type=F32)


def bdot(a, b, dims=NN):
    return lax.dot_general(a, b, dims, preferred_element_type=F32)


def dft_tables(lon_count, num_modes, h_size):
    modes, lons = np.arange(num_modes), np.arange(lon_count)
    angle = 2.0 * np.pi * ((modes[:, None] * lons[None, :]) % lon_count) / lon_count
    fwd = np.stack([np.cos(angle), -np.sin(angle)], 0) * lon_count ** -0.5
    inv = fwd * np.where(modes == 0, 1.0, 2.0)[None, :, None]

    def rows(table):
        table = table.reshape(2, h_size, num_modes // h_size, lon_count).transpose(1, 0, 2, 3)
        return table.reshape(2 * num_modes, lon_count).astype(np.float32)

    return rows(fwd), rows(inv)


def drain(ref, sem):
    pltpu.make_async_copy(ref, ref, sem).wait()


def rows_at(i, n):
    return pl.ds(pl.multiple_of(i * n, n), n)


def lanes_at(i):
    return pl.ds(pl.multiple_of(i * LANES, LANES), LANES)


def push(src, dst, sems, device):
    pltpu.make_async_remote_copy(src_ref=src, dst_ref=dst, send_sem=sems.at[0], recv_sem=sems.at[1],
                                 device_id=device, device_id_type=MESH).start()


def keep(src, dst, sems):
    pltpu.make_async_copy(src, dst, sems.at[1]).start()


def flip(v):
    return pltpu.roll(v, LANES // 2, 1)


def low(v):
    return lax.broadcasted_iota(jnp.int32, v.shape, 1) < LANES // 2


def weave(a, b):
    return jnp.where(low(a), a, flip(b)), jnp.where(low(a), flip(a), b)


def weave_wide(tiles):
    pairs = [weave(tiles[j], tiles[j + 1]) for j in range(0, len(tiles), 2)]
    return jnp.concatenate([p[0] for p in pairs], axis=1), jnp.concatenate([p[1] for p in pairs], axis=1)


def weave_tiles(a, b):
    out = []
    for j in range(0, a.shape[1], LANES):
        out.extend(weave(a[:, j:j + LANES], b[:, j:j + LANES]))
    return out


PARTS = 2
ORDER = " ".join((
    'go', 'sX21', 'tb2', 'st2', 'sX20', 'sX00', 'fd21', 'tb3', 'sX01', 'fd20',
    'fd00', 'fl2', 'sX11', 'fd01', 'fo2', 'fl0', 'sX10', 'fu2', 'fo0', 'fi20',
    'sY20', 'fd11', 'fi21', 'sY21', 'fd10', 'pw20', 'fu0', 'sD20', 'fl1', 'fi00',
    'sY00', 'fo1', 'fi01', 'sY01', 'fu1', 'pw21', 'sD21', 'fi10', 'sY10', 'pw01',
    'fi11', 'pw00', 'sY11', 'sD00', 'sD01', 'bd21', 'pw10', 'pw11', 'gw1', 'sD11',
    'sD10', 'bd20', 'bd00', 'bl2', 'bd01', 'gw2', 'bd11', 'bl0', 'bd10', 'gw3',
    'bo2', 'gw4', 'bl1', 'gw5', 'bu2', 'bo0', 'bo1', 'bi20', 'sN20', 'gw6',
    'gs1', 'gs20', 'bi21', 'bu1', 'pj1', 'gs21', 'gs30', 'bi11', 'sN11', 'pj2',
    'end', 'sN21', 'bu0', 'bi10', 'bi00', 'gs31', 'bi01', 'sN00', 'sN01', 'fn20',
    'gs40', 'fn21', 'sN10', 'gs41', 'fn11', 'fn01', 'fn00', 'fn10', 'gs50', 'gs51',
))


def block_kernel(sizes, total_points,
                 x, tgt, leg_p, leg_q, spec_w, lat, w1, w2, f_tab, g_tab, ft_tab, gt_tab,
                 dx_out, gs_out, gin_out, gout_out, loss_out,
                 xh, th, dout, pk, rows, yrow, hy,
                 xs, sr, dsr, ys, yr, dyr, als, ar, dar, bs, br, dbr, asave, dsave, aall, dall,
                 st_s, st_h, st_m, st_w, tab_s, tab_w, tab, down_p, down_q, up_p, up_q, ker,
                 gw, gw_z, gw_zs, gw_h, gw_hs, gw_w, gw_ws, gw_w2, gw_h2, gw_f,
                 ls, ls_z, ls_zs, ls_h, ls_hs, ls_w, gs_sum, gs_w,
                 sem_x, sem_y, sem_d, sem_n, sem_s, sem_ds, sem_u, sem_du, sem_a, sem_da, sem_b, sem_db, sem_az, sem_dz,
                 sem_in, sem_o, sem_st, sem_tab, sem_k, sem_gw, sem_ls, sem_gs, sem_gf, sem_fin):
    dp_size, h_size, w_size = sizes
    dp, h, w = lax.axis_index("dp"), lax.axis_index("h"), lax.axis_index("w")
    ndev = h_size * w_size
    me = h * w_size + w
    nb, nt, npl, nc = x.shape
    ntp = nt // 2
    part = ntp // PARTS
    nlon = npl * w_size
    nlat = nt * h_size
    nl = als.shape[1] // 8
    l_own = nl // ndev
    piece = 8 * l_own
    unsent, coming = {}, {}

    def got(key):
        coming.pop(key)()

    def peer(k):
        return (h + k // w_size) % h_size, (w + k % w_size) % w_size

    barrier = pltpu.get_barrier_semaphore()

    def meet(k, _):
        h2, w2_ = peer(k)
        pl.semaphore_signal(barrier, inc=1, device_id={"h": h2, "w": w2_}, device_id_type=MESH)
        return 0

    def meet_dp(k, _):
        pl.semaphore_signal(barrier, inc=1, device_id={"dp": (dp + k) % dp_size}, device_id_type=MESH)
        return 0

    lax.fori_loop(1, ndev, meet, 0)
    lax.fori_loop(1, dp_size, meet_dp, 0)
    loads = [pltpu.make_async_copy(x.at[b], xh.at[b], sem_in.at[b, 0]) for b in range(nb)]
    load_t = [pltpu.make_async_copy(tgt.at[b], th.at[b], sem_in.at[b, 1]) for b in range(nb)]
    load_k = pltpu.make_async_copy(spec_w.at[:, pl.ds(me * l_own, l_own)], ker, sem_k.at[0])
    for c in loads + [load_k] + load_t:
        c.start()
    coming["k"] = load_k.wait
    coming.update({("t", b): load_t[b].wait for b in range(nb)})
    tab_s[:, :, :nl] = leg_p[...]
    tab_s[:, :, nl:] = leg_q[...]
    for ref in (ar, br, dar, dbr, st_s, gw, ls):
        ref[...] = jnp.zeros_like(ref)

    def settle(*keys):
        for key in keys or list(unsent):
            for wait in unsent.pop(key, []):
                wait()

    def along(axis, refs, sems, sent, key=None):
        size, index = {"dp": (dp_size, dp), "h": (h_size, h), "w": (w_size, w)}[axis]
        src, dst = refs(index)
        keep(src, dst, sems)

        def body(k, _):
            other = (index + k) % size
            src, dst = refs(other)
            push(src, dst, sems, {axis: other})
            return 0

        lax.fori_loop(1, size, body, 0)
        unsent.setdefault(key, []).append(lambda: drain(sent, sems.at[0]))

    def holds(lin, h2):
        return (lin + 1) * l_own > 8 * h2

    def some(refs, sems, used, count, counts, key):
        src, dst = refs(h, w)
        keep(src, dst, sems)

        def body(k, _):
            h2, w2_ = peer(k)

            @pl.when(used(h2 * w_size + w2_, h2))
            def _():
                src, dst = refs(h2, w2_)
                push(src, dst, sems, {"h": h2, "w": w2_})
            return 0

        lax.fori_loop(1, ndev, body, 0)
        unsent.setdefault(key, []).append(lambda: take(sems.at[0], count - 1, [n - 1 for n in counts if n > 1]))

    def take(sem, count, counts):
        for n in counts:
            @pl.when(count == n)
            def _():
                drain(als.at[0, pl.ds(0, n * piece)], sem)

    n_orders = (((me + 1) * l_own + 7) // 8) * w_size
    n_owners = ndev - (8 * h) // l_own
    all_orders = [w_size * n for n in range(1, h_size + 1)]
    all_owners = [ndev - (8 * g) // l_own for g in range(h_size)]
    pairs = lambda k: pl.ds(k * part, part)

    def at_rows(i, k):
        return pl.ds(pl.multiple_of(i * 16 * ntp + k * 16 * part, 16 * part), 16 * part)

    def send_home_rows(b, k, sem, name):
        along("w", lambda o: (pk.at[b, o, pairs(k)], rows.at[b, pairs(k), rows_at(w, npl)]), sem.at[b, k],
              pk.at[b, pl.ds(0, w_size - 1), pairs(k)], ("pk", b, k))
        coming[name, b, k] = lambda: drain(rows.at[b, pairs(k)], sem.at[b, k, 1])

    def send_rows_home(b, k, sem, name):
        along("w", lambda o: (yrow.at[b, o, pairs(k)], hy.at[b, w, pairs(k)]), sem.at[b, k],
              yrow.at[b, pl.ds(0, w_size - 1), pairs(k)], ("yrow", b, k))
        coming[name, b, k] = lambda: drain(hy.at[b, :, pairs(k)], sem.at[b, k, 1])

    def send_orders(b, k, dst, sem, name):
        along("h", lambda o: (xs.at[b, o, at_rows(0, k)], dst.at[b, at_rows(h, k)]), sem.at[b, k],
              xs.at[b, pl.ds(0, h_size - 1), at_rows(0, k)], ("xs", b, k))
        coming[name, b, k] = lambda: drain(xs.at[b, :, at_rows(0, k)], sem.at[b, k, 1])

    def send_lats(b, dst, sem, name):
        for k in range(PARTS):
            along("h", lambda o: (ys.at[b, at_rows(o, k)], dst.at[b, h, at_rows(0, k)]), sem.at[b, k],
                  xs.at[b, pl.ds(0, h_size - 1), at_rows(0, k)], ("ys", b))
            coming[name, b, k] = lambda k=k: drain(dst.at[b, :, at_rows(0, k)], sem.at[b, k, 1])

    def send_owner(b, dst, sem, name):
        some(lambda h2, w2_: (als.at[b, rows_at(h2 * w_size + w2_, piece)], dst.at[b, h, :, lanes_at(w)]), sem.at[b],
             lambda lin, h2: holds(lin, h), n_owners, all_owners, ("als", b))
        coming[name, b] = lambda: take(sem.at[b, 1], n_orders, all_orders)

    def send_back(b, dst, sem, name):
        some(lambda h2, w2_: (bs.at[b, h2, w2_], dst.at[b, rows_at(me, piece)]), sem.at[b],
             lambda lin, h2: holds(me, h2), n_orders, all_orders, ("bs", b))
        coming[name, b] = lambda: take(sem.at[b, 1], n_owners, all_owners)

    def dft(b, k, table):
        settle(("xs", b, k))

        def body(n, _):
            i = 2 * n
            both = jnp.concatenate([rows[b, i], rows[b, i + 1]], axis=1)
            out = dot(table[...], both).reshape(h_size, 16, 2 * LANES)
            xs[b, :, rows_at(i, 16), :] = out[:, :, :LANES]
            xs[b, :, rows_at(i + 1, 16), :] = out[:, :, LANES:]
            return 0

        lax.fori_loop(k * part // 2, (k + 1) * part // 2, body, 0)

    def idft(b, k, table, src):
        settle(("yrow", b, k))

        def body(n, _):
            i = 2 * n
            both = jnp.concatenate([src[b, :, rows_at(i + j, 16), :].reshape(-1, LANES) for j in range(2)], axis=1)
            out = dot(table[...], both)
            for j in range(2):
                yrow[b, :, i + j] = out[:, j * LANES:(j + 1) * LANES].reshape(w_size, npl, LANES)
            return 0

        lax.fori_loop(k * part // 2, (k + 1) * part // 2, body, 0)

    def level(v):
        mean = jnp.mean(v, axis=0, keepdims=True)
        mean = 0.5 * (mean + flip(mean))
        return v - jnp.where(h == 0, mean, 0.0)

    def leg_down(b, table, src, fix):
        settle(("als", b))
        for m in range(8):
            parts = [src[b, pl.ds(ri * 8 + m, ntp * h_size, stride=16), :] for ri in range(2)]
            if fix and m == 0:
                parts[0] = level(parts[0])
            out = dot(table[m], jnp.concatenate(parts, axis=1))
            re0, re1 = out[:nl, :LANES], out[nl:, :LANES]
            im0, im1 = out[:nl, LANES:], out[nl:, LANES:]
            als[b, pl.ds(m, nl, stride=8), :] = jnp.where(low(re0), re0, im1) + flip(jnp.where(low(re0), im0, re1))

    def leg_up(b, table, src, fix):
        settle(("ys", b))
        for m in range(8):
            out = dot(table[m], src[b, pl.ds(m, nl, stride=8), :])
            re, im = weave(out[:nlat // 2], out[nlat // 2:])
            if fix and m == 0:
                re = level(re)
            ys[b, pl.ds(m, ntp * h_size, stride=16), :] = re
            ys[b, pl.ds(8 + m, ntp * h_size, stride=16), :] = im

    def owned(b, l, src):
        tiles = [src[b, :, l * 8:(l + 1) * 8, j * LANES:(j + 1) * LANES].reshape(-1, LANES) for j in range(w_size)]
        return weave_wide(tiles)

    def put_back(b, l, re, im):
        for j, tile in enumerate(weave_tiles(re, im)):
            bs[b, :, j, l * 8:(l + 1) * 8, :] = tile.reshape(h_size, 8, LANES)

    def put_rows(b, i, v0, v1):
        for j, tile in enumerate(weave_tiles(v0, v1)):
            pk[b, j, i] = tile

    def get_rows(b, i):
        return weave_wide([hy[b, j, i] for j in range(w_size)])

    count = nt * npl

    def combine(stats, n):
        mean = jnp.mean(stats, axis=0)
        dev = stats - mean[None]
        dev2 = jnp.sum(dev * dev, axis=0)
        m2 = jnp.sum(stats, axis=0)
        return [(mean[2 * b:2 * b + 1], m2[2 * b + 1:2 * b + 2] + n * dev2[2 * b:2 * b + 1]) for b in range(nb)]

    def go():
        for b in range(nb):
            loads[b].wait()

            def pack(i, total, b=b):
                v0, v1 = xh[b, i], xh[b, i + ntp]
                put_rows(b, i, v0, v1)
                return total + jnp.sum(v0 + v1, axis=0, keepdims=True)

            mean = lax.fori_loop(0, ntp, pack, jnp.zeros((1, nc), F32)) / count

            def spread(t, total, b=b, mean=mean):
                d = xh[b, t] - mean
                return total + jnp.sum(d * d, axis=0, keepdims=True)

            st_s[2 * b:2 * b + 1, :] = mean
            st_s[2 * b + 1:2 * b + 2, :] = lax.fori_loop(0, nt, spread, jnp.zeros((1, nc), F32))
        pl.semaphore_wait(barrier, ndev - 1 + dp_size - 1)
        along("w", lambda o: (st_s, st_w.at[w]), sem_st.at[0], st_w.at[pl.ds(0, w_size - 1)], "st")
        coming["st"] = lambda: drain(st_w, sem_st.at[0, 1])
        along("w", lambda o: (tab_s, tab_w.at[w]), sem_tab.at[0], tab_w.at[pl.ds(0, w_size - 1)])
        coming["tab"] = lambda: drain(tab_w, sem_tab.at[0, 1])

    def st2():
        got("st")
        st_m[...] = jnp.zeros_like(st_m)
        for b, (mean, m2) in enumerate(combine(st_w[...], count)):
            st_m[2 * b:2 * b + 1, :] = mean
            st_m[2 * b + 1:2 * b + 2, :] = m2
        along("h", lambda o: (st_m, st_h.at[h]), sem_st.at[1], st_h.at[pl.ds(0, h_size - 1)], "st")
        coming["st2"] = lambda: drain(st_h, sem_st.at[1, 1])

    means, scales = [], []

    def st3():
        got("st2")
        for mean, m2 in combine(st_h[...], count * w_size):
            means.append(mean)
            scales.append(lax.rsqrt(m2 / (count * ndev) + NORM_EPS))

    def tb2():
        got("tab")
        along("h", lambda o: (tab_w.at[o // 2, rows_at(o % 2, 8)], tab.at[:, rows_at(h, nt)]), sem_tab.at[1], tab.at[:, pl.ds(0, nlat - nt)])
        coming["tab2"] = lambda: drain(tab, sem_tab.at[1, 1])

    def tb3():
        got("tab2")
        for m in range(8):
            both = tab[m].reshape(h_size, 2, ntp, 2 * nl)
            t0, t1 = both[:, 0].reshape(-1, 2 * nl), both[:, 1].reshape(-1, 2 * nl)
            for k, (down, up) in enumerate(((down_p, up_p), (down_q, up_q))):
                a, z = t0[:, k * nl:(k + 1) * nl], t1[:, k * nl:(k + 1) * nl]
                up[m, :nlat // 2, :] = a
                up[m, nlat // 2:, :] = z
                down[m, :nl, :] = a.T
                down[m, nl:, :] = z.T

    def sX(b, k):
        send_home_rows(b, k, sem_x, "x")

    def fd(b, k):
        got(("x", b, k))
        dft(b, k, f_tab)
        send_orders(b, k, sr, sem_s, "s")

    def fl(b):
        for k in range(PARTS):
            got(("s", b, k))
        leg_down(b, down_p, sr, True)
        send_owner(b, ar, sem_a, "a")

    def fo(b):
        if not scales:
            got("k")
            st3()
        got(("a", b))
        settle(("bs", b))
        for l in range(l_own):
            re, im = owned(b, l, ar)
            a = jnp.concatenate([re, im], axis=0) * scales[b]
            asave[b, l] = a
            n = a.shape[0] // 2
            own, other = dot(a, ker[0, l]), dot(a, ker[1, l])
            put_back(b, l, own[:n] - other[n:], own[n:] + other[:n])
        send_back(b, br, sem_b, "b")
        along("dp", lambda o: (asave.at[b, o // 2], aall.at[dp, b]), sem_az.at[b], aall.at[pl.ds(0, dp_size - 1), b])
        coming["az", b] = lambda: drain(aall.at[:, b], sem_az.at[b, 1])

    def fu(b):
        got(("b", b))
        leg_up(b, up_q, br, False)
        send_lats(b, yr, sem_u, "u")

    def fi(b, k):
        got(("u", b, k))
        idft(b, k, gt_tab, yr)

    def sY(b, k):
        send_rows_home(b, k, sem_y, "y")

    def pw(b, k):
        got(("y", b, k))
        if ("t", b) in coming:
            got(("t", b))
        settle(("pk", b, k))

        def body(n, _):
            lats = [2 * n, 2 * n + ntp, 2 * n + 1, 2 * n + 1 + ntp]
            y = jnp.concatenate([v for j in range(2) for v in get_rows(b, 2 * n + j)], axis=0)
            yb = y.astype(BF16)
            hid = bdot(yb, w1[...])
            th_ = jnp.tanh(GELU_C * (hid + GELU_A * (hid * hid * hid)))
            act = (hid * (0.5 * (1.0 + th_))).astype(BF16)
            resid = y + bdot(act, w2[...])
            parts = []
            for j, t in enumerate(lats):
                r = resid[j * npl:(j + 1) * npl] + xh[b, t] - th[b, t]
                d = lat[t] * r
                ls[...] += jnp.sum((d * r).reshape(-1, 8, nc), axis=0)
                dout[b, t] = d
                parts.append(d)
            d = jnp.concatenate(parts, axis=0)
            db = d.astype(BF16)
            gw[2 * nc:, :] += bdot(act, db, TN)
            slope = 0.5 * (1.0 + th_) + (0.5 * GELU_C) * hid * (1.0 - th_ * th_) * (1.0 + (3.0 * GELU_A) * (hid * hid))
            dh = (bdot(db, w2[...], NT) * slope).astype(BF16)
            gin = bdot(yb, dh, TN)
            gw[:nc, :] += gin[:, :nc]
            gw[nc:2 * nc, :] += gin[:, nc:]
            dy = d + bdot(dh, w1[...], NT)
            for j in range(2):
                put_rows(b, 2 * n + j, dy[2 * j * npl:(2 * j + 1) * npl], dy[(2 * j + 1) * npl:(2 * j + 2) * npl])
            return 0

        lax.fori_loop(k * part // 2, (k + 1) * part // 2, body, 0)

    def sD(b, k):
        send_home_rows(b, k, sem_d, "d")

    def bd(b, k):
        got(("d", b, k))
        dft(b, k, g_tab)
        send_orders(b, k, dsr, sem_ds, "ds")

    def bl(b):
        for k in range(PARTS):
            got(("ds", b, k))
        leg_down(b, down_q, dsr, False)
        send_owner(b, dar, sem_da, "da")

    def bo(b):
        got(("da", b))
        settle(("bs", b), "st")
        s2 = jnp.zeros((1, nc), F32)
        for l in range(l_own):
            re, im = owned(b, l, dar)
            d = jnp.concatenate([re, im], axis=0)
            dsave[b, l] = d
            n = d.shape[0] // 2
            own, other = dot(d, ker[0, l], NT), dot(d, ker[1, l], NT)
            re, im = own[:n] + other[n:], own[n:] - other[:n]
            put_back(b, l, re, im)
            s2 = s2 + jnp.sum(re * asave[b, l, :n] + im * asave[b, l, n:], axis=0, keepdims=True)
        send_back(b, dbr, sem_db, "db")
        along("dp", lambda o: (dsave.at[b, o // 2, :, lanes_at(o % 2)], dall.at[dp, b]), sem_dz.at[b], dall.at[pl.ds(0, dp_size - 1), b])
        coming["dz", b] = lambda: drain(dall.at[:, b], sem_dz.at[b, 1])
        st_s[b:b + 1, :] = s2

    def bu(b):
        got(("db", b))
        leg_up(b, up_p, dbr, True)
        send_lats(b, dyr, sem_du, "du")

    def bi(b, k):
        got(("du", b, k))
        idft(b, k, ft_tab, dyr)

    def sN(b, k):
        send_rows_home(b, k, sem_n, "n")

    def pj1():
        st_s[nb:, :] = jnp.zeros_like(st_s[nb:, :])
        along("w", lambda o: (st_s, st_w.at[w]), sem_st.at[2], st_w.at[pl.ds(0, w_size - 1)])
        coming["pj"] = lambda: drain(st_w, sem_st.at[2, 1])

    def pj2():
        got("pj")
        st_m[...] = jnp.sum(st_w[...], axis=0)
        along("h", lambda o: (st_m, st_h.at[h]), sem_st.at[3], st_h.at[pl.ds(0, h_size - 1)])
        coming["pj2"] = lambda: drain(st_h, sem_st.at[3, 1])

    proj = []

    def fn(b, k):
        if not proj:
            got("pj2")
            proj.append(jnp.sum(st_h[...], axis=0) / (count * ndev))
        got(("n", b, k))

        def body(i, _):
            for t, dn in zip((i, i + ntp), get_rows(b, i)):
                normed = (xh[b, t] - means[b]) * scales[b]
                dout[b, t] = dout[b, t] + scales[b] * (dn - normed * proj[0][b:b + 1])
            return 0

        lax.fori_loop(k * part, (k + 1) * part, body, 0)
        for j in range(2):
            lats = pl.ds(j * ntp + k * part, part)
            pltpu.make_async_copy(dout.at[b, lats], dx_out.at[b, lats], sem_o.at[b, k, j]).start()
            unsent.setdefault(None, []).append(lambda lats=lats, j=j: drain(dx_out.at[b, lats], sem_o.at[b, k, j]))

    n_z, n_h, n_w = gw_zs.shape[0], gw_hs.shape[0], gw_ws.shape[0]

    def gw1():
        along("dp", lambda o: (gw.at[rows_at(o, n_z)], gw_z.at[dp]), sem_gw.at[0], gw_z.at[pl.ds(0, dp_size - 1)])
        along("dp", lambda o: (ls, ls_z.at[dp]), sem_ls.at[0], ls_z.at[pl.ds(0, dp_size - 1)])
        coming["gw1"] = lambda: (drain(gw_z, sem_gw.at[0, 1]), drain(ls_z, sem_ls.at[0, 1]))

    def gw2():
        got("gw1")
        gw_zs[...] = jnp.sum(gw_z[...], axis=0)
        ls_zs[...] = jnp.sum(ls_z[...], axis=0)
        along("h", lambda o: (gw_zs.at[rows_at(o, n_h)], gw_h.at[h]), sem_gw.at[1], gw_h.at[pl.ds(0, h_size - 1)])
        along("h", lambda o: (ls_zs, ls_h.at[h]), sem_ls.at[1], ls_h.at[pl.ds(0, h_size - 1)])
        coming["gw2"] = lambda: (drain(gw_h, sem_gw.at[1, 1]), drain(ls_h, sem_ls.at[1, 1]))

    def gw3():
        got("gw2")
        gw_hs[...] = jnp.sum(gw_h[...], axis=0)
        ls_hs[...] = jnp.sum(ls_h[...], axis=0)
        along("w", lambda o: (gw_hs.at[rows_at(o, n_w)], gw_w.at[w]), sem_gw.at[2], gw_w.at[pl.ds(0, w_size - 1)])
        along("w", lambda o: (ls_hs, ls_w.at[w]), sem_ls.at[2], ls_w.at[pl.ds(0, w_size - 1)])
        coming["gw3"] = lambda: (drain(gw_w, sem_gw.at[2, 1]), drain(ls_w, sem_ls.at[2, 1]))

    def gw4():
        got("gw3")
        gw_ws[...] = jnp.sum(gw_w[...], axis=0)
        loss_out[...] = jnp.sum(ls_w[...], keepdims=True).reshape(1, 1) / total_points
        along("w", lambda o: (gw_ws, gw_w2.at[rows_at(w, n_w)]), sem_gw.at[3], gw_w2.at[pl.ds(0, (w_size - 1) * n_w)])
        coming["gw4"] = lambda: drain(gw_w2, sem_gw.at[3, 1])

    def gw5():
        got("gw4")
        along("h", lambda o: (gw_w2, gw_h2.at[rows_at(h, n_h)]), sem_gw.at[4], gw_h2.at[pl.ds(0, (h_size - 1) * n_h)])
        coming["gw5"] = lambda: drain(gw_h2, sem_gw.at[4, 1])

    def gw6():
        got("gw5")
        along("dp", lambda o: (gw_h2, gw_f.at[rows_at(dp, n_z)]), sem_gw.at[5], gw_f.at[pl.ds(0, (dp_size - 1) * n_z)])
        coming["gw6"] = lambda: drain(gw_f, sem_gw.at[5, 1])

    def end():
        got("gw6")
        outs = [(gw_f.at[:nc], gin_out.at[:, :nc]), (gw_f.at[nc:2 * nc], gin_out.at[:, nc:]), (gw_f.at[2 * nc:], gout_out)]
        for i, (src, dst) in enumerate(outs):
            pltpu.make_async_copy(src, dst, sem_fin.at[i]).start()
            unsent.setdefault(None, []).append(lambda dst=dst, i=i: drain(dst, sem_fin.at[i]))

    cuts, _, n_g, _ = gs_sum.shape

    def gs1():
        for b in range(nb):
            got(("az", b))
            got(("dz", b))
        d = dall[...].reshape(dp_size * nb, 2, -1, LANES)
        turned = jnp.concatenate([d[:, 1:], -d[:, :1]], axis=1)
        both = jnp.concatenate([d.reshape(-1, LANES), turned.reshape(-1, LANES)], axis=1)
        out = dot(aall[...].reshape(-1, nc), both, TN)
        for q in range(cuts):
            for p in range(2):
                gs_sum[q, p] = out[q * n_g:(q + 1) * n_g, p * LANES:(p + 1) * LANES]

    def gs2(q):
        along("w", lambda o: (gs_sum.at[q], gs_w.at[q, w]), sem_gs.at[q], gs_w.at[q, pl.ds(0, w_size - 1)])
        coming["gs", q] = lambda: drain(gs_w.at[q], sem_gs.at[q, 1])

    right, left = (dp + 1) % dp_size, (dp + dp_size - 1) % dp_size
    block_at = lambda d, o, q: gs_out.at[:, l_own * o + d // 2, rows_at(q, n_g), lanes_at(d % 2)]

    def gs3(q):
        got(("gs", q))
        for o in range(w_size):
            pltpu.make_async_copy(gs_w.at[q, o], block_at(dp, o, q), sem_gf.at[q, 3, o, 0]).start()
            push(gs_w.at[q, o], block_at(dp, o, q), sem_gf.at[q, 0, o], {"dp": right})
            push(gs_w.at[q, o], block_at(dp, o, q), sem_gf.at[q, 1, o], {"dp": left})

    def gs4(q):
        for o in range(w_size):
            way = 0 if o < w_size // 2 else 1
            source, target = (left, right) if way == 0 else (right, left)
            drain(gs_w.at[q, o], sem_gf.at[q, way, o, 1])
            push(block_at(source, o, q), block_at(source, o, q), sem_gf.at[q, 2, o], {"dp": target})

    def gs5(q):
        for o in range(w_size):
            drain(gs_w.at[q, o], sem_gf.at[q, 1 if o < w_size // 2 else 0, o, 1])
            drain(gs_w.at[q, o], sem_gf.at[q, 2, o, 1])
            for i in range(4):
                drain(gs_w.at[q, o], sem_gf.at[q, i, o, 0])

    scope = dict(locals())
    for name in ORDER.split():
        call = name.rstrip("0123456789") or name
        if name in scope:
            scope[name]()
        elif name[:2] == "gs" and len(name) == 4:
            scope[name[:3]](int(name[3]))
        else:
            scope[call](*map(int, name[len(call):]))
    assert not coming
    settle()


def solution(mesh):
    dp_size, w_size, h_size = mesh.shape["dp"], mesh.shape["w"], mesh.shape["h"]

    def local_step(field, target, lat_weight, leg_fwd, leg_inv, spec_w, w_in, w_out):
        nb, nc, nt, npl = field.shape
        nlon = npl * w_size
        ntp = nt // 2
        nm = leg_fwd.shape[0] * w_size
        ndev = h_size * w_size
        nlat = nt * h_size
        nl = leg_fwd.shape[1]
        lo = nl // ndev
        assert nm == 8 * h_size and nc == w_size * LANES // 2 and h_size == 2 * w_size and 2 * lo == dp_size and 2 * nl == LANES
        total_points = nb * dp_size * nc * nlat * nlon
        fwd_np, inv_np = dft_tables(nlon, nm, h_size)
        any_spec = pl.BlockSpec(memory_space=pl.ANY)
        vmem_spec = pl.BlockSpec(memory_space=pltpu.VMEM)
        sds = lambda *s: jax.ShapeDtypeStruct(s, F32)
        vm = lambda *s: pltpu.VMEM(s, F32)
        dma = lambda *s: pltpu.SemaphoreType.DMA(s)
        n_rows = 2 * nc + w_out.shape[0]
        n_z, n_h, n_w = n_rows // dp_size, n_rows // dp_size // h_size, n_rows // dp_size // h_size // w_size
        home = vm(nb, nt, npl, nc)
        woven = vm(nb, w_size, ntp, npl, LANES)
        order = vm(nb, 16 * nlat // 2, LANES)
        degree = vm(nb, 8 * nl, LANES)
        owner = vm(nb, h_size, 8 * lo, w_size * LANES)
        saved = vm(nb, lo, 2 * nm, nc)
        cuts = 2
        d_x, g_spec, g_in, g_out, loss = pl.pallas_call(
            functools.partial(block_kernel, (dp_size, h_size, w_size), total_points),
            name="block",
            out_shape=[sds(nb, nt, npl, nc), sds(2, lo * w_size, nc, nc), sds(nc, 2 * nc), sds(2 * nc, nc), sds(1, 1)],
            in_specs=[any_spec] * 2 + [vmem_spec] * 2 + [any_spec] + [pl.BlockSpec(memory_space=pltpu.SMEM)] + [vmem_spec] * 6,
            out_specs=[any_spec] * 4 + [vmem_spec],
            scratch_shapes=[
                home, home, home, woven, vm(nb, ntp, nlon, LANES), woven, woven,
                vm(nb, h_size, 16 * ntp, LANES), order, order, order, vm(nb, h_size, 16 * ntp, LANES), vm(nb, h_size, 16 * ntp, LANES),
                degree, owner, owner, vm(nb, h_size, w_size, 8 * lo, LANES), degree, degree, saved, saved,
                vm(dp_size, nb, 2 * nm, nc), vm(dp_size, nb, 2 * nm, LANES),
                vm(8, nc), vm(h_size, 8, nc), vm(8, nc), vm(w_size, 8, nc),
                vm(leg_fwd.shape[0], nt, 2 * nl), vm(w_size, leg_fwd.shape[0], nt, 2 * nl), vm(8, nlat, 2 * nl),
                vm(8, 2 * nl, nlat // 2), vm(8, 2 * nl, nlat // 2), vm(8, nlat, nl), vm(8, nlat, nl),
                vm(2, lo, nc, nc),
                vm(n_rows, nc), vm(dp_size, n_z, nc), vm(n_z, nc), vm(h_size, n_h, nc), vm(n_h, nc), vm(w_size, n_w, nc), vm(n_w, nc),
                vm(n_h, nc), vm(n_z, nc), vm(n_rows, nc),
                vm(8, nc), vm(dp_size, 8, nc), vm(8, nc), vm(h_size, 8, nc), vm(8, nc), vm(w_size, 8, nc),
                vm(cuts, 2, nc // cuts, LANES), vm(cuts, w_size, 2, nc // cuts, LANES),
            ] + [dma(nb, PARTS, 2)] * 8 + [dma(nb, 2)] * 6 + [dma(nb, 2), dma(nb, PARTS, 2), dma(4, 2), dma(2, 2), dma(1), dma(6, 2), dma(3, 2),
                 dma(cuts, 2), dma(cuts, 4, w_size, 2), dma(3)],
            compiler_params=pltpu.CompilerParams(collective_id=0, has_side_effects=True, vmem_limit_bytes=62 * 1024 * 1024),
        )(field.transpose(0, 2, 3, 1), target.transpose(0, 2, 3, 1), leg_fwd.transpose(0, 2, 1), leg_inv.transpose(0, 2, 1),
          spec_w, lat_weight, w_in, w_out, jnp.asarray(fwd_np), jnp.asarray(inv_np), jnp.asarray(fwd_np.T.copy()), jnp.asarray(inv_np.T.copy()))
        return loss.reshape(()), d_x.transpose(0, 3, 1, 2), g_spec, g_in, g_out

    grid_spec = P("dp", None, "h", "w")
    table_spec = P("w", None, "h")
    kernel_spec = P(None, "h", None, None)
    return jax.shard_map(local_step, mesh=mesh, in_specs=(grid_spec, grid_spec, P("h"), table_spec, table_spec, P(), P(), P()), out_specs=(P(), grid_spec, kernel_spec, P(), P()), check_vma=False)
```

time: 267 us -> 225 us (0.84); the launches traced: 264 us -> 225 us
  Pallas kernels: 254 us -> 215 us
    pallas_call x1, Pallas kernels: 254 us -> 215 us  [local_step(): pl.pallas_call(functools.partial(block_kernel, (dp_size, h_size, w_size),...]
where the time goes in v7:
time: 225 us
  Pallas kernels  215 us (96%)
  local copies, waits for them, and re-layouts  7.67 us (3%)
  between operations  2.33 us (1%)
    pallas_call x1, Pallas kernels, local_step(): pl.pallas_call(functools.partial(block_kernel, (dp_size, h_size, w_size),...  215 us
    unnamed x10, local copies, waits for them, and re-layouts  7.67 us

profile of v7, /device:TPU:1, one launch (start us, length us, event | category | flops | bytes accessed | tf_op | source)
XLA Modules:
  0.0 225.2 jit_solution(1684139924019074300)
XLA Ops:
  0.6 215.2 %block.1 = (f32[3,16,64,256]{3,2,1,0:T(8,128)}, f32[2,8,256,256]{3,2,1,0:T(8,128)}, f32[256,512]{1,0:T(8,128)}, f32[512,256]{1,0:T(8,128)}, f32[1,1]{1,0:T(1,128)}) custom-call(f32[3,16,64,256]{3,2,1,0:T(8,128)} %bitcast.7, f32[3,16,64,256]{3,2,1,0:T(8,128)} %bitcast.8, f32[16,16,64]{2,1,0:T(8,128)} %bitcast.9, f32[16,16,64]{2,1,0:T(8,128)} %bitcast.10, ...), custom_call_target="tpu_custom_call" | custom-call | tf_op jit(solution)/shard_map/block/pallas_call | solution.py:661
  216.4 0.0 copy-start
  216.4 4.1 %copy.23 = f32[3,256,16,64]{1,3,2,0:T(8,128)} copy(f32[3,256,16,64]{1,3,2,0:T(8,128)} %bitcast.6) | data formatting | bytes 6291456
  220.5 0.0 copy-done
  220.5 0.0 copy-start.2
  220.5 0.0 copy-start.1
  220.5 2.0 copy.24
  222.5 0.0 copy-done.2
  222.5 0.8 copy.25
  223.3 0.0 copy-done.1
  223.3 0.8 copy.26
Async XLA Ops:
  216.4 4.1 %copy-start = (f32[2,8,256,256]{3,2,1,0:T(8,128)S(1)}, f32[2,8,256,256]{3,2,1,0:T(8,128)}, u32[]{:S(2)}) copy-start(f32[2,8,256,256]{3,2,1,0:T(8,128)} %get-tuple-element.22) | copy-start | bytes 12582916
  220.5 2.0 copy-start.2
  220.5 2.8 %copy-start.1 = (f32[512,256]{1,0:T(8,128)S(1)}, f32[512,256]{1,0:T(8,128)}, u32[]{:S(2)}) copy-start(f32[512,256]{1,0:T(8,128)} %get-tuple-element.24) | copy-start | bytes 1572868

commit v8 on v7

--- a/solution.py
+++ b/solution.py
@@ -88,29 +88,31 @@
 
 PARTS = 2
 ORDER = " ".join((
-    'go', 'sX21', 'tb2', 'st2', 'sX20', 'sX00', 'fd21', 'tb3', 'sX01', 'fd20',
-    'fd00', 'fl2', 'sX11', 'fd01', 'fo2', 'fl0', 'sX10', 'fu2', 'fo0', 'fi20',
-    'sY20', 'fd11', 'fi21', 'sY21', 'fd10', 'pw20', 'fu0', 'sD20', 'fl1', 'fi00',
-    'sY00', 'fo1', 'fi01', 'sY01', 'fu1', 'pw21', 'sD21', 'fi10', 'sY10', 'pw01',
-    'fi11', 'pw00', 'sY11', 'sD00', 'sD01', 'bd21', 'pw10', 'pw11', 'gw1', 'sD11',
-    'sD10', 'bd20', 'bd00', 'bl2', 'bd01', 'gw2', 'bd11', 'bl0', 'bd10', 'gw3',
-    'bo2', 'gw4', 'bl1', 'gw5', 'bu2', 'bo0', 'bo1', 'bi20', 'sN20', 'gw6',
-    'gs1', 'gs20', 'bi21', 'bu1', 'pj1', 'gs21', 'gs30', 'bi11', 'sN11', 'pj2',
-    'end', 'sN21', 'bu0', 'bi10', 'bi00', 'gs31', 'bi01', 'sN00', 'sN01', 'fn20',
-    'gs40', 'fn21', 'sN10', 'gs41', 'fn11', 'fn01', 'fn00', 'fn10', 'gs50', 'gs51',
+    'go', 'sX20', 'sX21', 'sX00', 'tb1', 'fd20', 'tb2', 'fd21', 'sX01', 'sX11',
+    'fd00', 'tb3', 'fl2', 'fd01', 'st2', 'sX10', 'fd11', 'fo2', 'fl0', 'fd10',
+    'fu2', 'fo0', 'fl1', 'fi20', 'sY20', 'fi21', 'sY21', 'fu0', 'fo1', 'fi00',
+    'sY00', 'fi01', 'sY01', 'fu1', 'pw00', 'sD00', 'fi10', 'sY10', 'fi11', 'pw21',
+    'pw20', 'bd00', 'pw01', 'sY11', 'sD01', 'pw10', 'sD10', 'pw11', 'gw1', 'sD11',
+    'sD21', 'bd01', 'sD20', 'bd10', 'bl0', 'bd11', 'gw2', 'bd21', 'bl1', 'gw3',
+    'bd20', 'bo0', 'gw4', 'bl2', 'gw5', 'bu0', 'bo1', 'bo2', 'gw6', 'pj1',
+    'bi00', 'sN00', 'gs1', 'gs20', 'bi01', 'pj2', 'bu2', 'gs300', 'sN01', 'bu1',
+    'gs303', 'gs302', 'bi21', 'fn00', 'end', 'sN21', 'gs301', 'bi11', 'sN11', 'gs403',
+    'bi10', 'fn21', 'gs400', 'bi20', 'sN10', 'fn01', 'fn11', 'sN20', 'gs401', 'gs402',
+    'fn10', 'gs501', 'gs502', 'gs500', 'gs503', 'fn20',
 ))
 
 
 def block_kernel(sizes, total_points,
-                 x, tgt, leg_p, leg_q, spec_w, lat, w1, w2, f_tab, g_tab, ft_tab, gt_tab,
+                 x, tgt, leg_p_in, leg_q_in, spec_w, lat_in, w1_in, w2_in, f_in, g_in,
                  dx_out, gs_out, gin_out, gout_out, loss_out,
+                 leg_p, leg_q, lat, w1, w2, f_tab, g_tab, ft_tab, gt_tab,
                  xh, th, dout, pk, rows, yrow, hy,
                  xs, sr, dsr, ys, yr, dyr, als, ar, dar, bs, br, dbr, asave, dsave, aall, dall,
                  st_s, st_h, st_m, st_w, tab_s, tab_w, tab, down_p, down_q, up_p, up_q, ker,
                  gw, gw_z, gw_zs, gw_h, gw_hs, gw_w, gw_ws, gw_w2, gw_h2, gw_f,
                  ls, ls_z, ls_zs, ls_h, ls_hs, ls_w, gs_sum, gs_w,
                  sem_x, sem_y, sem_d, sem_n, sem_s, sem_ds, sem_u, sem_du, sem_a, sem_da, sem_b, sem_db, sem_az, sem_dz,
-                 sem_in, sem_o, sem_st, sem_tab, sem_k, sem_gw, sem_ls, sem_gs, sem_gf, sem_fin):
+                 sem_in, sem_o, sem_st, sem_tab, sem_k, sem_gw, sem_ls, sem_gs, sem_gf, sem_fin, sem_small):
     dp_size, h_size, w_size = sizes
     dp, h, w = lax.axis_index("dp"), lax.axis_index("h"), lax.axis_index("w")
     ndev = h_size * w_size
@@ -147,12 +149,13 @@
     loads = [pltpu.make_async_copy(x.at[b], xh.at[b], sem_in.at[b, 0]) for b in range(nb)]
     load_t = [pltpu.make_async_copy(tgt.at[b], th.at[b], sem_in.at[b, 1]) for b in range(nb)]
     load_k = pltpu.make_async_copy(spec_w.at[:, pl.ds(me * l_own, l_own)], ker, sem_k.at[0])
-    for c in loads + [load_k] + load_t:
+    small = [pltpu.make_async_copy(src, dst, sem_small.at[i]) for i, (src, dst) in enumerate((
+        (leg_p_in, leg_p), (leg_q_in, leg_q), (f_in, f_tab), (g_in, g_tab), (lat_in, lat), (w1_in, w1), (w2_in, w2)))]
+    for c in loads + small[:4] + [load_k] + load_t + small[4:]:
         c.start()
     coming["k"] = load_k.wait
+    coming["small"] = lambda: [c.wait() for c in small[4:]]
     coming.update({("t", b): load_t[b].wait for b in range(nb)})
-    tab_s[:, :, :nl] = leg_p[...]
-    tab_s[:, :, nl:] = leg_q[...]
     for ref in (ar, br, dar, dbr, st_s, gw, ls):
         ref[...] = jnp.zeros_like(ref)
 
@@ -175,24 +178,25 @@
         lax.fori_loop(1, size, body, 0)
         unsent.setdefault(key, []).append(lambda: drain(sent, sems.at[0]))
 
-    def holds(lin, h2):
-        return (lin + 1) * l_own > 8 * h2
-
-    def some(refs, sems, used, count, counts, key):
+    def some(refs, sems, low_h, high_h, count, counts, key):
         src, dst = refs(h, w)
         keep(src, dst, sems)
 
-        def body(k, _):
-            h2, w2_ = peer(k)
-
-            @pl.when(used(h2 * w_size + w2_, h2))
-            def _():
-                src, dst = refs(h2, w2_)
-                push(src, dst, sems, {"h": h2, "w": w2_})
+        def one(h2, k):
+            w2_ = (w + k) % w_size
+            src, dst = refs(h2, w2_)
+            push(src, dst, sems, {"h": h2, "w": w2_})
+
+        for k in range(1, w_size):
+            one(h, k)
+
+        def body(h2, _):
+            for k in range(w_size):
+                one(h2, k)
             return 0
 
-        lax.fori_loop(1, ndev, body, 0)
-        unsent.setdefault(key, []).append(lambda: take(sems.at[0], count - 1, [n - 1 for n in counts if n > 1]))
+        lax.fori_loop(low_h, high_h, body, 0)
+        unsent.setdefault(key, []).append(lambda: take(sems.at[0], count - 1, [n - 1 for n in counts]))
 
     def take(sem, count, counts):
         for n in counts:
@@ -200,10 +204,8 @@
             def _():
                 drain(als.at[0, pl.ds(0, n * piece)], sem)
 
-    n_orders = (((me + 1) * l_own + 7) // 8) * w_size
-    n_owners = ndev - (8 * h) // l_own
-    all_orders = [w_size * n for n in range(1, h_size + 1)]
-    all_owners = [ndev - (8 * g) // l_own for g in range(h_size)]
+    n_orders, n_owners = (h + 1) * w_size, (h_size - h) * w_size
+    counts = [w_size * n for n in range(1, h_size + 1)]
     pairs = lambda k: pl.ds(k * part, part)
 
     def at_rows(i, k):
@@ -232,13 +234,13 @@
 
     def send_owner(b, dst, sem, name):
         some(lambda h2, w2_: (als.at[b, rows_at(h2 * w_size + w2_, piece)], dst.at[b, h, :, lanes_at(w)]), sem.at[b],
-             lambda lin, h2: holds(lin, h), n_owners, all_owners, ("als", b))
-        coming[name, b] = lambda: take(sem.at[b, 1], n_orders, all_orders)
+             h + 1, h_size, n_owners, counts, ("als", b))
+        coming[name, b] = lambda: take(sem.at[b, 1], n_orders, counts)
 
     def send_back(b, dst, sem, name):
         some(lambda h2, w2_: (bs.at[b, h2, w2_], dst.at[b, rows_at(me, piece)]), sem.at[b],
-             lambda lin, h2: holds(me, h2), n_orders, all_orders, ("bs", b))
-        coming[name, b] = lambda: take(sem.at[b, 1], n_owners, all_owners)
+             0, h, n_orders, counts, ("bs", b))
+        coming[name, b] = lambda: take(sem.at[b, 1], n_owners, counts)
 
     def dft(b, k, table):
         settle(("xs", b, k))
@@ -308,6 +310,7 @@
         return weave_wide([hy[b, j, i] for j in range(w_size)])
 
     count = nt * npl
+    n_tab = tab_s.shape[0] // dp_size
 
     def combine(stats, n):
         mean = jnp.mean(stats, axis=0)
@@ -333,11 +336,17 @@
 
             st_s[2 * b:2 * b + 1, :] = mean
             st_s[2 * b + 1:2 * b + 2, :] = lax.fori_loop(0, nt, spread, jnp.zeros((1, nc), F32))
+        for c in small[:4]:
+            c.wait()
+        tab_s[:, :, :nl] = leg_p[...]
+        tab_s[:, :, nl:] = leg_q[...]
+        ft_tab[...] = f_tab[...].T
+        gt_tab[...] = g_tab[...].T
         pl.semaphore_wait(barrier, ndev - 1 + dp_size - 1)
         along("w", lambda o: (st_s, st_w.at[w]), sem_st.at[0], st_w.at[pl.ds(0, w_size - 1)], "st")
         coming["st"] = lambda: drain(st_w, sem_st.at[0, 1])
-        along("w", lambda o: (tab_s, tab_w.at[w]), sem_tab.at[0], tab_w.at[pl.ds(0, w_size - 1)])
-        coming["tab"] = lambda: drain(tab_w, sem_tab.at[0, 1])
+        along("w", lambda o: (tab_s.at[rows_at(dp, n_tab)], tab_w.at[w, rows_at(dp, n_tab)]), sem_tab.at[0], tab_w.at[pl.ds(0, w_size - 1), pl.ds(0, n_tab)])
+        coming["tab"] = lambda: drain(tab_w.at[:, pl.ds(0, n_tab)], sem_tab.at[0, 1])
 
     def st2():
         got("st")
@@ -356,8 +365,17 @@
             means.append(mean)
             scales.append(lax.rsqrt(m2 / (count * ndev) + NORM_EPS))
 
+    def tb1():
+        got("tab")
+        share = tab_w.at[:, rows_at(dp, n_tab)]
+        for k in range(1, dp_size):
+            push(share, share, sem_tab.at[2], {"dp": (dp + k) % dp_size})
+        others = tab_w.at[:, pl.ds(0, (dp_size - 1) * n_tab)]
+        unsent.setdefault(None, []).append(lambda: drain(others, sem_tab.at[2, 0]))
+        coming["tab1"] = lambda: drain(others, sem_tab.at[2, 1])
+
     def tb2():
-        got("tab")
+        got("tab1")
         along("h", lambda o: (tab_w.at[o // 2, rows_at(o % 2, 8)], tab.at[:, rows_at(h, nt)]), sem_tab.at[1], tab.at[:, pl.ds(0, nlat - nt)])
         coming["tab2"] = lambda: drain(tab, sem_tab.at[1, 1])
 
@@ -420,6 +438,8 @@
         got(("y", b, k))
         if ("t", b) in coming:
             got(("t", b))
+        if "small" in coming:
+            got("small")
         settle(("pk", b, k))
 
         def body(n, _):
@@ -589,44 +609,72 @@
                 gs_sum[q, p] = out[q * n_g:(q + 1) * n_g, p * LANES:(p + 1) * LANES]
 
     def gs2(q):
-        along("w", lambda o: (gs_sum.at[q], gs_w.at[q, w]), sem_gs.at[q], gs_w.at[q, pl.ds(0, w_size - 1)])
-        coming["gs", q] = lambda: drain(gs_w.at[q], sem_gs.at[q, 1])
+        keep(gs_sum.at[q], gs_w.at[q, 0], sem_gs.at[q, 0])
+        for k in (1, 3, 2):
+            push(gs_sum.at[q], gs_w.at[q, k], sem_gs.at[q, k], {"w": (w + k) % w_size})
+            unsent.setdefault(None, []).append(lambda k=k: drain(gs_w.at[q, k], sem_gs.at[q, k, 0]))
+        coming.update({("gs", q, k): lambda k=k: drain(gs_w.at[q, k], sem_gs.at[q, k, 1]) for k in range(w_size)})
 
     right, left = (dp + 1) % dp_size, (dp + dp_size - 1) % dp_size
-    block_at = lambda d, o, q: gs_out.at[:, l_own * o + d // 2, rows_at(q, n_g), lanes_at(d % 2)]
-
-    def gs3(q):
-        got(("gs", q))
-        for o in range(w_size):
-            pltpu.make_async_copy(gs_w.at[q, o], block_at(dp, o, q), sem_gf.at[q, 3, o, 0]).start()
-            push(gs_w.at[q, o], block_at(dp, o, q), sem_gf.at[q, 0, o], {"dp": right})
-            push(gs_w.at[q, o], block_at(dp, o, q), sem_gf.at[q, 1, o], {"dp": left})
-
-    def gs4(q):
-        for o in range(w_size):
-            way = 0 if o < w_size // 2 else 1
-            source, target = (left, right) if way == 0 else (right, left)
-            drain(gs_w.at[q, o], sem_gf.at[q, way, o, 1])
-            push(block_at(source, o, q), block_at(source, o, q), sem_gf.at[q, 2, o], {"dp": target})
-
-    def gs5(q):
-        for o in range(w_size):
-            drain(gs_w.at[q, o], sem_gf.at[q, 1 if o < w_size // 2 else 0, o, 1])
-            drain(gs_w.at[q, o], sem_gf.at[q, 2, o, 1])
-            for i in range(4):
-                drain(gs_w.at[q, o], sem_gf.at[q, i, o, 0])
+    block_at = lambda d, k, q: gs_out.at[:, l_own * ((w + w_size - k) % w_size) + d // 2, rows_at(q, n_g), lanes_at(d % 2)]
+
+    def gs3(q, k):
+        got(("gs", q, k))
+        pltpu.make_async_copy(gs_w.at[q, k], block_at(dp, k, q), sem_gf.at[q, 3, k, 0]).start()
+        push(gs_w.at[q, k], block_at(dp, k, q), sem_gf.at[q, 0, k], {"dp": right})
+        push(gs_w.at[q, k], block_at(dp, k, q), sem_gf.at[q, 1, k], {"dp": left})
+
+    def gs4(q, k):
+        way = 0 if k < w_size // 2 else 1
+        source, target = (left, right) if way == 0 else (right, left)
+        drain(gs_w.at[q, k], sem_gf.at[q, way, k, 1])
+        push(block_at(source, k, q), block_at(source, k, q), sem_gf.at[q, 2, k], {"dp": target})
+
+    def gs5(q, k):
+        drain(gs_w.at[q, k], sem_gf.at[q, 1 if k < w_size // 2 else 0, k, 1])
+        drain(gs_w.at[q, k], sem_gf.at[q, 2, k, 1])
+        for i in range(4):
+            drain(gs_w.at[q, k], sem_gf.at[q, i, k, 0])
 
     scope = dict(locals())
     for name in ORDER.split():
         call = name.rstrip("0123456789") or name
         if name in scope:
             scope[name]()
-        elif name[:2] == "gs" and len(name) == 4:
-            scope[name[:3]](int(name[3]))
+        elif name[:3] in scope:
+            scope[name[:3]](*map(int, name[3:]))
         else:
             scope[call](*map(int, name[len(call):]))
     assert not coming
     settle()
+
+
+def hand_on_kernel(*refs):
+    n = len(refs) // 3
+    srcs, dsts, bufs, sem = refs[:n], refs[n:2 * n], refs[2 * n:3 * n], refs[3 * n]
+    cuts = [(i, k) for i in range(n) for k in range(srcs[i].shape[0])]
+    reads = [pltpu.make_async_copy(srcs[i].at[k], bufs[i].at[k], sem.at[0, j]) for j, (i, k) in enumerate(cuts)]
+    writes = [pltpu.make_async_copy(bufs[i].at[k], dsts[i].at[k], sem.at[1, j]) for j, (i, k) in enumerate(cuts)]
+    for c in reads:
+        c.start()
+    for c, d in zip(reads, writes):
+        c.wait()
+        d.start()
+    for d in writes:
+        d.wait()
+
+
+def hand_on(arrays):
+    views = [a.reshape(v) for a, v in zip(arrays, ((6, -1, LANES * 2), (8, -1, LANES * 2), (1, *arrays[2].shape), (1, *arrays[3].shape)))]
+    any_spec = pl.BlockSpec(memory_space=pl.ANY)
+    out = pl.pallas_call(
+        hand_on_kernel, name="hand_on",
+        out_shape=[jax.ShapeDtypeStruct(v.shape, F32) for v in views],
+        in_specs=[any_spec] * len(views), out_specs=[any_spec] * len(views),
+        scratch_shapes=[pltpu.VMEM(v.shape, F32) for v in views] + [pltpu.SemaphoreType.DMA((2, sum(v.shape[0] for v in views)))],
+        compiler_params=pltpu.CompilerParams(vmem_limit_bytes=62 * 1024 * 1024),
+    )(*views)
+    return [o.reshape(a.shape) for o, a in zip(out, arrays)]
 
 
 def solution(mesh):
@@ -657,14 +705,16 @@
         degree = vm(nb, 8 * nl, LANES)
         owner = vm(nb, h_size, 8 * lo, w_size * LANES)
         saved = vm(nb, lo, 2 * nm, nc)
-        cuts = 2
-        d_x, g_spec, g_in, g_out, loss = pl.pallas_call(
+        cuts = 1
+        results = pl.pallas_call(
             functools.partial(block_kernel, (dp_size, h_size, w_size), total_points),
             name="block",
             out_shape=[sds(nb, nt, npl, nc), sds(2, lo * w_size, nc, nc), sds(nc, 2 * nc), sds(2 * nc, nc), sds(1, 1)],
-            in_specs=[any_spec] * 2 + [vmem_spec] * 2 + [any_spec] + [pl.BlockSpec(memory_space=pltpu.SMEM)] + [vmem_spec] * 6,
+            in_specs=[any_spec] * 10,
             out_specs=[any_spec] * 4 + [vmem_spec],
             scratch_shapes=[
+                vm(*leg_fwd.shape[:1], nt, nl), vm(*leg_fwd.shape[:1], nt, nl), pltpu.SMEM((nt,), F32), pltpu.VMEM(w_in.shape, BF16),
+                pltpu.VMEM(w_out.shape, BF16), vm(2 * nm, nlon), vm(2 * nm, nlon), vm(nlon, 2 * nm), vm(nlon, 2 * nm),
                 home, home, home, woven, vm(nb, ntp, nlon, LANES), woven, woven,
                 vm(nb, h_size, 16 * ntp, LANES), order, order, order, vm(nb, h_size, 16 * ntp, LANES), vm(nb, h_size, 16 * ntp, LANES),
                 degree, owner, owner, vm(nb, h_size, w_size, 8 * lo, LANES), degree, degree, saved, saved,
@@ -677,11 +727,13 @@
                 vm(n_h, nc), vm(n_z, nc), vm(n_rows, nc),
                 vm(8, nc), vm(dp_size, 8, nc), vm(8, nc), vm(h_size, 8, nc), vm(8, nc), vm(w_size, 8, nc),
                 vm(cuts, 2, nc // cuts, LANES), vm(cuts, w_size, 2, nc // cuts, LANES),
-            ] + [dma(nb, PARTS, 2)] * 8 + [dma(nb, 2)] * 6 + [dma(nb, 2), dma(nb, PARTS, 2), dma(4, 2), dma(2, 2), dma(1), dma(6, 2), dma(3, 2),
-                 dma(cuts, 2), dma(cuts, 4, w_size, 2), dma(3)],
+            ] + [dma(nb, PARTS, 2)] * 8 + [dma(nb, 2)] * 6 + [dma(nb, 2), dma(nb, PARTS, 2), dma(4, 2), dma(3, 2), dma(1), dma(6, 2), dma(3, 2),
+                 dma(cuts, w_size, 2), dma(cuts, 4, w_size, 2), dma(3), dma(7)],
             compiler_params=pltpu.CompilerParams(collective_id=0, has_side_effects=True, vmem_limit_bytes=62 * 1024 * 1024),
         )(field.transpose(0, 2, 3, 1), target.transpose(0, 2, 3, 1), leg_fwd.transpose(0, 2, 1), leg_inv.transpose(0, 2, 1),
-          spec_w, lat_weight, w_in, w_out, jnp.asarray(fwd_np), jnp.asarray(inv_np), jnp.asarray(fwd_np.T.copy()), jnp.asarray(inv_np.T.copy()))
+          spec_w, lat_weight, w_in, w_out, jnp.asarray(fwd_np), jnp.asarray(inv_np))
+        d_x, g_spec, g_in, g_out = hand_on(results[:4])
+        loss = results[4]
         return loss.reshape(()), d_x.transpose(0, 3, 1, 2), g_spec, g_in, g_out
 
     grid_spec = P("dp", None, "h", "w")

time: 225 us -> 218 us (0.969)
  local copies, waits for them, and re-layouts: 7.67 us -> 0 us
    unnamed x10 -> x0, local copies, waits for them, and re-layouts: 7.67 us -> none
    pallas_call x0 -> x1, Pallas kernels: none -> 6.57 us  [hand_on(): pl.pallas_call(hand_on_kernel, name='hand_on', out_shape=[jax.ShapeDtypeS...]
    pallas_call x1, Pallas kernels: 215 us -> 209 us  [local_step(): pl.pallas_call(functools.partial(block_kernel, (dp_size, h_size, w_size),...]
where the time goes in v8:
time: 218 us
  Pallas kernels  215 us (99%)
  between operations  2.35 us (1%)
    pallas_call x1, Pallas kernels, local_step(): pl.pallas_call(functools.partial(block_kernel, (dp_size, h_size, w_size),...  209 us
    pallas_call x1, Pallas kernels, hand_on(): pl.pallas_call(hand_on_kernel, name='hand_on', out_shape=[jax.ShapeDtypeS...  6.57 us

profile of v8, /device:TPU:1, one launch (start us, length us, event | category | flops | bytes accessed | tf_op | source)
XLA Modules:
  0.0 217.6 jit_solution(8228454815375873654)
XLA Ops:
  0.6 208.6 %block.1 = (f32[3,16,64,256]{3,2,1,0:T(8,128)}, f32[2,8,256,256]{3,2,1,0:T(8,128)}, f32[256,512]{1,0:T(8,128)}, f32[512,256]{1,0:T(8,128)}, f32[1,1]{1,0:T(1,128)}) custom-call(f32[3,16,64,256]{3,2,1,0:T(8,128)} %bitcast.17, f32[3,16,64,256]{3,2,1,0:T(8,128)} %bitcast.18, f32[16,16,64]{2,1,0:T(8,128)} %bitcast.21, f32[16,16,64]{2,1,0:T(8,128)} %bitcast.22, ...), custom_call_target="tpu_custom_call" | custom-call | tf_op jit(solution)/shard_map/block/pallas_call | solution.py:709
  209.3 6.6 %hand_on.1 = (f32[6,512,256]{2,1,0:T(8,128)}, f32[8,512,256]{2,1,0:T(8,128)}, f32[1,256,512]{2,1,0:T(8,128)}, f32[1,512,256]{2,1,0:T(8,128)}) custom-call(f32[6,512,256]{2,1,0:T(8,128)} %bitcast.16, f32[8,512,256]{2,1,0:T(8,128)} %bitcast.15, f32[1,256,512]{2,1,0:T(8,128)} %bitcast.19, f32[1,512,256]{2,1,0:T(8,128)} %bitcast.20), custom_call_target="tpu_custom_call" | custom-call | tf_op jit(solution)/shard_map/hand_on/pallas_call | solution.py:670

commit v9 on v8

--- a/solution.py
+++ b/solution.py
@@ -104,15 +104,15 @@
 
 def block_kernel(sizes, total_points,
                  x, tgt, leg_p_in, leg_q_in, spec_w, lat_in, w1_in, w2_in, f_in, g_in,
-                 dx_out, gs_out, gin_out, gout_out, loss_out,
+                 dout, gs_out, gin_out, gout_out, loss_out,
                  leg_p, leg_q, lat, w1, w2, f_tab, g_tab, ft_tab, gt_tab,
-                 xh, th, dout, pk, rows, yrow, hy,
+                 xh, th, pk, rows, yrow, hy,
                  xs, sr, dsr, ys, yr, dyr, als, ar, dar, bs, br, dbr, asave, dsave, aall, dall,
                  st_s, st_h, st_m, st_w, tab_s, tab_w, tab, down_p, down_q, up_p, up_q, ker,
                  gw, gw_z, gw_zs, gw_h, gw_hs, gw_w, gw_ws, gw_w2, gw_h2, gw_f,
                  ls, ls_z, ls_zs, ls_h, ls_hs, ls_w, gs_sum, gs_w,
                  sem_x, sem_y, sem_d, sem_n, sem_s, sem_ds, sem_u, sem_du, sem_a, sem_da, sem_b, sem_db, sem_az, sem_dz,
-                 sem_in, sem_o, sem_st, sem_tab, sem_k, sem_gw, sem_ls, sem_gs, sem_gf, sem_fin, sem_small):
+                 sem_in, sem_st, sem_tab, sem_k, sem_gw, sem_ls, sem_gs, sem_gf, sem_fin, sem_small):
     dp_size, h_size, w_size = sizes
     dp, h, w = lax.axis_index("dp"), lax.axis_index("h"), lax.axis_index("w")
     ndev = h_size * w_size
@@ -542,10 +542,6 @@
             return 0
 
         lax.fori_loop(k * part, (k + 1) * part, body, 0)
-        for j in range(2):
-            lats = pl.ds(j * ntp + k * part, part)
-            pltpu.make_async_copy(dout.at[b, lats], dx_out.at[b, lats], sem_o.at[b, k, j]).start()
-            unsent.setdefault(None, []).append(lambda lats=lats, j=j: drain(dx_out.at[b, lats], sem_o.at[b, k, j]))
 
     n_z, n_h, n_w = gw_zs.shape[0], gw_hs.shape[0], gw_ws.shape[0]
 
@@ -650,31 +646,22 @@
 
 
 def hand_on_kernel(*refs):
-    n = len(refs) // 3
-    srcs, dsts, bufs, sem = refs[:n], refs[n:2 * n], refs[2 * n:3 * n], refs[3 * n]
-    cuts = [(i, k) for i in range(n) for k in range(srcs[i].shape[0])]
-    reads = [pltpu.make_async_copy(srcs[i].at[k], bufs[i].at[k], sem.at[0, j]) for j, (i, k) in enumerate(cuts)]
-    writes = [pltpu.make_async_copy(bufs[i].at[k], dsts[i].at[k], sem.at[1, j]) for j, (i, k) in enumerate(cuts)]
-    for c in reads:
+    n = len(refs) // 2
+    copies = [pltpu.make_async_copy(refs[i], refs[n + i], refs[2 * n].at[i]) for i in range(n)]
+    for c in copies:
         c.start()
-    for c, d in zip(reads, writes):
+    for c in copies:
         c.wait()
-        d.start()
-    for d in writes:
-        d.wait()
 
 
 def hand_on(arrays):
-    views = [a.reshape(v) for a, v in zip(arrays, ((6, -1, LANES * 2), (8, -1, LANES * 2), (1, *arrays[2].shape), (1, *arrays[3].shape)))]
-    any_spec = pl.BlockSpec(memory_space=pl.ANY)
-    out = pl.pallas_call(
+    return pl.pallas_call(
         hand_on_kernel, name="hand_on",
-        out_shape=[jax.ShapeDtypeStruct(v.shape, F32) for v in views],
-        in_specs=[any_spec] * len(views), out_specs=[any_spec] * len(views),
-        scratch_shapes=[pltpu.VMEM(v.shape, F32) for v in views] + [pltpu.SemaphoreType.DMA((2, sum(v.shape[0] for v in views)))],
-        compiler_params=pltpu.CompilerParams(vmem_limit_bytes=62 * 1024 * 1024),
-    )(*views)
-    return [o.reshape(a.shape) for o, a in zip(out, arrays)]
+        out_shape=[jax.ShapeDtypeStruct(a.shape, F32) for a in arrays],
+        in_specs=[pl.BlockSpec(memory_space=pltpu.VMEM)] * len(arrays), out_specs=[pl.BlockSpec(memory_space=pl.ANY)] * len(arrays),
+        scratch_shapes=[pltpu.SemaphoreType.DMA((len(arrays),))],
+        compiler_params=pltpu.CompilerParams(vmem_limit_bytes=12 * 1024 * 1024),
+    )(*[pltpu.with_memory_space_constraint(a, pltpu.VMEM) for a in arrays])
 
 
 def solution(mesh):
@@ -709,13 +696,13 @@
         results = pl.pallas_call(
             functools.partial(block_kernel, (dp_size, h_size, w_size), total_points),
             name="block",
-            out_shape=[sds(nb, nt, npl, nc), sds(2, lo * w_size, nc, nc), sds(nc, 2 * nc), sds(2 * nc, nc), sds(1, 1)],
+            out_shape=[vm(nb, nt, npl, nc), vm(2, lo * w_size, nc, nc), vm(nc, 2 * nc), vm(2 * nc, nc), sds(1, 1)],
             in_specs=[any_spec] * 10,
-            out_specs=[any_spec] * 4 + [vmem_spec],
+            out_specs=[vmem_spec] * 5,
             scratch_shapes=[
                 vm(*leg_fwd.shape[:1], nt, nl), vm(*leg_fwd.shape[:1], nt, nl), pltpu.SMEM((nt,), F32), pltpu.VMEM(w_in.shape, BF16),
                 pltpu.VMEM(w_out.shape, BF16), vm(2 * nm, nlon), vm(2 * nm, nlon), vm(nlon, 2 * nm), vm(nlon, 2 * nm),
-                home, home, home, woven, vm(nb, ntp, nlon, LANES), woven, woven,
+                home, home, woven, vm(nb, ntp, nlon, LANES), woven, woven,
                 vm(nb, h_size, 16 * ntp, LANES), order, order, order, vm(nb, h_size, 16 * ntp, LANES), vm(nb, h_size, 16 * ntp, LANES),
                 degree, owner, owner, vm(nb, h_size, w_size, 8 * lo, LANES), degree, degree, saved, saved,
                 vm(dp_size, nb, 2 * nm, nc), vm(dp_size, nb, 2 * nm, LANES),
@@ -727,9 +714,9 @@
                 vm(n_h, nc), vm(n_z, nc), vm(n_rows, nc),
                 vm(8, nc), vm(dp_size, 8, nc), vm(8, nc), vm(h_size, 8, nc), vm(8, nc), vm(w_size, 8, nc),
                 vm(cuts, 2, nc // cuts, LANES), vm(cuts, w_size, 2, nc // cuts, LANES),
-            ] + [dma(nb, PARTS, 2)] * 8 + [dma(nb, 2)] * 6 + [dma(nb, 2), dma(nb, PARTS, 2), dma(4, 2), dma(3, 2), dma(1), dma(6, 2), dma(3, 2),
+            ] + [dma(nb, PARTS, 2)] * 8 + [dma(nb, 2)] * 6 + [dma(nb, 2), dma(4, 2), dma(3, 2), dma(1), dma(6, 2), dma(3, 2),
                  dma(cuts, w_size, 2), dma(cuts, 4, w_size, 2), dma(3), dma(7)],
-            compiler_params=pltpu.CompilerParams(collective_id=0, has_side_effects=True, vmem_limit_bytes=62 * 1024 * 1024),
+            compiler_params=pltpu.CompilerParams(collective_id=0, has_side_effects=True, vmem_limit_bytes=54 * 1024 * 1024),
         )(field.transpose(0, 2, 3, 1), target.transpose(0, 2, 3, 1), leg_fwd.transpose(0, 2, 1), leg_inv.transpose(0, 2, 1),
           spec_w, lat_weight, w_in, w_out, jnp.asarray(fwd_np), jnp.asarray(inv_np))
         d_x, g_spec, g_in, g_out = hand_on(results[:4])

time: 218 us -> 214 us (0.982)
  Pallas kernels: 215 us -> 211 us
    pallas_call x1, Pallas kernels: 6.57 us -> 3.4 us  [hand_on(): pl.pallas_call(hand_on_kernel, name='hand_on', out_shape=[jax.ShapeDtypeS...]
where the time goes in v9:
time: 214 us; the launch traced here: 213 us
  Pallas kernels  211 us (99%)
  between operations  2.41 us (1%)
    pallas_call x1, Pallas kernels, local_step(): pl.pallas_call(functools.partial(block_kernel, (dp_size, h_size, w_size),...  208 us

profile of v9, /device:TPU:1, one launch (start us, length us, event | category | flops | bytes accessed | tf_op | source)
XLA Modules:
  0.0 213.4 jit_solution(5553233044691588022)
XLA Ops:
  0.6 207.6 %block.1 = (f32[3,16,64,256]{3,2,1,0:T(8,128)S(1)}, f32[2,8,256,256]{3,2,1,0:T(8,128)S(1)}, f32[256,512]{1,0:T(8,128)S(1)}, f32[512,256]{1,0:T(8,128)S(1)}, f32[1,1]{1,0:T(1,128)}) custom-call(f32[3,16,64,256]{3,2,1,0:T(8,128)} %bitcast.6, f32[3,16,64,256]{3,2,1,0:T(8,128)} %bitcast.7, f32[16,16,64]{2,1,0:T(8,128)} %bitcast.8, f32[16,16,64]{2,1,0:T(8,128)} %bitcast.9, ...), custom_call_target="tpu_custom_call" | custom-call | tf_op jit(solution)/shard_map/block/pallas_call | solution.py:696
  208.2 3.4 %hand_on.1 = (f32[3,16,64,256]{3,2,1,0:T(8,128)}, f32[2,8,256,256]{3,2,1,0:T(8,128)}, f32[256,512]{1,0:T(8,128)}, f32[512,256]{1,0:T(8,128)}) custom-call(f32[3,16,64,256]{3,2,1,0:T(8,128)S(1)} %get-tuple-element.15.refs_0_, f32[2,8,256,256]{3,2,1,0:T(8,128)S(1)} %get-tuple-element.16.refs_1_, f32[256,512]{1,0:T(8,128)S(1)} %get-tuple-element.17.refs_2_, ...), custom_call_target="tpu_custom_call" | custom-call | tf_op jit(solution)/shard_map/hand_on/pallas_call | solution.py:658

commit v10 on v9

--- a/solution.py
+++ b/solution.py
@@ -87,18 +87,22 @@
 
 
 PARTS = 2
+GS_ROWS = 176
+GS_FIRST = (0, 1, 2)
 ORDER = " ".join((
-    'go', 'sX20', 'sX21', 'sX00', 'tb1', 'fd20', 'tb2', 'fd21', 'sX01', 'sX11',
-    'fd00', 'tb3', 'fl2', 'fd01', 'st2', 'sX10', 'fd11', 'fo2', 'fl0', 'fd10',
-    'fu2', 'fo0', 'fl1', 'fi20', 'sY20', 'fi21', 'sY21', 'fu0', 'fo1', 'fi00',
-    'sY00', 'fi01', 'sY01', 'fu1', 'pw00', 'sD00', 'fi10', 'sY10', 'fi11', 'pw21',
-    'pw20', 'bd00', 'pw01', 'sY11', 'sD01', 'pw10', 'sD10', 'pw11', 'gw1', 'sD11',
-    'sD21', 'bd01', 'sD20', 'bd10', 'bl0', 'bd11', 'gw2', 'bd21', 'bl1', 'gw3',
-    'bd20', 'bo0', 'gw4', 'bl2', 'gw5', 'bu0', 'bo1', 'bo2', 'gw6', 'pj1',
-    'bi00', 'sN00', 'gs1', 'gs20', 'bi01', 'pj2', 'bu2', 'gs300', 'sN01', 'bu1',
-    'gs303', 'gs302', 'bi21', 'fn00', 'end', 'sN21', 'gs301', 'bi11', 'sN11', 'gs403',
-    'bi10', 'fn21', 'gs400', 'bi20', 'sN10', 'fn01', 'fn11', 'sN20', 'gs401', 'gs402',
-    'fn10', 'gs501', 'gs502', 'gs500', 'gs503', 'fn20',
+    'go', 'sX01', 'sX00', 'sX10', 'sX11', 'tb1', 'fd01', 'tb2', 'fd00', 'tb3',
+    'tb4', 'st2', 'fl0', 'fd10', 'sX21', 'fd11', 'fo0', 'fl1', 'tb5', 'sX20',
+    'fu0', 'fo1', 'fd21', 'fi00', 'sY00', 'fi01', 'sY01', 'fd20', 'pw00', 'sD00',
+    'fu1', 'fl2', 'pw01', 'fi10', 'sY10', 'bd00', 'fi11', 'sD01', 'fo2', 'pw10',
+    'sY11', 'bd01', 'sD10', 'fu2', 'pw11', 'sD11', 'bl0', 'fi21', 'sY21', 'fi20',
+    'bd10', 'bo0', 'sY20', 'bd11', 'pw21', 'sD21', 'bu0', 'pw20', 'sD20', 'bl1',
+    'bd21', 'gw1', 'gsa', 'bi00', 'bi01', 'gw2', 'sN01', 'bd20', 'bo1', 'gw3',
+    'bl2', 'sN00', 'bu1', 'bo2', 'pj1', 'gw4', 'bi10', 'sN10', 'gsb', 'gw5',
+    'gs1', 'gs20', 'gs21', 'gs310', 'gs300', 'bi11', 'gw6', 'gs61', 'sN11', 'gs303',
+    'gw7', 'gs311', 'gs301', 'bu2', 'gs313', 'gs60', 'gs411', 'gs400', 'gs312', 'bi20',
+    'gw8', 'pj2', 'gs403', 'bi21', 'sN21', 'fn00', 'gs413', 'gs302', 'gs500', 'gs410',
+    'sN20', 'gs401', 'gs511', 'fn10', 'end', 'gs510', 'gs412', 'gs402', 'gs502', 'fn11',
+    'gs501', 'gs513', 'fn01', 'fn20', 'fn21', 'gs503', 'gs512',
 ))
 
 
@@ -109,8 +113,8 @@
                  xh, th, pk, rows, yrow, hy,
                  xs, sr, dsr, ys, yr, dyr, als, ar, dar, bs, br, dbr, asave, dsave, aall, dall,
                  st_s, st_h, st_m, st_w, tab_s, tab_w, tab, down_p, down_q, up_p, up_q, ker,
-                 gw, gw_z, gw_zs, gw_h, gw_hs, gw_w, gw_ws, gw_w2, gw_h2, gw_f,
-                 ls, ls_z, ls_zs, ls_h, ls_hs, ls_w, gs_sum, gs_w,
+                 gw, gw_p, gw_a, gw_z, gw_zs, gw_h, gw_hs, gw_w, gw_ws, gw_w2, gw_h2, gw_f, gw_o,
+                 ls, ls_p, ls_a, ls_z, ls_zs, ls_h, ls_hs, ls_w, gs_acc, gs_sum0, gs_sum1, gs_b0, gs_b1,
                  sem_x, sem_y, sem_d, sem_n, sem_s, sem_ds, sem_u, sem_du, sem_a, sem_da, sem_b, sem_db, sem_az, sem_dz,
                  sem_in, sem_st, sem_tab, sem_k, sem_gw, sem_ls, sem_gs, sem_gf, sem_fin, sem_small):
     dp_size, h_size, w_size = sizes
@@ -310,7 +314,7 @@
         return weave_wide([hy[b, j, i] for j in range(w_size)])
 
     count = nt * npl
-    n_tab = tab_s.shape[0] // dp_size
+    n_tab = tab_s.shape[1] // dp_size
 
     def combine(stats, n):
         mean = jnp.mean(stats, axis=0)
@@ -338,15 +342,17 @@
             st_s[2 * b + 1:2 * b + 2, :] = lax.fori_loop(0, nt, spread, jnp.zeros((1, nc), F32))
         for c in small[:4]:
             c.wait()
-        tab_s[:, :, :nl] = leg_p[...]
-        tab_s[:, :, nl:] = leg_q[...]
+        for a, leg in enumerate((leg_p, leg_q)):
+            for m in range(leg.shape[0]):
+                tab_s[a, m // 2, :, m % 2 * nl:(m % 2 + 1) * nl] = leg[m]
         ft_tab[...] = f_tab[...].T
         gt_tab[...] = g_tab[...].T
         pl.semaphore_wait(barrier, ndev - 1 + dp_size - 1)
         along("w", lambda o: (st_s, st_w.at[w]), sem_st.at[0], st_w.at[pl.ds(0, w_size - 1)], "st")
         coming["st"] = lambda: drain(st_w, sem_st.at[0, 1])
-        along("w", lambda o: (tab_s.at[rows_at(dp, n_tab)], tab_w.at[w, rows_at(dp, n_tab)]), sem_tab.at[0], tab_w.at[pl.ds(0, w_size - 1), pl.ds(0, n_tab)])
-        coming["tab"] = lambda: drain(tab_w.at[:, pl.ds(0, n_tab)], sem_tab.at[0, 1])
+        along("w", lambda o: (tab_s.at[:, rows_at(dp, n_tab)], tab_w.at[:, w, rows_at(dp, n_tab)]), sem_tab.at[0],
+              tab_w.at[:, pl.ds(0, w_size - 1), pl.ds(0, n_tab)])
+        coming["tab"] = lambda: drain(tab_w.at[:, :, pl.ds(0, n_tab)], sem_tab.at[0, 1])
 
     def st2():
         got("st")
@@ -367,29 +373,40 @@
 
     def tb1():
         got("tab")
-        share = tab_w.at[:, rows_at(dp, n_tab)]
-        for k in range(1, dp_size):
-            push(share, share, sem_tab.at[2], {"dp": (dp + k) % dp_size})
-        others = tab_w.at[:, pl.ds(0, (dp_size - 1) * n_tab)]
-        unsent.setdefault(None, []).append(lambda: drain(others, sem_tab.at[2, 0]))
-        coming["tab1"] = lambda: drain(others, sem_tab.at[2, 1])
+        for a in range(2):
+            share = tab_w.at[a, :, rows_at(dp, n_tab)]
+            for k in range(1, dp_size):
+                push(share, share, sem_tab.at[1 + a], {"dp": (dp + k) % dp_size})
+            others = tab_w.at[a, :, pl.ds(0, (dp_size - 1) * n_tab)]
+            unsent.setdefault(None, []).append(lambda a=a, others=others: drain(others, sem_tab.at[1 + a, 0]))
+            coming["tab1", a] = lambda a=a, others=others: drain(others, sem_tab.at[1 + a, 1])
+
+    def table_out(a):
+        got(("tab1", a))
+        along("h", lambda o: (tab_w.at[a, o // 2, rows_at(o % 2, 4)], tab.at[a, :, rows_at(h, nt)]), sem_tab.at[3 + a],
+              tab.at[a, :, pl.ds(0, nlat - nt)])
+        coming["tab2", a] = lambda: drain(tab.at[a], sem_tab.at[3 + a, 1])
+
+    def table_in(a, down, up):
+        got(("tab2", a))
+        for m in range(8):
+            both = tab[a, m // 2].reshape(h_size, 2, ntp, 2 * nl)
+            for j in range(2):
+                t = both[:, j].reshape(-1, 2 * nl)[:, m % 2 * nl:(m % 2 + 1) * nl]
+                up[m, j * (nlat // 2):(j + 1) * (nlat // 2), :] = t
+                down[m, j * nl:(j + 1) * nl, :] = t.T
 
     def tb2():
-        got("tab1")
-        along("h", lambda o: (tab_w.at[o // 2, rows_at(o % 2, 8)], tab.at[:, rows_at(h, nt)]), sem_tab.at[1], tab.at[:, pl.ds(0, nlat - nt)])
-        coming["tab2"] = lambda: drain(tab, sem_tab.at[1, 1])
+        table_out(0)
 
     def tb3():
-        got("tab2")
-        for m in range(8):
-            both = tab[m].reshape(h_size, 2, ntp, 2 * nl)
-            t0, t1 = both[:, 0].reshape(-1, 2 * nl), both[:, 1].reshape(-1, 2 * nl)
-            for k, (down, up) in enumerate(((down_p, up_p), (down_q, up_q))):
-                a, z = t0[:, k * nl:(k + 1) * nl], t1[:, k * nl:(k + 1) * nl]
-                up[m, :nlat // 2, :] = a
-                up[m, nlat // 2:, :] = z
-                down[m, :nl, :] = a.T
-                down[m, nl:, :] = z.T
+        table_in(0, down_p, up_p)
+
+    def tb4():
+        table_out(1)
+
+    def tb5():
+        table_in(1, down_q, up_q)
 
     def sX(b, k):
         send_home_rows(b, k, sem_x, "x")
@@ -543,94 +560,157 @@
 
         lax.fori_loop(k * part, (k + 1) * part, body, 0)
 
-    n_z, n_h, n_w = gw_zs.shape[0], gw_hs.shape[0], gw_ws.shape[0]
+    n_c, n_z, n_h, n_w = gw_a.shape[0], gw_zs.shape[0], gw_hs.shape[0], gw_ws.shape[0]
+    chip, core = h // 2, h % 2
+    chips = h_size // 2
+
+    def over_chips(refs, sems, sent):
+        src, dst = refs(chip)
+        keep(src, dst, sems)
+        for k in range(1, chips):
+            o = (chip + k) % chips
+            src, dst = refs(o)
+            push(src, dst, sems, {"h": 2 * o + core})
+        unsent.setdefault(None, []).append(lambda: drain(sent, sems.at[0]))
+
+    def twin(src, dst, sems):
+        push(src, dst, sems, {"h": h + 1 - 2 * core})
+        unsent.setdefault(None, []).append(lambda: drain(dst, sems.at[0]))
 
     def gw1():
-        along("dp", lambda o: (gw.at[rows_at(o, n_z)], gw_z.at[dp]), sem_gw.at[0], gw_z.at[pl.ds(0, dp_size - 1)])
-        along("dp", lambda o: (ls, ls_z.at[dp]), sem_ls.at[0], ls_z.at[pl.ds(0, dp_size - 1)])
-        coming["gw1"] = lambda: (drain(gw_z, sem_gw.at[0, 1]), drain(ls_z, sem_ls.at[0, 1]))
+        twin(gw.at[rows_at(1 - core, n_c)], gw_p, sem_gw.at[0])
+        twin(ls, ls_p, sem_ls.at[0])
+        coming["gw1"] = lambda: (drain(gw_p, sem_gw.at[0, 1]), drain(ls_p, sem_ls.at[0, 1]))
 
     def gw2():
         got("gw1")
+        gw_a[...] = gw[rows_at(core, n_c), :] + gw_p[...]
+        ls_a[...] = ls[...] + ls_p[...]
+        along("dp", lambda o: (gw_a.at[rows_at(o, n_z)], gw_z.at[dp]), sem_gw.at[1], gw_z.at[pl.ds(0, dp_size - 1)])
+        along("dp", lambda o: (ls_a, ls_z.at[dp]), sem_ls.at[1], ls_z.at[pl.ds(0, dp_size - 1)])
+        coming["gw2"] = lambda: (drain(gw_z, sem_gw.at[1, 1]), drain(ls_z, sem_ls.at[1, 1]))
+
+    def gw3():
+        got("gw2")
         gw_zs[...] = jnp.sum(gw_z[...], axis=0)
         ls_zs[...] = jnp.sum(ls_z[...], axis=0)
-        along("h", lambda o: (gw_zs.at[rows_at(o, n_h)], gw_h.at[h]), sem_gw.at[1], gw_h.at[pl.ds(0, h_size - 1)])
-        along("h", lambda o: (ls_zs, ls_h.at[h]), sem_ls.at[1], ls_h.at[pl.ds(0, h_size - 1)])
-        coming["gw2"] = lambda: (drain(gw_h, sem_gw.at[1, 1]), drain(ls_h, sem_ls.at[1, 1]))
-
-    def gw3():
-        got("gw2")
+        over_chips(lambda o: (gw_zs.at[rows_at(o, n_h)], gw_h.at[chip]), sem_gw.at[2], gw_h.at[pl.ds(0, chips - 1)])
+        over_chips(lambda o: (ls_zs, ls_h.at[chip]), sem_ls.at[2], ls_h.at[pl.ds(0, chips - 1)])
+        coming["gw3"] = lambda: (drain(gw_h, sem_gw.at[2, 1]), drain(ls_h, sem_ls.at[2, 1]))
+
+    def gw4():
+        got("gw3")
         gw_hs[...] = jnp.sum(gw_h[...], axis=0)
         ls_hs[...] = jnp.sum(ls_h[...], axis=0)
-        along("w", lambda o: (gw_hs.at[rows_at(o, n_w)], gw_w.at[w]), sem_gw.at[2], gw_w.at[pl.ds(0, w_size - 1)])
-        along("w", lambda o: (ls_hs, ls_w.at[w]), sem_ls.at[2], ls_w.at[pl.ds(0, w_size - 1)])
-        coming["gw3"] = lambda: (drain(gw_w, sem_gw.at[2, 1]), drain(ls_w, sem_ls.at[2, 1]))
-
-    def gw4():
-        got("gw3")
+        along("w", lambda o: (gw_hs.at[rows_at(o, n_w)], gw_w.at[w]), sem_gw.at[3], gw_w.at[pl.ds(0, w_size - 1)])
+        along("w", lambda o: (ls_hs, ls_w.at[w]), sem_ls.at[3], ls_w.at[pl.ds(0, w_size - 1)])
+        coming["gw4"] = lambda: (drain(gw_w, sem_gw.at[3, 1]), drain(ls_w, sem_ls.at[3, 1]))
+
+    def gw5():
+        got("gw4")
         gw_ws[...] = jnp.sum(gw_w[...], axis=0)
         loss_out[...] = jnp.sum(ls_w[...], keepdims=True).reshape(1, 1) / total_points
-        along("w", lambda o: (gw_ws, gw_w2.at[rows_at(w, n_w)]), sem_gw.at[3], gw_w2.at[pl.ds(0, (w_size - 1) * n_w)])
-        coming["gw4"] = lambda: drain(gw_w2, sem_gw.at[3, 1])
-
-    def gw5():
-        got("gw4")
-        along("h", lambda o: (gw_w2, gw_h2.at[rows_at(h, n_h)]), sem_gw.at[4], gw_h2.at[pl.ds(0, (h_size - 1) * n_h)])
-        coming["gw5"] = lambda: drain(gw_h2, sem_gw.at[4, 1])
+        along("w", lambda o: (gw_ws, gw_w2.at[rows_at(w, n_w)]), sem_gw.at[4], gw_w2.at[pl.ds(0, (w_size - 1) * n_w)])
+        coming["gw5"] = lambda: drain(gw_w2, sem_gw.at[4, 1])
 
     def gw6():
         got("gw5")
-        along("dp", lambda o: (gw_h2, gw_f.at[rows_at(dp, n_z)]), sem_gw.at[5], gw_f.at[pl.ds(0, (dp_size - 1) * n_z)])
-        coming["gw6"] = lambda: drain(gw_f, sem_gw.at[5, 1])
+        over_chips(lambda o: (gw_w2, gw_h2.at[rows_at(chip, n_h)]), sem_gw.at[5], gw_h2.at[pl.ds(0, (chips - 1) * n_h)])
+        coming["gw6"] = lambda: drain(gw_h2, sem_gw.at[5, 1])
+
+    def gw7():
+        got("gw6")
+        along("dp", lambda o: (gw_h2, gw_f.at[rows_at(dp, n_z)]), sem_gw.at[6], gw_f.at[pl.ds(0, (dp_size - 1) * n_z)])
+        coming["gw7"] = lambda: drain(gw_f, sem_gw.at[6, 1])
+
+    def gw8():
+        got("gw7")
+        twin(gw_f, gw_o, sem_gw.at[7])
+        coming["gw8"] = lambda: drain(gw_o, sem_gw.at[7, 1])
 
     def end():
-        got("gw6")
-        outs = [(gw_f.at[:nc], gin_out.at[:, :nc]), (gw_f.at[nc:2 * nc], gin_out.at[:, nc:]), (gw_f.at[2 * nc:], gout_out)]
-        for i, (src, dst) in enumerate(outs):
-            pltpu.make_async_copy(src, dst, sem_fin.at[i]).start()
+        got("gw8")
+        for c, halves in enumerate(((gw_f, gw_o), (gw_o, gw_f))):
+            @pl.when(core == c)
+            def _():
+                first, second = halves
+                for i, (src, dst) in enumerate(((first.at[:nc], gin_out.at[:, :nc]), (first.at[nc:], gin_out.at[:, nc:]), (second, gout_out))):
+                    pltpu.make_async_copy(src, dst, sem_fin.at[i]).start()
+        for i, dst in enumerate((gin_out.at[:, :nc], gin_out.at[:, nc:], gout_out)):
             unsent.setdefault(None, []).append(lambda dst=dst, i=i: drain(dst, sem_fin.at[i]))
 
-    cuts, _, n_g, _ = gs_sum.shape
-
-    def gs1():
-        for b in range(nb):
-            got(("az", b))
-            got(("dz", b))
-        d = dall[...].reshape(dp_size * nb, 2, -1, LANES)
+    gs_sum, gs_b = (gs_sum0, gs_sum1), (gs_b0, gs_b1)
+    first_rows = (0, gs_sum0.shape[1])
+    axes = (("w", "dp"), ("dp", "w"))
+    place = {"w": (w, w_size), "dp": (dp, dp_size)}
+
+    def next_to(axis, k):
+        index, size = place[axis]
+        return (index + k + size) % size
+
+    def sample_grad(b):
+        got(("az", b))
+        got(("dz", b))
+        d = dall[:, b].reshape(dp_size, 2, -1, LANES)
         turned = jnp.concatenate([d[:, 1:], -d[:, :1]], axis=1)
         both = jnp.concatenate([d.reshape(-1, LANES), turned.reshape(-1, LANES)], axis=1)
-        out = dot(aall[...].reshape(-1, nc), both, TN)
-        for q in range(cuts):
+        return dot(aall[:, b].reshape(-1, nc), both, TN)
+
+    def gsa():
+        gs_acc[...] = sample_grad(GS_FIRST[0])
+
+    def gsb():
+        gs_acc[...] += sample_grad(GS_FIRST[1])
+
+    def gs1():
+        out = gs_acc[...] + sample_grad(GS_FIRST[2])
+        for q in range(2):
             for p in range(2):
-                gs_sum[q, p] = out[q * n_g:(q + 1) * n_g, p * LANES:(p + 1) * LANES]
+                gs_sum[q][p] = out[first_rows[q]:first_rows[q] + gs_sum[q].shape[1], p * LANES:(p + 1) * LANES]
+
+    def once(key):
+        if key in coming:
+            got(key)
+
+    def sent_later(ref, sem):
+        unsent.setdefault(None, []).append(lambda: drain(ref, sem))
 
     def gs2(q):
-        keep(gs_sum.at[q], gs_w.at[q, 0], sem_gs.at[q, 0])
-        for k in (1, 3, 2):
-            push(gs_sum.at[q], gs_w.at[q, k], sem_gs.at[q, k], {"w": (w + k) % w_size})
-            unsent.setdefault(None, []).append(lambda k=k: drain(gs_w.at[q, k], sem_gs.at[q, k, 0]))
-        coming.update({("gs", q, k): lambda k=k: drain(gs_w.at[q, k], sem_gs.at[q, k, 1]) for k in range(w_size)})
-
-    right, left = (dp + 1) % dp_size, (dp + dp_size - 1) % dp_size
-    block_at = lambda d, k, q: gs_out.at[:, l_own * ((w + w_size - k) % w_size) + d // 2, rows_at(q, n_g), lanes_at(d % 2)]
+        keep(gs_sum[q], gs_b[q].at[0], sem_gs.at[q, 0])
+        for slot, k in ((1, 1), (3, -1)):
+            push(gs_sum[q], gs_b[q].at[slot], sem_gs.at[q, slot], {axes[q][0]: next_to(axes[q][0], k)})
+            sent_later(gs_sum[q], sem_gs.at[q, slot, 0])
+        coming.update({("gs", q, k): lambda k=k: drain(gs_b[q].at[k], sem_gs.at[q, k, 1]) for k in (0, 1, 3)})
+
+    def gs6(q):
+        for slot, p, k, i in ((1, 0, 1, 2), (3, 1, -1, 4)):
+            once(("gs", q, slot))
+            push(gs_b[q].at[slot, p], gs_b[q].at[2, p], sem_gs.at[q, i], {axes[q][0]: next_to(axes[q][0], k)})
+            sent_later(gs_b[q].at[2, p], sem_gs.at[q, i, 0])
+        coming["gs", q, 2] = lambda: (drain(gs_b[q].at[2, 0], sem_gs.at[q, 2, 1]), drain(gs_b[q].at[2, 1], sem_gs.at[q, 4, 1]))
+
+    def block_at(q, k, shift):
+        at = {axes[q][0]: next_to(axes[q][0], -k), axes[q][1]: next_to(axes[q][1], shift)}
+        return gs_out.at[:, l_own * at["w"] + at["dp"] // 2, pl.ds(first_rows[q], gs_sum[q].shape[1]), lanes_at(at["dp"] % 2)]
 
     def gs3(q, k):
-        got(("gs", q, k))
-        pltpu.make_async_copy(gs_w.at[q, k], block_at(dp, k, q), sem_gf.at[q, 3, k, 0]).start()
-        push(gs_w.at[q, k], block_at(dp, k, q), sem_gf.at[q, 0, k], {"dp": right})
-        push(gs_w.at[q, k], block_at(dp, k, q), sem_gf.at[q, 1, k], {"dp": left})
+        once(("gs", q, k))
+        mine = block_at(q, k, 0)
+        pltpu.make_async_copy(gs_b[q].at[k], mine, sem_gf.at[q, 3, k, 0]).start()
+        for way, shift in ((0, 1), (1, -1)):
+            push(gs_b[q].at[k], mine, sem_gf.at[q, way, k], {axes[q][1]: next_to(axes[q][1], shift)})
 
     def gs4(q, k):
-        way = 0 if k < w_size // 2 else 1
-        source, target = (left, right) if way == 0 else (right, left)
-        drain(gs_w.at[q, k], sem_gf.at[q, way, k, 1])
-        push(block_at(source, k, q), block_at(source, k, q), sem_gf.at[q, 2, k], {"dp": target})
+        way, shift = (0, 1) if k < 2 else (1, -1)
+        drain(gs_b[q].at[k], sem_gf.at[q, way, k, 1])
+        block = block_at(q, k, -shift)
+        push(block, block, sem_gf.at[q, 2, k], {axes[q][1]: next_to(axes[q][1], shift)})
 
     def gs5(q, k):
-        drain(gs_w.at[q, k], sem_gf.at[q, 1 if k < w_size // 2 else 0, k, 1])
-        drain(gs_w.at[q, k], sem_gf.at[q, 2, k, 1])
+        drain(gs_b[q].at[k], sem_gf.at[q, 1 if k < 2 else 0, k, 1])
+        drain(gs_b[q].at[k], sem_gf.at[q, 2, k, 1])
         for i in range(4):
-            drain(gs_w.at[q, k], sem_gf.at[q, i, k, 0])
+            drain(gs_b[q].at[k], sem_gf.at[q, i, k, 0])
 
     scope = dict(locals())
     for name in ORDER.split():
@@ -692,7 +772,10 @@
         degree = vm(nb, 8 * nl, LANES)
         owner = vm(nb, h_size, 8 * lo, w_size * LANES)
         saved = vm(nb, lo, 2 * nm, nc)
-        cuts = 1
+        cut = GS_ROWS
+        n_pairs = leg_fwd.shape[0] // 2
+        n_c = n_rows // 2
+        n_z, n_h, n_w = n_c // dp_size, n_c // dp_size // w_size, n_c // dp_size // w_size // w_size
         results = pl.pallas_call(
             functools.partial(block_kernel, (dp_size, h_size, w_size), total_points),
             name="block",
@@ -707,15 +790,15 @@
                 degree, owner, owner, vm(nb, h_size, w_size, 8 * lo, LANES), degree, degree, saved, saved,
                 vm(dp_size, nb, 2 * nm, nc), vm(dp_size, nb, 2 * nm, LANES),
                 vm(8, nc), vm(h_size, 8, nc), vm(8, nc), vm(w_size, 8, nc),
-                vm(leg_fwd.shape[0], nt, 2 * nl), vm(w_size, leg_fwd.shape[0], nt, 2 * nl), vm(8, nlat, 2 * nl),
+                vm(2, n_pairs, nt, 2 * nl), vm(2, w_size, n_pairs, nt, 2 * nl), vm(2, 4, nlat, 2 * nl),
                 vm(8, 2 * nl, nlat // 2), vm(8, 2 * nl, nlat // 2), vm(8, nlat, nl), vm(8, nlat, nl),
                 vm(2, lo, nc, nc),
-                vm(n_rows, nc), vm(dp_size, n_z, nc), vm(n_z, nc), vm(h_size, n_h, nc), vm(n_h, nc), vm(w_size, n_w, nc), vm(n_w, nc),
-                vm(n_h, nc), vm(n_z, nc), vm(n_rows, nc),
-                vm(8, nc), vm(dp_size, 8, nc), vm(8, nc), vm(h_size, 8, nc), vm(8, nc), vm(w_size, 8, nc),
-                vm(cuts, 2, nc // cuts, LANES), vm(cuts, w_size, 2, nc // cuts, LANES),
-            ] + [dma(nb, PARTS, 2)] * 8 + [dma(nb, 2)] * 6 + [dma(nb, 2), dma(4, 2), dma(3, 2), dma(1), dma(6, 2), dma(3, 2),
-                 dma(cuts, w_size, 2), dma(cuts, 4, w_size, 2), dma(3), dma(7)],
+                vm(n_rows, nc), vm(n_c, nc), vm(n_c, nc), vm(dp_size, n_z, nc), vm(n_z, nc), vm(w_size, n_h, nc), vm(n_h, nc),
+                vm(w_size, n_w, nc), vm(n_w, nc), vm(n_h, nc), vm(n_z, nc), vm(n_c, nc), vm(n_c, nc),
+                vm(8, nc), vm(8, nc), vm(8, nc), vm(dp_size, 8, nc), vm(8, nc), vm(w_size, 8, nc), vm(8, nc), vm(w_size, 8, nc),
+                vm(nc, nc), vm(2, cut, LANES), vm(2, nc - cut, LANES), vm(4, 2, cut, LANES), vm(4, 2, nc - cut, LANES),
+            ] + [dma(nb, PARTS, 2)] * 8 + [dma(nb, 2)] * 6 + [dma(nb, 2), dma(4, 2), dma(5, 2), dma(1), dma(8, 2), dma(4, 2),
+                 dma(2, 5, 2), dma(2, 4, 4, 2), dma(3), dma(7)],
             compiler_params=pltpu.CompilerParams(collective_id=0, has_side_effects=True, vmem_limit_bytes=54 * 1024 * 1024),
         )(field.transpose(0, 2, 3, 1), target.transpose(0, 2, 3, 1), leg_fwd.transpose(0, 2, 1), leg_inv.transpose(0, 2, 1),
           spec_w, lat_weight, w_in, w_out, jnp.asarray(fwd_np), jnp.asarray(inv_np))

time: 214 us -> 209 us (0.977)
  Pallas kernels: 211 us -> 205 us
    pallas_call x1, Pallas kernels: 208 us -> 201 us  [local_step(): pl.pallas_call(functools.partial(block_kernel, (dp_size, h_size, w_size),...]
where the time goes in v10:
time: 209 us; the launch traced here: 207 us
  Pallas kernels  205 us (98%)
  between operations  2.41 us (1%)
    pallas_call x1, Pallas kernels, local_step(): pl.pallas_call(functools.partial(block_kernel, (dp_size, h_size, w_size),...  201 us

profile of v10, /device:TPU:1, one launch (start us, length us, event | category | flops | bytes accessed | tf_op | source)
XLA Modules:
  0.0 207.0 jit_solution(14933803148972540864)
XLA Ops:
  0.6 201.2 %block.1 = (f32[3,16,64,256]{3,2,1,0:T(8,128)S(1)}, f32[2,8,256,256]{3,2,1,0:T(8,128)S(1)}, f32[256,512]{1,0:T(8,128)S(1)}, f32[512,256]{1,0:T(8,128)S(1)}, f32[1,1]{1,0:T(1,128)}) custom-call(f32[3,16,64,256]{3,2,1,0:T(8,128)} %bitcast.6, f32[3,16,64,256]{3,2,1,0:T(8,128)} %bitcast.7, f32[16,16,64]{2,1,0:T(8,128)} %bitcast.8, f32[16,16,64]{2,1,0:T(8,128)} %bitcast.9, ...), custom_call_target="tpu_custom_call" | custom-call | tf_op jit(solution)/shard_map/block/pallas_call | solution.py:779
  201.9 3.4 %hand_on.1 = (f32[3,16,64,256]{3,2,1,0:T(8,128)}, f32[2,8,256,256]{3,2,1,0:T(8,128)}, f32[256,512]{1,0:T(8,128)}, f32[512,256]{1,0:T(8,128)}) custom-call(f32[3,16,64,256]{3,2,1,0:T(8,128)S(1)} %get-tuple-element.15.refs_0_, f32[2,8,256,256]{3,2,1,0:T(8,128)S(1)} %get-tuple-element.16.refs_1_, f32[256,512]{1,0:T(8,128)S(1)} %get-tuple-element.17.refs_2_, ...), custom_call_target="tpu_custom_call" | custom-call | tf_op jit(solution)/shard_map/hand_on/pallas_call | solution.py:738

commit v11 on v10

--- a/solution.py
+++ b/solution.py
@@ -28,17 +28,12 @@
     return lax.dot_general(a, b, dims, preferred_element_type=F32)
 
 
-def dft_tables(lon_count, num_modes, h_size):
+def dft_table(lon_count, num_modes, h_size):
     modes, lons = np.arange(num_modes), np.arange(lon_count)
     angle = 2.0 * np.pi * ((modes[:, None] * lons[None, :]) % lon_count) / lon_count
-    fwd = np.stack([np.cos(angle), -np.sin(angle)], 0) * lon_count ** -0.5
-    inv = fwd * np.where(modes == 0, 1.0, 2.0)[None, :, None]
-
-    def rows(table):
-        table = table.reshape(2, h_size, num_modes // h_size, lon_count).transpose(1, 0, 2, 3)
-        return table.reshape(2 * num_modes, lon_count).astype(np.float32)
-
-    return rows(fwd), rows(inv)
+    table = np.stack([np.cos(angle), -np.sin(angle)], 0) * lon_count ** -0.5
+    table = table.reshape(2, h_size, num_modes // h_size, lon_count).transpose(1, 0, 2, 3)
+    return table.reshape(2 * num_modes, lon_count).astype(np.float32)
 
 
 def drain(ref, sem):
@@ -86,28 +81,34 @@
     return out
 
 
-PARTS = 2
+PARTS = 4
 GS_ROWS = 176
 GS_FIRST = (0, 1, 2)
 ORDER = " ".join((
-    'go', 'sX01', 'sX00', 'sX10', 'sX11', 'tb1', 'fd01', 'tb2', 'fd00', 'tb3',
-    'tb4', 'st2', 'fl0', 'fd10', 'sX21', 'fd11', 'fo0', 'fl1', 'tb5', 'sX20',
-    'fu0', 'fo1', 'fd21', 'fi00', 'sY00', 'fi01', 'sY01', 'fd20', 'pw00', 'sD00',
-    'fu1', 'fl2', 'pw01', 'fi10', 'sY10', 'bd00', 'fi11', 'sD01', 'fo2', 'pw10',
-    'sY11', 'bd01', 'sD10', 'fu2', 'pw11', 'sD11', 'bl0', 'fi21', 'sY21', 'fi20',
-    'bd10', 'bo0', 'sY20', 'bd11', 'pw21', 'sD21', 'bu0', 'pw20', 'sD20', 'bl1',
-    'bd21', 'gw1', 'gsa', 'bi00', 'bi01', 'gw2', 'sN01', 'bd20', 'bo1', 'gw3',
-    'bl2', 'sN00', 'bu1', 'bo2', 'pj1', 'gw4', 'bi10', 'sN10', 'gsb', 'gw5',
-    'gs1', 'gs20', 'gs21', 'gs310', 'gs300', 'bi11', 'gw6', 'gs61', 'sN11', 'gs303',
-    'gw7', 'gs311', 'gs301', 'bu2', 'gs313', 'gs60', 'gs411', 'gs400', 'gs312', 'bi20',
-    'gw8', 'pj2', 'gs403', 'bi21', 'sN21', 'fn00', 'gs413', 'gs302', 'gs500', 'gs410',
-    'sN20', 'gs401', 'gs511', 'fn10', 'end', 'gs510', 'gs412', 'gs402', 'gs502', 'fn11',
-    'gs501', 'gs513', 'fn01', 'fn20', 'fn21', 'gs503', 'gs512',
+    'go', 'sX03', 'sX00', 'tb1', 'sX02', 'sX01', 'st2', 'fd03', 'tb2', 'sX10',
+    'fd00', 'sX13', 'fd02', 'fd01', 'tb4', 'sX12', 'sX11', 'tb3', 'fd13', 'fl0',
+    'fd10', 'sX20', 'sX22', 'fd11', 'tb5', 'fd12', 'fo0', 'fl1', 'sX23', 'fd20',
+    'fu0', 'sX21', 'fo1', 'fi00', 'sY00', 'fd23', 'fi02', 'sY02', 'fi03', 'sY03',
+    'fi01', 'pw00', 'sD00', 'fu1', 'sY01', 'pw02', 'pw03', 'fd21', 'sD02', 'bd00',
+    'fd22', 'fi10', 'fi11', 'sD03', 'fi12', 'pw01', 'sD01', 'sY10', 'fl2', 'sY11',
+    'bd01', 'fi13', 'bd02', 'pw10', 'sY12', 'bd03', 'fo2', 'sY13', 'pw11', 'sD11',
+    'bl0', 'pw12', 'sD10', 'fu2', 'sD12', 'fi21', 'sY21', 'bo0', 'fi23', 'bd12',
+    'bd10', 'sY23', 'bd11', 'fi22', 'pw21', 'sY22', 'fi20', 'sY20', 'bu0', 'pw23',
+    'pw13', 'sD13', 'pw22', 'sD22', 'sD23', 'bi01', 'bd13', 'sD21', 'pw20', 'bi03',
+    'gw1', 'bd22', 'sD20', 'bl1', 'bi00', 'bd23', 'bi02', 'bd21', 'sN00', 'gw2',
+    'sN03', 'bd20', 'bo1', 'bl2', 'sN01', 'sN02', 'gw3', 'bu1', 'gsa', 'bo2',
+    'gsb', 'pj1', 'gw4', 'bi10', 'sN10', 'bi11', 'sN11', 'gs1', 'pj2', 'gs20',
+    'gw5', 'bi13', 'gs21', 'gs310', 'bu2', 'gs300', 'gs311', 'gs61', 'fn11', 'bi12',
+    'sN13', 'gs301', 'gw6', 'sN12', 'gs303', 'gs313', 'gs60', 'bi22', 'gs410', 'gw7',
+    'fn03', 'bi23', 'bi20', 'sN20', 'bi21', 'gs312', 'gs302', 'sN22', 'fn00', 'fn13',
+    'gs401', 'fn12', 'gw8', 'sN23', 'gs411', 'sN21', 'gs413', 'gs403', 'gs510', 'gs412',
+    'fn02', 'fn20', 'fn01', 'gs400', 'fn22', 'gs402', 'end', 'gs500', 'fn10', 'gs503',
+    'gs511', 'gs502', 'fn21', 'gs513', 'fn23', 'gs501', 'gs512',
 ))
 
 
 def block_kernel(sizes, total_points,
-                 x, tgt, leg_p_in, leg_q_in, spec_w, lat_in, w1_in, w2_in, f_in, g_in,
+                 x, tgt, leg_p_in, leg_q_in, spec_w, lat_in, w1_in, w2_in, f_in,
                  dout, gs_out, gin_out, gout_out, loss_out,
                  leg_p, leg_q, lat, w1, w2, f_tab, g_tab, ft_tab, gt_tab,
                  xh, th, pk, rows, yrow, hy,
@@ -154,11 +155,11 @@
     load_t = [pltpu.make_async_copy(tgt.at[b], th.at[b], sem_in.at[b, 1]) for b in range(nb)]
     load_k = pltpu.make_async_copy(spec_w.at[:, pl.ds(me * l_own, l_own)], ker, sem_k.at[0])
     small = [pltpu.make_async_copy(src, dst, sem_small.at[i]) for i, (src, dst) in enumerate((
-        (leg_p_in, leg_p), (leg_q_in, leg_q), (f_in, f_tab), (g_in, g_tab), (lat_in, lat), (w1_in, w1), (w2_in, w2)))]
-    for c in loads + small[:4] + [load_k] + load_t + small[4:]:
+        (leg_p_in, leg_p), (leg_q_in, leg_q), (f_in, f_tab), (lat_in, lat), (w1_in, w1), (w2_in, w2)))]
+    for c in loads + small[:3] + [load_k] + load_t + small[3:]:
         c.start()
     coming["k"] = load_k.wait
-    coming["small"] = lambda: [c.wait() for c in small[4:]]
+    coming["small"] = lambda: [c.wait() for c in small[3:]]
     coming.update({("t", b): load_t[b].wait for b in range(nb)})
     for ref in (ar, br, dar, dbr, st_s, gw, ls):
         ref[...] = jnp.zeros_like(ref)
@@ -231,9 +232,19 @@
         coming[name, b, k] = lambda: drain(xs.at[b, :, at_rows(0, k)], sem.at[b, k, 1])
 
     def send_lats(b, dst, sem, name):
+        def one(k, _):
+            keep(ys.at[b, at_rows(h, k)], dst.at[b, h, at_rows(0, k)], sem.at[b, k])
+
+            def body(j, _):
+                o = (h + j) % h_size
+                push(ys.at[b, at_rows(o, k)], dst.at[b, h, at_rows(0, k)], sem.at[b, k], {"h": o})
+                return 0
+
+            return lax.fori_loop(1, h_size, body, 0)
+
+        lax.fori_loop(0, PARTS, one, 0)
         for k in range(PARTS):
-            along("h", lambda o: (ys.at[b, at_rows(o, k)], dst.at[b, h, at_rows(0, k)]), sem.at[b, k],
-                  xs.at[b, pl.ds(0, h_size - 1), at_rows(0, k)], ("ys", b))
+            unsent.setdefault(("ys", b), []).append(lambda k=k: drain(xs.at[b, pl.ds(0, h_size - 1), at_rows(0, k)], sem.at[b, k, 0]))
             coming[name, b, k] = lambda k=k: drain(dst.at[b, :, at_rows(0, k)], sem.at[b, k, 1])
 
     def send_owner(b, dst, sem, name):
@@ -272,39 +283,50 @@
 
         lax.fori_loop(k * part // 2, (k + 1) * part // 2, body, 0)
 
-    def level(v):
+    def level(v, here):
         mean = jnp.mean(v, axis=0, keepdims=True)
         mean = 0.5 * (mean + flip(mean))
-        return v - jnp.where(h == 0, mean, 0.0)
+        return v - jnp.where(jnp.logical_and(h == 0, here), mean, 0.0)
+
+    def orders(body):
+        def four(n, _):
+            for i in range(4):
+                body(4 * n + i, n == 0 if i == 0 else None)
+            return 0
+
+        lax.fori_loop(0, 2, four, 0)
 
     def leg_down(b, table, src, fix):
         settle(("als", b))
-        for m in range(8):
-            parts = [src[b, pl.ds(ri * 8 + m, ntp * h_size, stride=16), :] for ri in range(2)]
-            if fix and m == 0:
-                parts[0] = level(parts[0])
-            out = dot(table[m], jnp.concatenate(parts, axis=1))
-            re0, re1 = out[:nl, :LANES], out[nl:, :LANES]
-            im0, im1 = out[:nl, LANES:], out[nl:, LANES:]
-            als[b, pl.ds(m, nl, stride=8), :] = jnp.where(low(re0), re0, im1) + flip(jnp.where(low(re0), im0, re1))
+
+        def one(m, here):
+            re, im = (src[b, pl.ds(ri * 8 + m, ntp * h_size, stride=16), :] for ri in range(2))
+            if fix and here is not None:
+                re = level(re, here)
+            als[b, pl.ds(m, nl, stride=8), :] = dot(table[m], jnp.concatenate(weave(re, im), axis=0))
+
+        orders(one)
 
     def leg_up(b, table, src, fix):
         settle(("ys", b))
-        for m in range(8):
+
+        def one(m, here):
             out = dot(table[m], src[b, pl.ds(m, nl, stride=8), :])
             re, im = weave(out[:nlat // 2], out[nlat // 2:])
-            if fix and m == 0:
-                re = level(re)
+            if fix and here is not None:
+                re = level(re, here)
             ys[b, pl.ds(m, ntp * h_size, stride=16), :] = re
             ys[b, pl.ds(8 + m, ntp * h_size, stride=16), :] = im
 
+        orders(one)
+
     def owned(b, l, src):
-        tiles = [src[b, :, l * 8:(l + 1) * 8, j * LANES:(j + 1) * LANES].reshape(-1, LANES) for j in range(w_size)]
+        tiles = [src[b, :, rows_at(l, 8), j * LANES:(j + 1) * LANES].reshape(-1, LANES) for j in range(w_size)]
         return weave_wide(tiles)
 
     def put_back(b, l, re, im):
         for j, tile in enumerate(weave_tiles(re, im)):
-            bs[b, :, j, l * 8:(l + 1) * 8, :] = tile.reshape(h_size, 8, LANES)
+            bs[b, :, j, rows_at(l, 8), :] = tile.reshape(h_size, 8, LANES)
 
     def put_rows(b, i, v0, v1):
         for j, tile in enumerate(weave_tiles(v0, v1)):
@@ -340,11 +362,12 @@
 
             st_s[2 * b:2 * b + 1, :] = mean
             st_s[2 * b + 1:2 * b + 2, :] = lax.fori_loop(0, nt, spread, jnp.zeros((1, nc), F32))
-        for c in small[:4]:
+        for c in small[:3]:
             c.wait()
         for a, leg in enumerate((leg_p, leg_q)):
             for m in range(leg.shape[0]):
                 tab_s[a, m // 2, :, m % 2 * nl:(m % 2 + 1) * nl] = leg[m]
+        g_tab[...] = jnp.where(lax.broadcasted_iota(jnp.int32, f_tab.shape, 0) == 0, 1.0, 2.0) * f_tab[...]
         ft_tab[...] = f_tab[...].T
         gt_tab[...] = g_tab[...].T
         pl.semaphore_wait(barrier, ndev - 1 + dp_size - 1)
@@ -389,12 +412,17 @@
 
     def table_in(a, down, up):
         got(("tab2", a))
-        for m in range(8):
-            both = tab[a, m // 2].reshape(h_size, 2, ntp, 2 * nl)
+
+        def body(n, _):
+            both = tab[a, n].reshape(h_size, 2, ntp, 2 * nl)
+            both = jnp.concatenate([both[:, j].reshape(-1, 2 * nl) for j in range(2)], axis=0)
             for j in range(2):
-                t = both[:, j].reshape(-1, 2 * nl)[:, m % 2 * nl:(m % 2 + 1) * nl]
-                up[m, j * (nlat // 2):(j + 1) * (nlat // 2), :] = t
-                down[m, j * nl:(j + 1) * nl, :] = t.T
+                t = both[:, j * nl:(j + 1) * nl]
+                up[2 * n + j] = t
+                down[2 * n + j] = t.T
+            return 0
+
+        lax.fori_loop(0, tab.shape[1], body, 0)
 
     def tb2():
         table_out(0)
@@ -428,13 +456,17 @@
             st3()
         got(("a", b))
         settle(("bs", b))
-        for l in range(l_own):
+
+        def one(l, _):
             re, im = owned(b, l, ar)
             a = jnp.concatenate([re, im], axis=0) * scales[b]
             asave[b, l] = a
             n = a.shape[0] // 2
             own, other = dot(a, ker[0, l]), dot(a, ker[1, l])
             put_back(b, l, own[:n] - other[n:], own[n:] + other[:n])
+            return 0
+
+        lax.fori_loop(0, l_own, one, 0)
         send_back(b, br, sem_b, "b")
         along("dp", lambda o: (asave.at[b, o // 2], aall.at[dp, b]), sem_az.at[b], aall.at[pl.ds(0, dp_size - 1), b])
         coming["az", b] = lambda: drain(aall.at[:, b], sem_az.at[b, 1])
@@ -460,8 +492,8 @@
         settle(("pk", b, k))
 
         def body(n, _):
-            lats = [2 * n, 2 * n + ntp, 2 * n + 1, 2 * n + 1 + ntp]
-            y = jnp.concatenate([v for j in range(2) for v in get_rows(b, 2 * n + j)], axis=0)
+            lats = [n, n + ntp]
+            y = jnp.concatenate(get_rows(b, n), axis=0)
             yb = y.astype(BF16)
             hid = bdot(yb, w1[...])
             th_ = jnp.tanh(GELU_C * (hid + GELU_A * (hid * hid * hid)))
@@ -483,11 +515,10 @@
             gw[:nc, :] += gin[:, :nc]
             gw[nc:2 * nc, :] += gin[:, nc:]
             dy = d + bdot(dh, w1[...], NT)
-            for j in range(2):
-                put_rows(b, 2 * n + j, dy[2 * j * npl:(2 * j + 1) * npl], dy[(2 * j + 1) * npl:(2 * j + 2) * npl])
-            return 0
-
-        lax.fori_loop(k * part // 2, (k + 1) * part // 2, body, 0)
+            put_rows(b, n, dy[:npl], dy[npl:])
+            return 0
+
+        lax.fori_loop(k * part, (k + 1) * part, body, 0)
 
     def sD(b, k):
         send_home_rows(b, k, sem_d, "d")
@@ -506,8 +537,8 @@
     def bo(b):
         got(("da", b))
         settle(("bs", b), "st")
-        s2 = jnp.zeros((1, nc), F32)
-        for l in range(l_own):
+
+        def one(l, s2):
             re, im = owned(b, l, dar)
             d = jnp.concatenate([re, im], axis=0)
             dsave[b, l] = d
@@ -515,7 +546,9 @@
             own, other = dot(d, ker[0, l], NT), dot(d, ker[1, l], NT)
             re, im = own[:n] + other[n:], own[n:] - other[:n]
             put_back(b, l, re, im)
-            s2 = s2 + jnp.sum(re * asave[b, l, :n] + im * asave[b, l, n:], axis=0, keepdims=True)
+            return s2 + jnp.sum(re * asave[b, l, :n] + im * asave[b, l, n:], axis=0, keepdims=True)
+
+        s2 = lax.fori_loop(0, l_own, one, jnp.zeros((1, nc), F32))
         send_back(b, dbr, sem_db, "db")
         along("dp", lambda o: (dsave.at[b, o // 2, :, lanes_at(o % 2)], dall.at[dp, b]), sem_dz.at[b], dall.at[pl.ds(0, dp_size - 1), b])
         coming["dz", b] = lambda: drain(dall.at[:, b], sem_dz.at[b, 1])
@@ -648,25 +681,32 @@
         index, size = place[axis]
         return (index + k + size) % size
 
-    def sample_grad(b):
+    def add_sample(b):
         got(("az", b))
         got(("dz", b))
-        d = dall[:, b].reshape(dp_size, 2, -1, LANES)
-        turned = jnp.concatenate([d[:, 1:], -d[:, :1]], axis=1)
-        both = jnp.concatenate([d.reshape(-1, LANES), turned.reshape(-1, LANES)], axis=1)
-        return dot(aall[:, b].reshape(-1, nc), both, TN)
+
+        def body(n, _):
+            d = dall[n, b]
+            half = d.shape[0] // 2
+            both = jnp.concatenate([d, jnp.concatenate([d[half:], -d[:half]], axis=0)], axis=1)
+            gs_acc[...] += dot(aall[n, b], both, TN)
+            return 0
+
+        lax.fori_loop(0, dp_size, body, 0)
 
     def gsa():
-        gs_acc[...] = sample_grad(GS_FIRST[0])
+        gs_acc[...] = jnp.zeros_like(gs_acc)
+        add_sample(GS_FIRST[0])
 
     def gsb():
-        gs_acc[...] += sample_grad(GS_FIRST[1])
+        add_sample(GS_FIRST[1])
 
     def gs1():
-        out = gs_acc[...] + sample_grad(GS_FIRST[2])
+        add_sample(GS_FIRST[2])
         for q in range(2):
+            rows_q = pl.ds(first_rows[q], gs_sum[q].shape[1])
             for p in range(2):
-                gs_sum[q][p] = out[first_rows[q]:first_rows[q] + gs_sum[q].shape[1], p * LANES:(p + 1) * LANES]
+                gs_sum[q][p] = gs_acc[rows_q, p * LANES:(p + 1) * LANES]
 
     def once(key):
         if key in coming:
@@ -727,7 +767,11 @@
 
 def hand_on_kernel(*refs):
     n = len(refs) // 2
-    copies = [pltpu.make_async_copy(refs[i], refs[n + i], refs[2 * n].at[i]) for i in range(n)]
+    pairs = []
+    for src, dst in zip(refs[:n], refs[n:2 * n]):
+        lead = [()] if len(src.shape) == 2 else [(i,) for i in range(src.shape[0])]
+        pairs += [(src.at[i], dst.at[i]) if i else (src, dst) for i in lead]
+    copies = [pltpu.make_async_copy(src, dst, refs[2 * n].at[i]) for i, (src, dst) in enumerate(pairs)]
     for c in copies:
         c.start()
     for c in copies:
@@ -739,7 +783,7 @@
         hand_on_kernel, name="hand_on",
         out_shape=[jax.ShapeDtypeStruct(a.shape, F32) for a in arrays],
         in_specs=[pl.BlockSpec(memory_space=pltpu.VMEM)] * len(arrays), out_specs=[pl.BlockSpec(memory_space=pl.ANY)] * len(arrays),
-        scratch_shapes=[pltpu.SemaphoreType.DMA((len(arrays),))],
+        scratch_shapes=[pltpu.SemaphoreType.DMA((32,))],
         compiler_params=pltpu.CompilerParams(vmem_limit_bytes=12 * 1024 * 1024),
     )(*[pltpu.with_memory_space_constraint(a, pltpu.VMEM) for a in arrays])
 
@@ -758,7 +802,6 @@
         lo = nl // ndev
         assert nm == 8 * h_size and nc == w_size * LANES // 2 and h_size == 2 * w_size and 2 * lo == dp_size and 2 * nl == LANES
         total_points = nb * dp_size * nc * nlat * nlon
-        fwd_np, inv_np = dft_tables(nlon, nm, h_size)
         any_spec = pl.BlockSpec(memory_space=pl.ANY)
         vmem_spec = pl.BlockSpec(memory_space=pltpu.VMEM)
         sds = lambda *s: jax.ShapeDtypeStruct(s, F32)
@@ -780,7 +823,7 @@
             functools.partial(block_kernel, (dp_size, h_size, w_size), total_points),
             name="block",
             out_shape=[vm(nb, nt, npl, nc), vm(2, lo * w_size, nc, nc), vm(nc, 2 * nc), vm(2 * nc, nc), sds(1, 1)],
-            in_specs=[any_spec] * 10,
+            in_specs=[any_spec] * 9,
             out_specs=[vmem_spec] * 5,
             scratch_shapes=[
                 vm(*leg_fwd.shape[:1], nt, nl), vm(*leg_fwd.shape[:1], nt, nl), pltpu.SMEM((nt,), F32), pltpu.VMEM(w_in.shape, BF16),
@@ -791,17 +834,17 @@
                 vm(dp_size, nb, 2 * nm, nc), vm(dp_size, nb, 2 * nm, LANES),
                 vm(8, nc), vm(h_size, 8, nc), vm(8, nc), vm(w_size, 8, nc),
                 vm(2, n_pairs, nt, 2 * nl), vm(2, w_size, n_pairs, nt, 2 * nl), vm(2, 4, nlat, 2 * nl),
-                vm(8, 2 * nl, nlat // 2), vm(8, 2 * nl, nlat // 2), vm(8, nlat, nl), vm(8, nlat, nl),
+                vm(8, nl, nlat), vm(8, nl, nlat), vm(8, nlat, nl), vm(8, nlat, nl),
                 vm(2, lo, nc, nc),
                 vm(n_rows, nc), vm(n_c, nc), vm(n_c, nc), vm(dp_size, n_z, nc), vm(n_z, nc), vm(w_size, n_h, nc), vm(n_h, nc),
                 vm(w_size, n_w, nc), vm(n_w, nc), vm(n_h, nc), vm(n_z, nc), vm(n_c, nc), vm(n_c, nc),
                 vm(8, nc), vm(8, nc), vm(8, nc), vm(dp_size, 8, nc), vm(8, nc), vm(w_size, 8, nc), vm(8, nc), vm(w_size, 8, nc),
                 vm(nc, nc), vm(2, cut, LANES), vm(2, nc - cut, LANES), vm(4, 2, cut, LANES), vm(4, 2, nc - cut, LANES),
             ] + [dma(nb, PARTS, 2)] * 8 + [dma(nb, 2)] * 6 + [dma(nb, 2), dma(4, 2), dma(5, 2), dma(1), dma(8, 2), dma(4, 2),
-                 dma(2, 5, 2), dma(2, 4, 4, 2), dma(3), dma(7)],
+                 dma(2, 5, 2), dma(2, 4, 4, 2), dma(3), dma(6)],
             compiler_params=pltpu.CompilerParams(collective_id=0, has_side_effects=True, vmem_limit_bytes=54 * 1024 * 1024),
         )(field.transpose(0, 2, 3, 1), target.transpose(0, 2, 3, 1), leg_fwd.transpose(0, 2, 1), leg_inv.transpose(0, 2, 1),
-          spec_w, lat_weight, w_in, w_out, jnp.asarray(fwd_np), jnp.asarray(inv_np))
+          spec_w, lat_weight, w_in, w_out, jnp.asarray(dft_table(nlon, nm, h_size)))
         d_x, g_spec, g_in, g_out = hand_on(results[:4])
         loss = results[4]
         return loss.reshape(()), d_x.transpose(0, 3, 1, 2), g_spec, g_in, g_out

time: 209 us -> 207 us (level); the launches traced: 207 us -> 207 us
  no operation moved by 1% of the time
where the time goes in v11:
time: 207 us
  Pallas kernels  205 us (99%)
  between operations  2.41 us (1%)
    pallas_call x1, Pallas kernels, local_step(): pl.pallas_call(functools.partial(block_kernel, (dp_size, h_size, w_size),...  201 us

profile of v11, /device:TPU:1, one launch (start us, length us, event | category | flops | bytes accessed | tf_op | source)
XLA Modules:
  0.0 207.2 jit_solution(16843014359306629058)
XLA Ops:
  0.6 201.2 %block.1 = (f32[3,16,64,256]{3,2,1,0:T(8,128)S(1)}, f32[2,8,256,256]{3,2,1,0:T(8,128)S(1)}, f32[256,512]{1,0:T(8,128)S(1)}, f32[512,256]{1,0:T(8,128)S(1)}, f32[1,1]{1,0:T(1,128)}) custom-call(f32[3,16,64,256]{3,2,1,0:T(8,128)} %bitcast.6, f32[3,16,64,256]{3,2,1,0:T(8,128)} %bitcast.7, f32[16,16,64]{2,1,0:T(8,128)} %bitcast.8, f32[16,16,64]{2,1,0:T(8,128)} %bitcast.9, ...), custom_call_target="tpu_custom_call" | custom-call | tf_op jit(solution)/shard_map/block/pallas_call | solution.py:822
  201.8 3.6 %hand_on.1 = (f32[3,16,64,256]{3,2,1,0:T(8,128)}, f32[2,8,256,256]{3,2,1,0:T(8,128)}, f32[256,512]{1,0:T(8,128)}, f32[512,256]{1,0:T(8,128)}) custom-call(f32[3,16,64,256]{3,2,1,0:T(8,128)S(1)} %get-tuple-element.15.refs_0_, f32[2,8,256,256]{3,2,1,0:T(8,128)S(1)} %get-tuple-element.16.refs_1_, f32[256,512]{1,0:T(8,128)S(1)} %get-tuple-element.17.refs_2_, ...), custom_call_target="tpu_custom_call" | custom-call | tf_op jit(solution)/shard_map/hand_on/pallas_call | solution.py:782

commit v12 on v11

--- a/solution.py
+++ b/solution.py
@@ -85,25 +85,26 @@
 GS_ROWS = 176
 GS_FIRST = (0, 1, 2)
 ORDER = " ".join((
-    'go', 'sX03', 'sX00', 'tb1', 'sX02', 'sX01', 'st2', 'fd03', 'tb2', 'sX10',
-    'fd00', 'sX13', 'fd02', 'fd01', 'tb4', 'sX12', 'sX11', 'tb3', 'fd13', 'fl0',
-    'fd10', 'sX20', 'sX22', 'fd11', 'tb5', 'fd12', 'fo0', 'fl1', 'sX23', 'fd20',
-    'fu0', 'sX21', 'fo1', 'fi00', 'sY00', 'fd23', 'fi02', 'sY02', 'fi03', 'sY03',
-    'fi01', 'pw00', 'sD00', 'fu1', 'sY01', 'pw02', 'pw03', 'fd21', 'sD02', 'bd00',
-    'fd22', 'fi10', 'fi11', 'sD03', 'fi12', 'pw01', 'sD01', 'sY10', 'fl2', 'sY11',
-    'bd01', 'fi13', 'bd02', 'pw10', 'sY12', 'bd03', 'fo2', 'sY13', 'pw11', 'sD11',
-    'bl0', 'pw12', 'sD10', 'fu2', 'sD12', 'fi21', 'sY21', 'bo0', 'fi23', 'bd12',
-    'bd10', 'sY23', 'bd11', 'fi22', 'pw21', 'sY22', 'fi20', 'sY20', 'bu0', 'pw23',
-    'pw13', 'sD13', 'pw22', 'sD22', 'sD23', 'bi01', 'bd13', 'sD21', 'pw20', 'bi03',
-    'gw1', 'bd22', 'sD20', 'bl1', 'bi00', 'bd23', 'bi02', 'bd21', 'sN00', 'gw2',
-    'sN03', 'bd20', 'bo1', 'bl2', 'sN01', 'sN02', 'gw3', 'bu1', 'gsa', 'bo2',
-    'gsb', 'pj1', 'gw4', 'bi10', 'sN10', 'bi11', 'sN11', 'gs1', 'pj2', 'gs20',
-    'gw5', 'bi13', 'gs21', 'gs310', 'bu2', 'gs300', 'gs311', 'gs61', 'fn11', 'bi12',
-    'sN13', 'gs301', 'gw6', 'sN12', 'gs303', 'gs313', 'gs60', 'bi22', 'gs410', 'gw7',
-    'fn03', 'bi23', 'bi20', 'sN20', 'bi21', 'gs312', 'gs302', 'sN22', 'fn00', 'fn13',
-    'gs401', 'fn12', 'gw8', 'sN23', 'gs411', 'sN21', 'gs413', 'gs403', 'gs510', 'gs412',
-    'fn02', 'fn20', 'fn01', 'gs400', 'fn22', 'gs402', 'end', 'gs500', 'fn10', 'gs503',
-    'gs511', 'gs502', 'fn21', 'gs513', 'fn23', 'gs501', 'gs512',
+    'pk0', 'pk1', 'go', 'sX03', 'sX01', 'pk2', 'tb1', 'sX00', 'sX02', 'sX11',
+    'sX10', 'fd03', 'sX13', 'tb2', 'fd00', 'fd01', 'fd02', 'tb3', 'st1', 'tb4',
+    'sX12', 'fd11', 'fl0', 'st2', 'fd13', 'fd10', 'sX20', 'fd12', 'sX22', 'tb5',
+    'fo0', 'sX23', 'fl1', 'fu0', 'fd23', 'sX21', 'fd22', 'fd20', 'fo1', 'fi00',
+    'sY00', 'fi02', 'sY02', 'fi01', 'fi03', 'fd21', 'sY03', 'pw00', 'sY01', 'pw02',
+    'sD02', 'fl2', 'fu1', 'pw03', 'sD03', 'pw01', 'sD00', 'fo2', 'fi11', 'sD01',
+    'sY11', 'fi12', 'sY12', 'fi13', 'fi10', 'sY10', 'bd00', 'bd02', 'bd03', 'bd01',
+    'sY13', 'fu2', 'bl0', 'fi21', 'sY21', 'fi22', 'pw10', 'pw13', 'sY22', 'pw11',
+    'pw12', 'sD10', 'bo0', 'fi20', 'sD12', 'pw21', 'fi23', 'sY23', 'pw22', 'bd10',
+    'sD11', 'sY20', 'bu0', 'pw23', 'sD13', 'bi00', 'bd11', 'sD23', 'bd12', 'pw20',
+    'sD22', 'gw1', 'sD20', 'bi01', 'bd13', 'gw2', 'sD21', 'bd23', 'bi03', 'bi02',
+    'bl1', 'sN03', 'bd22', 'bd20', 'bd21', 'sN02', 'gw3', 'bo1', 'bl2', 'gw4',
+    'sN01', 'sN00', 'bu1', 'gw5', 'bo2', 'pj1', 'bi10', 'sN10', 'bi11', 'gsa',
+    'sN11', 'gsb', 'gs1', 'gs21', 'gs20', 'gw6', 'bi12', 'gs300', 'sN12', 'bu2',
+    'gs311', 'gs61', 'gs313', 'gs301', 'gw7', 'bi13', 'bi21', 'gs303', 'gs60', 'gs312',
+    'sN13', 'gs411', 'pj2', 'fn10', 'bi22', 'gs310', 'bi23', 'gs302', 'sN23', 'fn01',
+    'gw8', 'gs401', 'fn02', 'sN21', 'gs410', 'fn00', 'sN22', 'fn03', 'bi20', 'gs403',
+    'end', 'fn13', 'sN20', 'gs412', 'gs402', 'gs510', 'gs413', 'gs501', 'fn21', 'fn11',
+    'gs511', 'gs400', 'fn12', 'gs503', 'fn20', 'fn22', 'gs512', 'fn23', 'gs500', 'gs502',
+    'gs513',
 ))
 
 
@@ -345,37 +346,44 @@
         m2 = jnp.sum(stats, axis=0)
         return [(mean[2 * b:2 * b + 1], m2[2 * b + 1:2 * b + 2] + n * dev2[2 * b:2 * b + 1]) for b in range(nb)]
 
+    sums = {}
+
+    def pk_(b):
+        loads[b].wait()
+
+        def body(i, total):
+            v0, v1 = xh[b, i], xh[b, i + ntp]
+            put_rows(b, i, v0, v1)
+            return total + jnp.sum(v0 + v1, axis=0, keepdims=True)
+
+        sums[b] = lax.fori_loop(0, ntp, body, jnp.zeros((1, nc), F32))
+
     def go():
-        for b in range(nb):
-            loads[b].wait()
-
-            def pack(i, total, b=b):
-                v0, v1 = xh[b, i], xh[b, i + ntp]
-                put_rows(b, i, v0, v1)
-                return total + jnp.sum(v0 + v1, axis=0, keepdims=True)
-
-            mean = lax.fori_loop(0, ntp, pack, jnp.zeros((1, nc), F32)) / count
-
-            def spread(t, total, b=b, mean=mean):
-                d = xh[b, t] - mean
-                return total + jnp.sum(d * d, axis=0, keepdims=True)
-
-            st_s[2 * b:2 * b + 1, :] = mean
-            st_s[2 * b + 1:2 * b + 2, :] = lax.fori_loop(0, nt, spread, jnp.zeros((1, nc), F32))
         for c in small[:3]:
             c.wait()
         for a, leg in enumerate((leg_p, leg_q)):
             for m in range(leg.shape[0]):
                 tab_s[a, m // 2, :, m % 2 * nl:(m % 2 + 1) * nl] = leg[m]
+        pl.semaphore_wait(barrier, ndev - 1 + dp_size - 1)
+        along("w", lambda o: (tab_s.at[:, rows_at(dp, n_tab)], tab_w.at[:, w, rows_at(dp, n_tab)]), sem_tab.at[0],
+              tab_w.at[:, pl.ds(0, w_size - 1), pl.ds(0, n_tab)])
+        coming["tab"] = lambda: drain(tab_w.at[:, :, pl.ds(0, n_tab)], sem_tab.at[0, 1])
+
+    def st1():
+        for b in range(nb):
+            mean = sums[b] / count
+
+            def body(t, total, b=b, mean=mean):
+                d = xh[b, t] - mean
+                return total + jnp.sum(d * d, axis=0, keepdims=True)
+
+            st_s[2 * b:2 * b + 1, :] = mean
+            st_s[2 * b + 1:2 * b + 2, :] = lax.fori_loop(0, nt, body, jnp.zeros((1, nc), F32))
+        along("w", lambda o: (st_s, st_w.at[w]), sem_st.at[0], st_w.at[pl.ds(0, w_size - 1)], "st")
+        coming["st"] = lambda: drain(st_w, sem_st.at[0, 1])
         g_tab[...] = jnp.where(lax.broadcasted_iota(jnp.int32, f_tab.shape, 0) == 0, 1.0, 2.0) * f_tab[...]
         ft_tab[...] = f_tab[...].T
         gt_tab[...] = g_tab[...].T
-        pl.semaphore_wait(barrier, ndev - 1 + dp_size - 1)
-        along("w", lambda o: (st_s, st_w.at[w]), sem_st.at[0], st_w.at[pl.ds(0, w_size - 1)], "st")
-        coming["st"] = lambda: drain(st_w, sem_st.at[0, 1])
-        along("w", lambda o: (tab_s.at[:, rows_at(dp, n_tab)], tab_w.at[:, w, rows_at(dp, n_tab)]), sem_tab.at[0],
-              tab_w.at[:, pl.ds(0, w_size - 1), pl.ds(0, n_tab)])
-        coming["tab"] = lambda: drain(tab_w.at[:, :, pl.ds(0, n_tab)], sem_tab.at[0, 1])
 
     def st2():
         got("st")
@@ -753,6 +761,7 @@
             drain(gs_b[q].at[k], sem_gf.at[q, i, k, 0])
 
     scope = dict(locals())
+    scope["pk"] = pk_
     for name in ORDER.split():
         call = name.rstrip("0123456789") or name
         if name in scope:

time: 207 us -> 205 us (level)
  Pallas kernels: 205 us -> 202 us
    pallas_call x1, Pallas kernels: 201 us -> 199 us  [local_step(): pl.pallas_call(functools.partial(block_kernel, (dp_size, h_size, w_size),...]
where the time goes in v12:
time: 205 us
  Pallas kernels  202 us (99%)
  between operations  2.41 us (1%)
    pallas_call x1, Pallas kernels, local_step(): pl.pallas_call(functools.partial(block_kernel, (dp_size, h_size, w_size),...  199 us

profile of v12, /device:TPU:1, one launch (start us, length us, event | category | flops | bytes accessed | tf_op | source)
XLA Modules:
  0.0 204.7 jit_solution(714603985832515387)
XLA Ops:
  0.6 198.7 %block.1 = (f32[3,16,64,256]{3,2,1,0:T(8,128)S(1)}, f32[2,8,256,256]{3,2,1,0:T(8,128)S(1)}, f32[256,512]{1,0:T(8,128)S(1)}, f32[512,256]{1,0:T(8,128)S(1)}, f32[1,1]{1,0:T(1,128)}) custom-call(f32[3,16,64,256]{3,2,1,0:T(8,128)} %bitcast.6, f32[3,16,64,256]{3,2,1,0:T(8,128)} %bitcast.7, f32[16,16,64]{2,1,0:T(8,128)} %bitcast.8, f32[16,16,64]{2,1,0:T(8,128)} %bitcast.9, ...), custom_call_target="tpu_custom_call" | custom-call | tf_op jit(solution)/shard_map/block/pallas_call | solution.py:831
  199.3 3.6 %hand_on.1 = (f32[3,16,64,256]{3,2,1,0:T(8,128)}, f32[2,8,256,256]{3,2,1,0:T(8,128)}, f32[256,512]{1,0:T(8,128)}, f32[512,256]{1,0:T(8,128)}) custom-call(f32[3,16,64,256]{3,2,1,0:T(8,128)S(1)} %get-tuple-element.15.refs_0_, f32[2,8,256,256]{3,2,1,0:T(8,128)S(1)} %get-tuple-element.16.refs_1_, f32[256,512]{1,0:T(8,128)S(1)} %get-tuple-element.17.refs_2_, ...), custom_call_target="tpu_custom_call" | custom-call | tf_op jit(solution)/shard_map/hand_on/pallas_call | solution.py:791

commit v13 on v12

--- a/solution.py
+++ b/solution.py
@@ -32,7 +32,8 @@
     modes, lons = np.arange(num_modes), np.arange(lon_count)
     angle = 2.0 * np.pi * ((modes[:, None] * lons[None, :]) % lon_count) / lon_count
     table = np.stack([np.cos(angle), -np.sin(angle)], 0) * lon_count ** -0.5
-    table = table.reshape(2, h_size, num_modes // h_size, lon_count).transpose(1, 0, 2, 3)
+    groups = table.reshape(2, 2 * h_size, num_modes // h_size // 2, lon_count)
+    table = np.stack([groups[:, :h_size], groups[:, :h_size - 1:-1]], 2).transpose(1, 0, 2, 3, 4)
     return table.reshape(2 * num_modes, lon_count).astype(np.float32)
 
 
@@ -82,29 +83,28 @@
 
 
 PARTS = 4
+N_PARTS = 2
 GS_ROWS = 176
 GS_FIRST = (0, 1, 2)
 ORDER = " ".join((
-    'pk0', 'pk1', 'go', 'sX03', 'sX01', 'pk2', 'tb1', 'sX00', 'sX02', 'sX11',
-    'sX10', 'fd03', 'sX13', 'tb2', 'fd00', 'fd01', 'fd02', 'tb3', 'st1', 'tb4',
-    'sX12', 'fd11', 'fl0', 'st2', 'fd13', 'fd10', 'sX20', 'fd12', 'sX22', 'tb5',
-    'fo0', 'sX23', 'fl1', 'fu0', 'fd23', 'sX21', 'fd22', 'fd20', 'fo1', 'fi00',
-    'sY00', 'fi02', 'sY02', 'fi01', 'fi03', 'fd21', 'sY03', 'pw00', 'sY01', 'pw02',
-    'sD02', 'fl2', 'fu1', 'pw03', 'sD03', 'pw01', 'sD00', 'fo2', 'fi11', 'sD01',
-    'sY11', 'fi12', 'sY12', 'fi13', 'fi10', 'sY10', 'bd00', 'bd02', 'bd03', 'bd01',
-    'sY13', 'fu2', 'bl0', 'fi21', 'sY21', 'fi22', 'pw10', 'pw13', 'sY22', 'pw11',
-    'pw12', 'sD10', 'bo0', 'fi20', 'sD12', 'pw21', 'fi23', 'sY23', 'pw22', 'bd10',
-    'sD11', 'sY20', 'bu0', 'pw23', 'sD13', 'bi00', 'bd11', 'sD23', 'bd12', 'pw20',
-    'sD22', 'gw1', 'sD20', 'bi01', 'bd13', 'gw2', 'sD21', 'bd23', 'bi03', 'bi02',
-    'bl1', 'sN03', 'bd22', 'bd20', 'bd21', 'sN02', 'gw3', 'bo1', 'bl2', 'gw4',
-    'sN01', 'sN00', 'bu1', 'gw5', 'bo2', 'pj1', 'bi10', 'sN10', 'bi11', 'gsa',
-    'sN11', 'gsb', 'gs1', 'gs21', 'gs20', 'gw6', 'bi12', 'gs300', 'sN12', 'bu2',
-    'gs311', 'gs61', 'gs313', 'gs301', 'gw7', 'bi13', 'bi21', 'gs303', 'gs60', 'gs312',
-    'sN13', 'gs411', 'pj2', 'fn10', 'bi22', 'gs310', 'bi23', 'gs302', 'sN23', 'fn01',
-    'gw8', 'gs401', 'fn02', 'sN21', 'gs410', 'fn00', 'sN22', 'fn03', 'bi20', 'gs403',
-    'end', 'fn13', 'sN20', 'gs412', 'gs402', 'gs510', 'gs413', 'gs501', 'fn21', 'fn11',
-    'gs511', 'gs400', 'fn12', 'gs503', 'fn20', 'fn22', 'gs512', 'fn23', 'gs500', 'gs502',
-    'gs513',
+    'go', 'pk0', 'sX03', 'pk2', 'sX00', 'pk1', 'sX02', 'tb1', 'sX01', 'st1',
+    'sX11', 'fd03', 'fd00', 'sX10', 'tb2', 'fd01', 'fd02', 'tb4', 'sX12', 'tb3',
+    'st2', 'sX13', 'fd10', 'fl0', 'sX21', 'fd12', 'fd13', 'fd11', 'tb5', 'sX23',
+    'fo0', 'fl1', 'sX20', 'sX22', 'fu0', 'fo1', 'fi00', 'sY00', 'fd23', 'fi01',
+    'fd21', 'sY01', 'fd22', 'fi02', 'sY02', 'fd20', 'pw00', 'fi03', 'sY03', 'fu1',
+    'pw01', 'sD01', 'fl2', 'sD00', 'fi12', 'fi10', 'pw02', 'sY12', 'bd01', 'sY10',
+    'fi11', 'fi13', 'fo2', 'sY11', 'pw03', 'sY13', 'pw12', 'sD03', 'sD02', 'fu2',
+    'bd00', 'pw10', 'pw13', 'fi20', 'sD10', 'sD12', 'fi21', 'pw11', 'sD13', 'sD11',
+    'bd02', 'bd03', 'sY20', 'fi22', 'bl0', 'bd11', 'bd12', 'bd13', 'bd10', 'sY21',
+    'fi23', 'sY23', 'bo0', 'pw20', 'sY22', 'bl1', 'pw21', 'pw23', 'sD20', 'bu0',
+    'sD23', 'pw22', 'sD21', 'sD22', 'gw1', 'bo1', 'bd20', 'gw2', 'bd23', 'bi00',
+    'sN00', 'bd21', 'bd22', 'gsa', 'gw3', 'bi01', 'bl2', 'bu1', 'gw4', 'sN01',
+    'gsb', 'gw5', 'bo2', 'bi10', 'sN10', 'gw6', 'pj1', 'gs1', 'gs20', 'gs21',
+    'bi11', 'bu2', 'gs300', 'gw7', 'sN11', 'gs61', 'pj2', 'gs60', 'bi20', 'gs310',
+    'gs400', 'gs313', 'bi21', 'fn10', 'fn11', 'sN21', 'gs303', 'gs311', 'gs312', 'gs302',
+    'gs403', 'gs301', 'gs410', 'fn01', 'sN20', 'gs402', 'gs413', 'fn21', 'gs401', 'gw8',
+    'gs412', 'gs503', 'fn00', 'gs411', 'end', 'gs501', 'fn20', 'gs513', 'gs510', 'gs500',
+    'gs512', 'gs502', 'gs511',
 ))
 
 
@@ -113,8 +113,8 @@
                  dout, gs_out, gin_out, gout_out, loss_out,
                  leg_p, leg_q, lat, w1, w2, f_tab, g_tab, ft_tab, gt_tab,
                  xh, th, pk, rows, yrow, hy,
-                 xs, sr, dsr, ys, yr, dyr, als, ar, dar, bs, br, dbr, asave, dsave, aall, dall,
-                 st_s, st_h, st_m, st_w, tab_s, tab_w, tab, down_p, down_q, up_p, up_q, ker,
+                 xs, sr, dsr, ys, yr, dyr, als, ar, dar, bs, br, dbr, asave, dsave, aall, dall, mix,
+                 st_s, st_h, st_m, st_w, tab_s, tab_w, tab, turned, down_p, down_q, up_p, up_q, ker,
                  gw, gw_p, gw_a, gw_z, gw_zs, gw_h, gw_hs, gw_w, gw_ws, gw_w2, gw_h2, gw_f, gw_o,
                  ls, ls_p, ls_a, ls_z, ls_zs, ls_h, ls_hs, ls_w, gs_acc, gs_sum0, gs_sum1, gs_b0, gs_b1,
                  sem_x, sem_y, sem_d, sem_n, sem_s, sem_ds, sem_u, sem_du, sem_a, sem_da, sem_b, sem_db, sem_az, sem_dz,
@@ -125,7 +125,6 @@
     me = h * w_size + w
     nb, nt, npl, nc = x.shape
     ntp = nt // 2
-    part = ntp // PARTS
     nlon = npl * w_size
     nlat = nt * h_size
     nl = als.shape[1] // 8
@@ -184,79 +183,108 @@
         lax.fori_loop(1, size, body, 0)
         unsent.setdefault(key, []).append(lambda: drain(sent, sems.at[0]))
 
-    def some(refs, sems, low_h, high_h, count, counts, key):
-        src, dst = refs(h, w)
-        keep(src, dst, sems)
-
-        def one(h2, k):
-            w2_ = (w + k) % w_size
-            src, dst = refs(h2, w2_)
-            push(src, dst, sems, {"h": h2, "w": w2_})
-
-        for k in range(1, w_size):
-            one(h, k)
-
-        def body(h2, _):
-            for k in range(w_size):
-                one(h2, k)
-            return 0
-
-        lax.fori_loop(low_h, high_h, body, 0)
-        unsent.setdefault(key, []).append(lambda: take(sems.at[0], count - 1, [n - 1 for n in counts]))
-
     def take(sem, count, counts):
         for n in counts:
             @pl.when(count == n)
             def _():
-                drain(als.at[0, pl.ds(0, n * piece)], sem)
-
-    n_orders, n_owners = (h + 1) * w_size, (h_size - h) * w_size
-    counts = [w_size * n for n in range(1, h_size + 1)]
-    pairs = lambda k: pl.ds(k * part, part)
-
-    def at_rows(i, k):
-        return pl.ds(pl.multiple_of(i * 16 * ntp + k * 16 * part, 16 * part), 16 * part)
+                drain(als.at[0, pl.ds(0, n * 8)], sem)
+
+    n_groups = 2 * h_size
+    reach = ((me + 1) * l_own + 3) // 4
+    last = n_groups - 1
+    low_owner = (4 * h // l_own, 4 * (last - h) // l_own)
+    both_mine = last - h < reach
+    n_met = 2 * ndev - 4 * last // l_own
+    reaches = [(n, ((n + 1) * l_own + 3) // 4) for n in range(ndev)]
+    back_counts = sorted({r * w_size - 1 - int(last - n // w_size < r) for n, r in reaches})
+    pairs = lambda k, parts: pl.ds(k * (ntp // parts), ntp // parts)
+
+    def at_rows(i, k, parts):
+        size = 16 * ntp // parts
+        return pl.ds(pl.multiple_of(i * 16 * ntp + k * size, size), size)
 
     def send_home_rows(b, k, sem, name):
-        along("w", lambda o: (pk.at[b, o, pairs(k)], rows.at[b, pairs(k), rows_at(w, npl)]), sem.at[b, k],
-              pk.at[b, pl.ds(0, w_size - 1), pairs(k)], ("pk", b, k))
-        coming[name, b, k] = lambda: drain(rows.at[b, pairs(k)], sem.at[b, k, 1])
-
-    def send_rows_home(b, k, sem, name):
-        along("w", lambda o: (yrow.at[b, o, pairs(k)], hy.at[b, w, pairs(k)]), sem.at[b, k],
-              yrow.at[b, pl.ds(0, w_size - 1), pairs(k)], ("yrow", b, k))
-        coming[name, b, k] = lambda: drain(hy.at[b, :, pairs(k)], sem.at[b, k, 1])
+        along("w", lambda o: (pk.at[b, o, pairs(k, PARTS)], rows.at[b, pairs(k, PARTS), rows_at(w, npl)]), sem.at[b, k],
+              pk.at[b, pl.ds(0, w_size - 1), pairs(k, PARTS)], ("pk", b, k))
+        coming[name, b, k] = lambda: drain(rows.at[b, pairs(k, PARTS)], sem.at[b, k, 1])
+
+    def send_rows_home(b, k, sem, name, parts):
+        along("w", lambda o: (yrow.at[b, o, pairs(k, parts)], hy.at[b, w, pairs(k, parts)]), sem.at[b, k],
+              yrow.at[b, pl.ds(0, w_size - 1), pairs(k, parts)], (name, "row", b, k))
+        coming[name, b, k] = lambda: drain(hy.at[b, :, pairs(k, parts)], sem.at[b, k, 1])
 
     def send_orders(b, k, dst, sem, name):
-        along("h", lambda o: (xs.at[b, o, at_rows(0, k)], dst.at[b, at_rows(h, k)]), sem.at[b, k],
-              xs.at[b, pl.ds(0, h_size - 1), at_rows(0, k)], ("xs", b, k))
-        coming[name, b, k] = lambda: drain(xs.at[b, :, at_rows(0, k)], sem.at[b, k, 1])
-
-    def send_lats(b, dst, sem, name):
+        along("h", lambda o: (xs.at[b, o, at_rows(0, k, PARTS)], dst.at[b, at_rows(h, k, PARTS)]), sem.at[b, k],
+              xs.at[b, pl.ds(0, h_size - 1), at_rows(0, k, PARTS)], ("xs", b, k))
+        coming[name, b, k] = lambda: drain(xs.at[b, :, at_rows(0, k, PARTS)], sem.at[b, k, 1])
+
+    def send_lats(b, dst, sem, name, parts):
         def one(k, _):
-            keep(ys.at[b, at_rows(h, k)], dst.at[b, h, at_rows(0, k)], sem.at[b, k])
+            keep(ys.at[b, at_rows(h, k, parts)], dst.at[b, h, at_rows(0, k, parts)], sem.at[b, k])
 
             def body(j, _):
                 o = (h + j) % h_size
-                push(ys.at[b, at_rows(o, k)], dst.at[b, h, at_rows(0, k)], sem.at[b, k], {"h": o})
+                push(ys.at[b, at_rows(o, k, parts)], dst.at[b, h, at_rows(0, k, parts)], sem.at[b, k], {"h": o})
                 return 0
 
             return lax.fori_loop(1, h_size, body, 0)
 
-        lax.fori_loop(0, PARTS, one, 0)
-        for k in range(PARTS):
-            unsent.setdefault(("ys", b), []).append(lambda k=k: drain(xs.at[b, pl.ds(0, h_size - 1), at_rows(0, k)], sem.at[b, k, 0]))
-            coming[name, b, k] = lambda k=k: drain(dst.at[b, :, at_rows(0, k)], sem.at[b, k, 1])
+        lax.fori_loop(0, parts, one, 0)
+        for k in range(parts):
+            unsent.setdefault(("ys", b), []).append(lambda k=k: drain(xs.at[b, pl.ds(0, h_size - 1), at_rows(0, k, parts)], sem.at[b, k, 0]))
+            coming[name, b, k] = lambda k=k: drain(dst.at[b, :, at_rows(0, k, parts)], sem.at[b, k, 1])
 
     def send_owner(b, dst, sem, name):
-        some(lambda h2, w2_: (als.at[b, rows_at(h2 * w_size + w2_, piece)], dst.at[b, h, :, lanes_at(w)]), sem.at[b],
-             h + 1, h_size, n_owners, counts, ("als", b))
-        coming[name, b] = lambda: take(sem.at[b, 1], n_orders, counts)
+        sems = sem.at[b]
+        for g in range(2):
+            tile = lambda lin, g=g: (als.at[b, rows_at(lin * 2 + g, 8)], dst.at[b, h, pl.ds(g * 8, 8), lanes_at(w)])
+
+            def body(n, _, g=g, tile=tile):
+                lin = low_owner[g] + (n + me) % (ndev - low_owner[g])
+
+                @pl.when(lin != me)
+                def _():
+                    push(*tile(lin), sems, {"h": lin // w_size, "w": lin % w_size})
+                return 0
+
+            if g == 0:
+                keep(*tile(me), sems)
+            else:
+                @pl.when(both_mine)
+                def _():
+                    keep(*tile(me), sems)
+            lax.fori_loop(0, ndev - low_owner[g], body, 0)
+        unsent.setdefault(("als", b), []).append(lambda: take(sems.at[0], n_met - 1 - jnp.where(both_mine, 1, 0), [n_met - 1, n_met - 2]))
+        coming[name, b] = lambda: take(sems.at[1], reach * w_size, [n * w_size for n in range(1, n_groups + 1)])
 
     def send_back(b, dst, sem, name):
-        some(lambda h2, w2_: (bs.at[b, h2, w2_], dst.at[b, rows_at(me, piece)]), sem.at[b],
-             0, h, n_orders, counts, ("bs", b))
-        coming[name, b] = lambda: take(sem.at[b, 1], n_owners, counts)
+        sems = sem.at[b]
+        tile = lambda h2, w2_, g: (bs.at[b, h2, w2_, rows_at(g, 8)], dst.at[b, rows_at(me * 2 + g, 8)])
+
+        def body(n, _):
+            g = n // h_size
+            h2 = jnp.where(g == 0, n, last - n)
+            for k in range(w_size):
+                w2_ = (w + k) % w_size
+                if k:
+                    push(*tile(h2, w2_, g), sems, {"h": h2, "w": w2_})
+                else:
+                    @pl.when(h2 != h)
+                    def _():
+                        push(*tile(h2, w2_, g), sems, {"h": h2, "w": w2_})
+            return 0
+
+        keep(*tile(h, w, 0), sems)
+
+        @pl.when(both_mine)
+        def _():
+            keep(*tile(h, w, 1), sems)
+
+        lax.fori_loop(0, reach, body, 0)
+        count = reach * w_size - 1 - jnp.where(both_mine, 1, 0)
+        unsent.setdefault(("bs", b), []).append(
+            lambda: take(sems.at[0], count, back_counts))
+        coming[name, b] = lambda: drain(als.at[0, pl.ds(0, n_met * 8)], sems.at[1])
 
     def dft(b, k, table):
         settle(("xs", b, k))
@@ -269,10 +297,10 @@
             xs[b, :, rows_at(i + 1, 16), :] = out[:, :, LANES:]
             return 0
 
-        lax.fori_loop(k * part // 2, (k + 1) * part // 2, body, 0)
-
-    def idft(b, k, table, src):
-        settle(("yrow", b, k))
+        lax.fori_loop(k * ntp // PARTS // 2, (k + 1) * ntp // PARTS // 2, body, 0)
+
+    def idft(b, k, table, src, parts):
+        settle(*(("y", "row", b, j) for j in range(PARTS * k // parts, PARTS * (k + 1) // parts)))
 
         def body(n, _):
             i = 2 * n
@@ -282,7 +310,7 @@
                 yrow[b, :, i + j] = out[:, j * LANES:(j + 1) * LANES].reshape(w_size, npl, LANES)
             return 0
 
-        lax.fori_loop(k * part // 2, (k + 1) * part // 2, body, 0)
+        lax.fori_loop(k * ntp // parts // 2, (k + 1) * ntp // parts // 2, body, 0)
 
     def level(v, here):
         mean = jnp.mean(v, axis=0, keepdims=True)
@@ -292,7 +320,7 @@
     def orders(body):
         def four(n, _):
             for i in range(4):
-                body(4 * n + i, n == 0 if i == 0 else None)
+                body(4 * n + i, n == 0 if i == 0 else None, [pl.ds(8 * n + 4 * l + i, nl // 2, stride=16) for l in range(2)])
             return 0
 
         lax.fori_loop(0, 2, four, 0)
@@ -300,19 +328,21 @@
     def leg_down(b, table, src, fix):
         settle(("als", b))
 
-        def one(m, here):
+        def one(m, here, at):
             re, im = (src[b, pl.ds(ri * 8 + m, ntp * h_size, stride=16), :] for ri in range(2))
             if fix and here is not None:
                 re = level(re, here)
-            als[b, pl.ds(m, nl, stride=8), :] = dot(table[m], jnp.concatenate(weave(re, im), axis=0))
+            out = dot(table[m], jnp.concatenate(weave(re, im), axis=0))
+            for l in range(2):
+                als[b, at[l], :] = out[l * (nl // 2):(l + 1) * (nl // 2)]
 
         orders(one)
 
     def leg_up(b, table, src, fix):
         settle(("ys", b))
 
-        def one(m, here):
-            out = dot(table[m], src[b, pl.ds(m, nl, stride=8), :])
+        def one(m, here, at):
+            out = dot(table[m], jnp.concatenate([src[b, at[l], :] for l in range(2)], axis=0))
             re, im = weave(out[:nlat // 2], out[nlat // 2:])
             if fix and here is not None:
                 re = level(re, here)
@@ -321,13 +351,28 @@
 
         orders(one)
 
-    def owned(b, l, src):
-        tiles = [src[b, :, rows_at(l, 8), j * LANES:(j + 1) * LANES].reshape(-1, LANES) for j in range(w_size)]
-        return weave_wide(tiles)
-
-    def put_back(b, l, re, im):
+    def halves(a, b):
+        upper = lax.broadcasted_iota(jnp.int32, a.shape, 1) < 4
+        turn = lambda v: jnp.concatenate([v[:, 4:], v[:, :4]], axis=1)
+        return jnp.where(upper, a, turn(b)), jnp.where(upper, turn(a), b)
+
+    def take_in(b, src):
+        for j in range(w_size):
+            lanes = slice(j * LANES, (j + 1) * LANES)
+            for l, v in enumerate(halves(src[b, :, :8, lanes], src[b, :, 8:, lanes])):
+                mix[l, j] = v.reshape(-1, LANES)
+
+    def give_out(b):
+        for j in range(w_size):
+            for g, v in enumerate(halves(*(mix[l, j].reshape(h_size, 8, LANES) for l in range(2)))):
+                bs[b, :, j, g * 8:(g + 1) * 8, :] = v
+
+    def owned(l):
+        return weave_wide([mix[l, j] for j in range(w_size)])
+
+    def put_back(l, re, im):
         for j, tile in enumerate(weave_tiles(re, im)):
-            bs[b, :, j, rows_at(l, 8), :] = tile.reshape(h_size, 8, LANES)
+            mix[l, j] = tile
 
     def put_rows(b, i, v0, v1):
         for j, tile in enumerate(weave_tiles(v0, v1)):
@@ -414,8 +459,16 @@
 
     def table_out(a):
         got(("tab1", a))
-        along("h", lambda o: (tab_w.at[a, o // 2, rows_at(o % 2, 4)], tab.at[a, :, rows_at(h, nt)]), sem_tab.at[3 + a],
-              tab.at[a, :, pl.ds(0, nlat - nt)])
+        shards = w_size
+        for g in range(2):
+            def refs(o, g=g):
+                group = o if g == 0 else last - o
+                return tab_w.at[a, group // shards, rows_at(group % shards, 2)], tab.at[a, pl.ds(2 * g, 2), rows_at(h, nt)]
+
+            along("h", refs, sem_tab.at[3 + a], tab.at[a, pl.ds(0, 2), pl.ds(0, nlat - nt)], ("table", a, g))
+        for g in range(2):
+            unsent.pop(("table", a, g))
+        unsent.setdefault(None, []).append(lambda: drain(tab.at[a, :, pl.ds(0, nlat - nt)], sem_tab.at[3 + a, 0]))
         coming["tab2", a] = lambda: drain(tab.at[a], sem_tab.at[3 + a, 1])
 
     def table_in(a, down, up):
@@ -425,9 +478,10 @@
             both = tab[a, n].reshape(h_size, 2, ntp, 2 * nl)
             both = jnp.concatenate([both[:, j].reshape(-1, 2 * nl) for j in range(2)], axis=0)
             for j in range(2):
-                t = both[:, j * nl:(j + 1) * nl]
-                up[2 * n + j] = t
-                down[2 * n + j] = t.T
+                turned[...] = both[:, j * nl:(j + 1) * nl].T
+                t = jnp.concatenate([turned[pl.ds(l, nl // 2, stride=2), :] for l in range(2)], axis=0)
+                down[2 * n + j] = t
+                up[2 * n + j] = t.T
             return 0
 
         lax.fori_loop(0, tab.shape[1], body, 0)
@@ -466,15 +520,17 @@
         settle(("bs", b))
 
         def one(l, _):
-            re, im = owned(b, l, ar)
+            re, im = owned(l)
             a = jnp.concatenate([re, im], axis=0) * scales[b]
             asave[b, l] = a
             n = a.shape[0] // 2
             own, other = dot(a, ker[0, l]), dot(a, ker[1, l])
-            put_back(b, l, own[:n] - other[n:], own[n:] + other[:n])
+            put_back(l, own[:n] - other[n:], own[n:] + other[:n])
             return 0
 
+        take_in(b, ar)
         lax.fori_loop(0, l_own, one, 0)
+        give_out(b)
         send_back(b, br, sem_b, "b")
         along("dp", lambda o: (asave.at[b, o // 2], aall.at[dp, b]), sem_az.at[b], aall.at[pl.ds(0, dp_size - 1), b])
         coming["az", b] = lambda: drain(aall.at[:, b], sem_az.at[b, 1])
@@ -482,14 +538,14 @@
     def fu(b):
         got(("b", b))
         leg_up(b, up_q, br, False)
-        send_lats(b, yr, sem_u, "u")
+        send_lats(b, yr, sem_u, "u", PARTS)
 
     def fi(b, k):
         got(("u", b, k))
-        idft(b, k, gt_tab, yr)
+        idft(b, k, gt_tab, yr, PARTS)
 
     def sY(b, k):
-        send_rows_home(b, k, sem_y, "y")
+        send_rows_home(b, k, sem_y, "y", PARTS)
 
     def pw(b, k):
         got(("y", b, k))
@@ -526,7 +582,7 @@
             put_rows(b, n, dy[:npl], dy[npl:])
             return 0
 
-        lax.fori_loop(k * part, (k + 1) * part, body, 0)
+        lax.fori_loop(k * ntp // PARTS, (k + 1) * ntp // PARTS, body, 0)
 
     def sD(b, k):
         send_home_rows(b, k, sem_d, "d")
@@ -547,16 +603,18 @@
         settle(("bs", b), "st")
 
         def one(l, s2):
-            re, im = owned(b, l, dar)
+            re, im = owned(l)
             d = jnp.concatenate([re, im], axis=0)
             dsave[b, l] = d
             n = d.shape[0] // 2
             own, other = dot(d, ker[0, l], NT), dot(d, ker[1, l], NT)
             re, im = own[:n] + other[n:], own[n:] - other[:n]
-            put_back(b, l, re, im)
+            put_back(l, re, im)
             return s2 + jnp.sum(re * asave[b, l, :n] + im * asave[b, l, n:], axis=0, keepdims=True)
 
+        take_in(b, dar)
         s2 = lax.fori_loop(0, l_own, one, jnp.zeros((1, nc), F32))
+        give_out(b)
         send_back(b, dbr, sem_db, "db")
         along("dp", lambda o: (dsave.at[b, o // 2, :, lanes_at(o % 2)], dall.at[dp, b]), sem_dz.at[b], dall.at[pl.ds(0, dp_size - 1), b])
         coming["dz", b] = lambda: drain(dall.at[:, b], sem_dz.at[b, 1])
@@ -565,14 +623,14 @@
     def bu(b):
         got(("db", b))
         leg_up(b, up_p, dbr, True)
-        send_lats(b, dyr, sem_du, "du")
+        send_lats(b, dyr, sem_du, "du", N_PARTS)
 
     def bi(b, k):
         got(("du", b, k))
-        idft(b, k, ft_tab, dyr)
+        idft(b, k, ft_tab, dyr, N_PARTS)
 
     def sN(b, k):
-        send_rows_home(b, k, sem_n, "n")
+        send_rows_home(b, k, sem_n, "n", N_PARTS)
 
     def pj1():
         st_s[nb:, :] = jnp.zeros_like(st_s[nb:, :])
@@ -599,7 +657,7 @@
                 dout[b, t] = dout[b, t] + scales[b] * (dn - normed * proj[0][b:b + 1])
             return 0
 
-        lax.fori_loop(k * part, (k + 1) * part, body, 0)
+        lax.fori_loop(k * ntp // N_PARTS, (k + 1) * ntp // N_PARTS, body, 0)
 
     n_c, n_z, n_h, n_w = gw_a.shape[0], gw_zs.shape[0], gw_hs.shape[0], gw_ws.shape[0]
     chip, core = h // 2, h % 2
@@ -840,9 +898,9 @@
                 home, home, woven, vm(nb, ntp, nlon, LANES), woven, woven,
                 vm(nb, h_size, 16 * ntp, LANES), order, order, order, vm(nb, h_size, 16 * ntp, LANES), vm(nb, h_size, 16 * ntp, LANES),
                 degree, owner, owner, vm(nb, h_size, w_size, 8 * lo, LANES), degree, degree, saved, saved,
-                vm(dp_size, nb, 2 * nm, nc), vm(dp_size, nb, 2 * nm, LANES),
+                vm(dp_size, nb, 2 * nm, nc), vm(dp_size, nb, 2 * nm, LANES), vm(lo, w_size, nm, LANES),
                 vm(8, nc), vm(h_size, 8, nc), vm(8, nc), vm(w_size, 8, nc),
-                vm(2, n_pairs, nt, 2 * nl), vm(2, w_size, n_pairs, nt, 2 * nl), vm(2, 4, nlat, 2 * nl),
+                vm(2, n_pairs, nt, 2 * nl), vm(2, w_size, n_pairs, nt, 2 * nl), vm(2, 4, nlat, 2 * nl), vm(nl, nlat),
                 vm(8, nl, nlat), vm(8, nl, nlat), vm(8, nlat, nl), vm(8, nlat, nl),
                 vm(2, lo, nc, nc),
                 vm(n_rows, nc), vm(n_c, nc), vm(n_c, nc), vm(dp_size, n_z, nc), vm(n_z, nc), vm(w_size, n_h, nc), vm(n_h, nc),

time: 205 us -> 206 us (level)
  no operation moved by 1% of the time
where the time goes in v13:
time: 206 us; the launch traced here: 205 us
  Pallas kernels  203 us (99%)
  between operations  2.41 us (1%)
    pallas_call x1, Pallas kernels, local_step(): pl.pallas_call(functools.partial(block_kernel, (dp_size, h_size, w_size),...  199 us

profile of v13, /device:TPU:1, one launch (start us, length us, event | category | flops | bytes accessed | tf_op | source)
XLA Modules:
  0.0 205.4 jit_solution(6901298786152370421)
XLA Ops:
  0.6 199.4 %block.1 = (f32[3,16,64,256]{3,2,1,0:T(8,128)S(1)}, f32[2,8,256,256]{3,2,1,0:T(8,128)S(1)}, f32[256,512]{1,0:T(8,128)S(1)}, f32[512,256]{1,0:T(8,128)S(1)}, f32[1,1]{1,0:T(1,128)}) custom-call(f32[3,16,64,256]{3,2,1,0:T(8,128)} %bitcast.6, f32[3,16,64,256]{3,2,1,0:T(8,128)} %bitcast.7, f32[16,16,64]{2,1,0:T(8,128)} %bitcast.8, f32[16,16,64]{2,1,0:T(8,128)} %bitcast.9, ...), custom_call_target="tpu_custom_call" | custom-call | tf_op jit(solution)/shard_map/block/pallas_call | solution.py:889
  200.1 3.6 %hand_on.1 = (f32[3,16,64,256]{3,2,1,0:T(8,128)}, f32[2,8,256,256]{3,2,1,0:T(8,128)}, f32[256,512]{1,0:T(8,128)}, f32[512,256]{1,0:T(8,128)}) custom-call(f32[3,16,64,256]{3,2,1,0:T(8,128)S(1)} %get-tuple-element.15.refs_0_, f32[2,8,256,256]{3,2,1,0:T(8,128)S(1)} %get-tuple-element.16.refs_1_, f32[256,512]{1,0:T(8,128)S(1)} %get-tuple-element.17.refs_2_, ...), custom_call_target="tpu_custom_call" | custom-call | tf_op jit(solution)/shard_map/hand_on/pallas_call | solution.py:849

commit v14 on v13

--- a/solution.py
+++ b/solution.py
@@ -87,24 +87,24 @@
 GS_ROWS = 176
 GS_FIRST = (0, 1, 2)
 ORDER = " ".join((
-    'go', 'pk0', 'sX03', 'pk2', 'sX00', 'pk1', 'sX02', 'tb1', 'sX01', 'st1',
-    'sX11', 'fd03', 'fd00', 'sX10', 'tb2', 'fd01', 'fd02', 'tb4', 'sX12', 'tb3',
-    'st2', 'sX13', 'fd10', 'fl0', 'sX21', 'fd12', 'fd13', 'fd11', 'tb5', 'sX23',
-    'fo0', 'fl1', 'sX20', 'sX22', 'fu0', 'fo1', 'fi00', 'sY00', 'fd23', 'fi01',
-    'fd21', 'sY01', 'fd22', 'fi02', 'sY02', 'fd20', 'pw00', 'fi03', 'sY03', 'fu1',
-    'pw01', 'sD01', 'fl2', 'sD00', 'fi12', 'fi10', 'pw02', 'sY12', 'bd01', 'sY10',
-    'fi11', 'fi13', 'fo2', 'sY11', 'pw03', 'sY13', 'pw12', 'sD03', 'sD02', 'fu2',
-    'bd00', 'pw10', 'pw13', 'fi20', 'sD10', 'sD12', 'fi21', 'pw11', 'sD13', 'sD11',
-    'bd02', 'bd03', 'sY20', 'fi22', 'bl0', 'bd11', 'bd12', 'bd13', 'bd10', 'sY21',
-    'fi23', 'sY23', 'bo0', 'pw20', 'sY22', 'bl1', 'pw21', 'pw23', 'sD20', 'bu0',
-    'sD23', 'pw22', 'sD21', 'sD22', 'gw1', 'bo1', 'bd20', 'gw2', 'bd23', 'bi00',
-    'sN00', 'bd21', 'bd22', 'gsa', 'gw3', 'bi01', 'bl2', 'bu1', 'gw4', 'sN01',
-    'gsb', 'gw5', 'bo2', 'bi10', 'sN10', 'gw6', 'pj1', 'gs1', 'gs20', 'gs21',
-    'bi11', 'bu2', 'gs300', 'gw7', 'sN11', 'gs61', 'pj2', 'gs60', 'bi20', 'gs310',
-    'gs400', 'gs313', 'bi21', 'fn10', 'fn11', 'sN21', 'gs303', 'gs311', 'gs312', 'gs302',
-    'gs403', 'gs301', 'gs410', 'fn01', 'sN20', 'gs402', 'gs413', 'fn21', 'gs401', 'gw8',
-    'gs412', 'gs503', 'fn00', 'gs411', 'end', 'gs501', 'fn20', 'gs513', 'gs510', 'gs500',
-    'gs512', 'gs502', 'gs511',
+    'pk1', 'pk0', 'go', 'sX03', 'pk2', 'sX02', 'sX01', 'st1', 'tb1', 'fd03',
+    'sX00', 'sX11', 'tb2', 'sX13', 'fd02', 'sX12', 'st2', 'fd01', 'fd00', 'tb3',
+    'fd11', 'sX10', 'tb4', 'fl0', 'fd13', 'sX21', 'fd10', 'tb5', 'sX23', 'fd12',
+    'fo0', 'fl1', 'sX22', 'fu0', 'sX20', 'fo1', 'fi00', 'sY00', 'fi01', 'fd20',
+    'sY01', 'fi02', 'fi03', 'fd21', 'sY03', 'fd23', 'pw00', 'fd22', 'sY02', 'fu1',
+    'sD00', 'fi10', 'sY10', 'fi11', 'fl2', 'fi12', 'pw03', 'sY11', 'pw01', 'fi13',
+    'sY13', 'pw02', 'fo2', 'sD02', 'pw11', 'sY12', 'sD03', 'sD01', 'pw13', 'pw10',
+    'fu2', 'sD13', 'sD11', 'bd00', 'bd03', 'pw12', 'fi22', 'sD12', 'fi20', 'bd02',
+    'sY20', 'bd01', 'bl0', 'fi23', 'fi21', 'bd12', 'sD10', 'pw20', 'bd11', 'sY22',
+    'bd13', 'sY21', 'bo0', 'sY23', 'sD20', 'bd10', 'pw22', 'pw21', 'bl1', 'bu0',
+    'pw23', 'sD23', 'gw1', 'sD22', 'bd20', 'gsa', 'sD21', 'gw2', 'bo1', 'bi01',
+    'bd23', 'bd22', 'sN01', 'bd21', 'gw3', 'gsb', 'bi00', 'bl2', 'gw4', 'bu1',
+    'sN00', 'gw5', 'bo2', 'bi10', 'sN10', 'gs1', 'pj1', 'gs20', 'gs21', 'gs300',
+    'gs310', 'bu2', 'gs311', 'bi11', 'gs303', 'gs61', 'gs60', 'bi20', 'gw6', 'sN20',
+    'gs301', 'pj2', 'gs410', 'fn10', 'gw7', 'fn01', 'gs400', 'sN11', 'gs312', 'gs302',
+    'gs403', 'gs411', 'bi21', 'gs401', 'gs313', 'sN21', 'fn20', 'gs511', 'gs413', 'fn11',
+    'fn00', 'gs412', 'gs402', 'gw8', 'fn21', 'gs510', 'gs500', 'end', 'gs502', 'gs513',
+    'gs501', 'gs503', 'gs512',
 ))
 
 
@@ -190,13 +190,14 @@
                 drain(als.at[0, pl.ds(0, n * 8)], sem)
 
     n_groups = 2 * h_size
-    reach = ((me + 1) * l_own + 3) // 4
     last = n_groups - 1
-    low_owner = (4 * h // l_own, 4 * (last - h) // l_own)
+    reach = 2 * h + 2
+    low_h = (h // 2, (last - h) // 2)
     both_mine = last - h < reach
-    n_met = 2 * ndev - 4 * last // l_own
-    reaches = [(n, ((n + 1) * l_own + 3) // 4) for n in range(ndev)]
-    back_counts = sorted({r * w_size - 1 - int(last - n // w_size < r) for n, r in reaches})
+    n_met = (h_size + 1) * w_size
+    assert l_own * w_size == 8 and all(2 * h_size - i // 2 - (last - i) // 2 == h_size + 1 for i in range(h_size))
+    counts = [(2 * i + 2) * w_size for i in range(h_size)]
+    back_counts = [n - 1 - int(last - i < 2 * i + 2) for i, n in enumerate(counts)]
     pairs = lambda k, parts: pl.ds(k * (ntp // parts), ntp // parts)
 
     def at_rows(i, k, parts):
@@ -237,25 +238,28 @@
     def send_owner(b, dst, sem, name):
         sems = sem.at[b]
         for g in range(2):
-            tile = lambda lin, g=g: (als.at[b, rows_at(lin * 2 + g, 8)], dst.at[b, h, pl.ds(g * 8, 8), lanes_at(w)])
-
-            def body(n, _, g=g, tile=tile):
-                lin = low_owner[g] + (n + me) % (ndev - low_owner[g])
-
-                @pl.when(lin != me)
-                def _():
-                    push(*tile(lin), sems, {"h": lin // w_size, "w": lin % w_size})
+            tile = lambda h2, w2_, g=g: (als.at[b, rows_at((h2 * w_size + w2_) * 2 + g, 8)], dst.at[b, h, pl.ds(g * 8, 8), lanes_at(w)])
+
+            def body(h2, _, tile=tile):
+                for k in range(w_size):
+                    w2_ = (w + k) % w_size
+                    if k:
+                        push(*tile(h2, w2_), sems, {"h": h2, "w": w2_})
+                    else:
+                        @pl.when(h2 != h)
+                        def _():
+                            push(*tile(h2, w2_), sems, {"h": h2, "w": w2_})
                 return 0
 
             if g == 0:
-                keep(*tile(me), sems)
+                keep(*tile(h, w), sems)
             else:
                 @pl.when(both_mine)
                 def _():
-                    keep(*tile(me), sems)
-            lax.fori_loop(0, ndev - low_owner[g], body, 0)
+                    keep(*tile(h, w), sems)
+            lax.fori_loop(low_h[g], h_size, body, 0)
         unsent.setdefault(("als", b), []).append(lambda: take(sems.at[0], n_met - 1 - jnp.where(both_mine, 1, 0), [n_met - 1, n_met - 2]))
-        coming[name, b] = lambda: take(sems.at[1], reach * w_size, [n * w_size for n in range(1, n_groups + 1)])
+        coming[name, b] = lambda: take(sems.at[1], reach * w_size, counts)
 
     def send_back(b, dst, sem, name):
         sems = sem.at[b]

time: 206 us -> 207 us (level)
  no operation moved by 1% of the time
where the time goes in v14:
time: 207 us
  Pallas kernels  204 us (99%)
  between operations  2.41 us (1%)
    pallas_call x1, Pallas kernels, local_step(): pl.pallas_call(functools.partial(block_kernel, (dp_size, h_size, w_size),...  201 us

profile of v14, /device:TPU:1, one launch (start us, length us, event | category | flops | bytes accessed | tf_op | source)
XLA Modules:
  0.0 206.6 jit_solution(1406500380222297802)
XLA Ops:
  0.6 200.6 %block.1 = (f32[3,16,64,256]{3,2,1,0:T(8,128)S(1)}, f32[2,8,256,256]{3,2,1,0:T(8,128)S(1)}, f32[256,512]{1,0:T(8,128)S(1)}, f32[512,256]{1,0:T(8,128)S(1)}, f32[1,1]{1,0:T(1,128)}) custom-call(f32[3,16,64,256]{3,2,1,0:T(8,128)} %bitcast.6, f32[3,16,64,256]{3,2,1,0:T(8,128)} %bitcast.7, f32[16,16,64]{2,1,0:T(8,128)} %bitcast.8, f32[16,16,64]{2,1,0:T(8,128)} %bitcast.9, ...), custom_call_target="tpu_custom_call" | custom-call | tf_op jit(solution)/shard_map/block/pallas_call | solution.py:893
  201.2 3.6 %hand_on.1 = (f32[3,16,64,256]{3,2,1,0:T(8,128)}, f32[2,8,256,256]{3,2,1,0:T(8,128)}, f32[256,512]{1,0:T(8,128)}, f32[512,256]{1,0:T(8,128)}) custom-call(f32[3,16,64,256]{3,2,1,0:T(8,128)S(1)} %get-tuple-element.15.refs_0_, f32[2,8,256,256]{3,2,1,0:T(8,128)S(1)} %get-tuple-element.16.refs_1_, f32[256,512]{1,0:T(8,128)S(1)} %get-tuple-element.17.refs_2_, ...), custom_call_target="tpu_custom_call" | custom-call | tf_op jit(solution)/shard_map/hand_on/pallas_call | solution.py:853

commit v15 on v12

--- a/solution.py
+++ b/solution.py
@@ -85,26 +85,26 @@
 GS_ROWS = 176
 GS_FIRST = (0, 1, 2)
 ORDER = " ".join((
-    'pk0', 'pk1', 'go', 'sX03', 'sX01', 'pk2', 'tb1', 'sX00', 'sX02', 'sX11',
-    'sX10', 'fd03', 'sX13', 'tb2', 'fd00', 'fd01', 'fd02', 'tb3', 'st1', 'tb4',
-    'sX12', 'fd11', 'fl0', 'st2', 'fd13', 'fd10', 'sX20', 'fd12', 'sX22', 'tb5',
-    'fo0', 'sX23', 'fl1', 'fu0', 'fd23', 'sX21', 'fd22', 'fd20', 'fo1', 'fi00',
-    'sY00', 'fi02', 'sY02', 'fi01', 'fi03', 'fd21', 'sY03', 'pw00', 'sY01', 'pw02',
-    'sD02', 'fl2', 'fu1', 'pw03', 'sD03', 'pw01', 'sD00', 'fo2', 'fi11', 'sD01',
-    'sY11', 'fi12', 'sY12', 'fi13', 'fi10', 'sY10', 'bd00', 'bd02', 'bd03', 'bd01',
-    'sY13', 'fu2', 'bl0', 'fi21', 'sY21', 'fi22', 'pw10', 'pw13', 'sY22', 'pw11',
-    'pw12', 'sD10', 'bo0', 'fi20', 'sD12', 'pw21', 'fi23', 'sY23', 'pw22', 'bd10',
-    'sD11', 'sY20', 'bu0', 'pw23', 'sD13', 'bi00', 'bd11', 'sD23', 'bd12', 'pw20',
-    'sD22', 'gw1', 'sD20', 'bi01', 'bd13', 'gw2', 'sD21', 'bd23', 'bi03', 'bi02',
-    'bl1', 'sN03', 'bd22', 'bd20', 'bd21', 'sN02', 'gw3', 'bo1', 'bl2', 'gw4',
-    'sN01', 'sN00', 'bu1', 'gw5', 'bo2', 'pj1', 'bi10', 'sN10', 'bi11', 'gsa',
-    'sN11', 'gsb', 'gs1', 'gs21', 'gs20', 'gw6', 'bi12', 'gs300', 'sN12', 'bu2',
-    'gs311', 'gs61', 'gs313', 'gs301', 'gw7', 'bi13', 'bi21', 'gs303', 'gs60', 'gs312',
-    'sN13', 'gs411', 'pj2', 'fn10', 'bi22', 'gs310', 'bi23', 'gs302', 'sN23', 'fn01',
-    'gw8', 'gs401', 'fn02', 'sN21', 'gs410', 'fn00', 'sN22', 'fn03', 'bi20', 'gs403',
-    'end', 'fn13', 'sN20', 'gs412', 'gs402', 'gs510', 'gs413', 'gs501', 'fn21', 'fn11',
-    'gs511', 'gs400', 'fn12', 'gs503', 'fn20', 'fn22', 'gs512', 'fn23', 'gs500', 'gs502',
-    'gs513',
+    'go', 'pk0', 'sX01', 'pk2', 'pk1', 'sX03', 'tb1', 'sX00', 'sX02', 'sX12',
+    'fd01', 'fd03', 'sX10', 'tb2', 'fd00', 'fd02', 'tb4', 'st1', 'sX11', 'sX13',
+    'tb3', 'fd12', 'fl0', 'st2', 'fd10', 'tb5', 'sX21', 'fd13', 'fd11', 'sX20',
+    'fo0', 'fl1', 'sX23', 'sX22', 'fd20', 'fu0', 'fo1', 'fd23', 'fd21', 'fi00',
+    'sY00', 'fi01', 'sY01', 'fi02', 'fd22', 'fi03', 'sY02', 'sY03', 'pw00', 'fu1',
+    'sD00', 'fl2', 'pw02', 'sD02', 'pw01', 'pw03', 'sD03', 'sD01', 'fi12', 'bd02',
+    'fi10', 'sY12', 'fi13', 'bd00', 'fo2', 'bd01', 'sY10', 'bd03', 'fi11', 'sY11',
+    'pw12', 'sY13', 'fu2', 'pw10', 'sD12', 'bl0', 'sD10', 'pw11', 'fi21', 'fi20',
+    'sY20', 'sY21', 'pw13', 'fi22', 'sD11', 'fi23', 'bd10', 'sD13', 'bo0', 'sY22',
+    'pw21', 'bd12', 'sY23', 'sD21', 'bd13', 'pw20', 'sD20', 'bd11', 'bu0', 'pw22',
+    'pw23', 'sD22', 'sD23', 'gw1', 'gsa', 'bd21', 'gw2', 'bl1', 'bi03', 'bi02',
+    'bd22', 'sN02', 'bi01', 'sN01', 'bd20', 'bd23', 'gw3', 'bo1', 'bl2', 'bi00',
+    'sN03', 'gw4', 'sN00', 'bu1', 'bo2', 'gw5', 'pj1', 'bi10', 'sN10', 'gsb',
+    'bi11', 'sN11', 'pj2', 'gs1', 'gs20', 'gs21', 'bi13', 'sN13', 'gs300', 'gw6',
+    'bu2', 'gs310', 'gs61', 'bi12', 'sN12', 'gs303', 'gw7', 'gs313', 'fn11', 'gs60',
+    'bi20', 'gs311', 'fn12', 'bi23', 'fn10', 'fn02', 'gs312', 'gs403', 'gs301', 'gs413',
+    'gs410', 'sN23', 'sN20', 'gs302', 'gs400', 'bi22', 'fn13', 'bi21', 'gw8', 'sN21',
+    'sN22', 'fn00', 'gs503', 'gs412', 'gs401', 'fn20', 'gs402', 'fn01', 'gs411', 'end',
+    'gs502', 'gs500', 'gs510', 'fn23', 'fn03', 'gs501', 'fn22', 'gs512', 'fn21', 'gs513',
+    'gs511',
 ))
 
 

time: 205 us -> 203 us (level)
    pallas_call x1, Pallas kernels: 199 us -> 196 us  [local_step(): pl.pallas_call(functools.partial(block_kernel, (dp_size, h_size, w_size),...]
where the time goes in v15:
time: 203 us; the launch traced here: 202 us
  Pallas kernels  200 us (99%)
  between operations  2.41 us (1%)
    pallas_call x1, Pallas kernels, local_step(): pl.pallas_call(functools.partial(block_kernel, (dp_size, h_size, w_size),...  196 us

profile of v15, /device:TPU:1, one launch (start us, length us, event | category | flops | bytes accessed | tf_op | source)
XLA Modules:
  0.0 202.4 jit_solution(1848788190562128719)
XLA Ops:
  0.6 196.4 %block.1 = (f32[3,16,64,256]{3,2,1,0:T(8,128)S(1)}, f32[2,8,256,256]{3,2,1,0:T(8,128)S(1)}, f32[256,512]{1,0:T(8,128)S(1)}, f32[512,256]{1,0:T(8,128)S(1)}, f32[1,1]{1,0:T(1,128)}) custom-call(f32[3,16,64,256]{3,2,1,0:T(8,128)} %bitcast.6, f32[3,16,64,256]{3,2,1,0:T(8,128)} %bitcast.7, f32[16,16,64]{2,1,0:T(8,128)} %bitcast.8, f32[16,16,64]{2,1,0:T(8,128)} %bitcast.9, ...), custom_call_target="tpu_custom_call" | custom-call | tf_op jit(solution)/shard_map/block/pallas_call | solution.py:831
  197.1 3.6 %hand_on.1 = (f32[3,16,64,256]{3,2,1,0:T(8,128)}, f32[2,8,256,256]{3,2,1,0:T(8,128)}, f32[256,512]{1,0:T(8,128)}, f32[512,256]{1,0:T(8,128)}) custom-call(f32[3,16,64,256]{3,2,1,0:T(8,128)S(1)} %get-tuple-element.15.refs_0_, f32[2,8,256,256]{3,2,1,0:T(8,128)S(1)} %get-tuple-element.16.refs_1_, f32[256,512]{1,0:T(8,128)S(1)} %get-tuple-element.17.refs_2_, ...), custom_call_target="tpu_custom_call" | custom-call | tf_op jit(solution)/shard_map/hand_on/pallas_call | solution.py:791

commit v16 on v15

--- a/solution.py
+++ b/solution.py
@@ -776,11 +776,7 @@
 
 def hand_on_kernel(*refs):
     n = len(refs) // 2
-    pairs = []
-    for src, dst in zip(refs[:n], refs[n:2 * n]):
-        lead = [()] if len(src.shape) == 2 else [(i,) for i in range(src.shape[0])]
-        pairs += [(src.at[i], dst.at[i]) if i else (src, dst) for i in lead]
-    copies = [pltpu.make_async_copy(src, dst, refs[2 * n].at[i]) for i, (src, dst) in enumerate(pairs)]
+    copies = [pltpu.make_async_copy(refs[i], refs[n + i], refs[2 * n].at[i]) for i in range(n)]
     for c in copies:
         c.start()
     for c in copies:
@@ -792,7 +788,7 @@
         hand_on_kernel, name="hand_on",
         out_shape=[jax.ShapeDtypeStruct(a.shape, F32) for a in arrays],
         in_specs=[pl.BlockSpec(memory_space=pltpu.VMEM)] * len(arrays), out_specs=[pl.BlockSpec(memory_space=pl.ANY)] * len(arrays),
-        scratch_shapes=[pltpu.SemaphoreType.DMA((32,))],
+        scratch_shapes=[pltpu.SemaphoreType.DMA((len(arrays),))],
         compiler_params=pltpu.CompilerParams(vmem_limit_bytes=12 * 1024 * 1024),
     )(*[pltpu.with_memory_space_constraint(a, pltpu.VMEM) for a in arrays])
 

time: 203 us -> 202 us (level)
  no operation moved by 1% of the time
where the time goes in v16:
time: 202 us
  Pallas kernels  200 us (99%)
  between operations  2.41 us (1%)
    pallas_call x1, Pallas kernels, local_step(): pl.pallas_call(functools.partial(block_kernel, (dp_size, h_size, w_size),...  196 us

profile of v16, /device:TPU:1, one launch (start us, length us, event | category | flops | bytes accessed | tf_op | source)
XLA Modules:
  0.0 202.2 jit_solution(6089893756464197870)
XLA Ops:
  0.6 196.4 %block.1 = (f32[3,16,64,256]{3,2,1,0:T(8,128)S(1)}, f32[2,8,256,256]{3,2,1,0:T(8,128)S(1)}, f32[256,512]{1,0:T(8,128)S(1)}, f32[512,256]{1,0:T(8,128)S(1)}, f32[1,1]{1,0:T(1,128)}) custom-call(f32[3,16,64,256]{3,2,1,0:T(8,128)} %bitcast.6, f32[3,16,64,256]{3,2,1,0:T(8,128)} %bitcast.7, f32[16,16,64]{2,1,0:T(8,128)} %bitcast.8, f32[16,16,64]{2,1,0:T(8,128)} %bitcast.9, ...), custom_call_target="tpu_custom_call" | custom-call | tf_op jit(solution)/shard_map/block/pallas_call | solution.py:827
  197.1 3.4 %hand_on.1 = (f32[3,16,64,256]{3,2,1,0:T(8,128)}, f32[2,8,256,256]{3,2,1,0:T(8,128)}, f32[256,512]{1,0:T(8,128)}, f32[512,256]{1,0:T(8,128)}) custom-call(f32[3,16,64,256]{3,2,1,0:T(8,128)S(1)} %get-tuple-element.15.refs_0_, f32[2,8,256,256]{3,2,1,0:T(8,128)S(1)} %get-tuple-element.16.refs_1_, f32[256,512]{1,0:T(8,128)S(1)} %get-tuple-element.17.refs_2_, ...), custom_call_target="tpu_custom_call" | custom-call | tf_op jit(solution)/shard_map/hand_on/pallas_call | solution.py:787

commit v17 on v16

--- a/solution.py
+++ b/solution.py
@@ -170,13 +170,17 @@
             for wait in unsent.pop(key, []):
                 wait()
 
+    def far_first(k, size):
+        j = k - 1
+        return size // 2 + (j // 2) * (1 - j % 2) - ((j + 1) // 2) * (j % 2)
+
     def along(axis, refs, sems, sent, key=None):
         size, index = {"dp": (dp_size, dp), "h": (h_size, h), "w": (w_size, w)}[axis]
         src, dst = refs(index)
         keep(src, dst, sems)
 
         def body(k, _):
-            other = (index + k) % size
+            other = (index + far_first(k, size)) % size
             src, dst = refs(other)
             push(src, dst, sems, {axis: other})
             return 0
@@ -193,15 +197,14 @@
             src, dst = refs(h2, w2_)
             push(src, dst, sems, {"h": h2, "w": w2_})
 
-        for k in range(1, w_size):
+        def body(h2, _):
+            for k in (2, 1, 3, 0):
+                one(h2, k)
+            return 0
+
+        lax.fori_loop(low_h, high_h, body, 0)
+        for k in (2, 1, 3):
             one(h, k)
-
-        def body(h2, _):
-            for k in range(w_size):
-                one(h2, k)
-            return 0
-
-        lax.fori_loop(low_h, high_h, body, 0)
         unsent.setdefault(key, []).append(lambda: take(sems.at[0], count - 1, [n - 1 for n in counts]))
 
     def take(sem, count, counts):
@@ -237,7 +240,7 @@
             keep(ys.at[b, at_rows(h, k)], dst.at[b, h, at_rows(0, k)], sem.at[b, k])
 
             def body(j, _):
-                o = (h + j) % h_size
+                o = (h + far_first(j, h_size)) % h_size
                 push(ys.at[b, at_rows(o, k)], dst.at[b, h, at_rows(0, k)], sem.at[b, k], {"h": o})
                 return 0
 

time: 202 us -> 200 us (0.990)
  no operation moved by 1% of the time
where the time goes in v17:
time: 200 us
  Pallas kernels  198 us (99%)
  between operations  2.41 us (1%)
    pallas_call x1, Pallas kernels, local_step(): pl.pallas_call(functools.partial(block_kernel, (dp_size, h_size, w_size),...  195 us

profile of v17, /device:TPU:1, one launch (start us, length us, event | category | flops | bytes accessed | tf_op | source)
XLA Modules:
  0.0 200.4 jit_solution(1874189310809901550)
XLA Ops:
  0.6 194.5 %block.1 = (f32[3,16,64,256]{3,2,1,0:T(8,128)S(1)}, f32[2,8,256,256]{3,2,1,0:T(8,128)S(1)}, f32[256,512]{1,0:T(8,128)S(1)}, f32[512,256]{1,0:T(8,128)S(1)}, f32[1,1]{1,0:T(1,128)}) custom-call(f32[3,16,64,256]{3,2,1,0:T(8,128)} %bitcast.6, f32[3,16,64,256]{3,2,1,0:T(8,128)} %bitcast.7, f32[16,16,64]{2,1,0:T(8,128)} %bitcast.8, f32[16,16,64]{2,1,0:T(8,128)} %bitcast.9, ...), custom_call_target="tpu_custom_call" | custom-call | tf_op jit(solution)/shard_map/block/pallas_call | solution.py:830
  195.2 3.4 %hand_on.1 = (f32[3,16,64,256]{3,2,1,0:T(8,128)}, f32[2,8,256,256]{3,2,1,0:T(8,128)}, f32[256,512]{1,0:T(8,128)}, f32[512,256]{1,0:T(8,128)}) custom-call(f32[3,16,64,256]{3,2,1,0:T(8,128)S(1)} %get-tuple-element.15.refs_0_, f32[2,8,256,256]{3,2,1,0:T(8,128)S(1)} %get-tuple-element.16.refs_1_, f32[256,512]{1,0:T(8,128)S(1)} %get-tuple-element.17.refs_2_, ...), custom_call_target="tpu_custom_call" | custom-call | tf_op jit(solution)/shard_map/hand_on/pallas_call | solution.py:790
